TPU v7x, 32 devices: a 4x4x1 block of a 4x4x8 slice. The times are simulated.
32 devices in a mesh: dp: 1 (over z), sp: 32 (over y, x, core).
Axes of the slice: x: 4, y: 4, z: 1, core: 2. Of those that a mesh axis runs over, the one named last changes fastest.
The devices are a block of a 4x4x8 slice.
Arguments:
- x_in: bfloat16 [3, 2048, 2560], P('dp', 'sp')
- positions: int32 [3, 2048], P('dp', 'sp')
- keep_mask: int32 [3, 2048], P('dp', 'sp')
- ln_gain: float32 [2560], replicated
- ln_bias: float32 [2560], replicated
- w_qkv: bfloat16 [2560, 32, 3, 80], replicated
- b_qkv: float32 [32, 3, 80], replicated
- w_out: bfloat16 [2560, 2560], replicated
- b_out: float32 [2560], replicated
- grad_y: bfloat16 [3, 2048, 2560], P('dp', 'sp')
Outputs:
- output 1: bfloat16 [3, 2048, 2560], P('dp', 'sp')
- output 2: bfloat16 [3, 2048, 2560], P('dp', 'sp')
- output 3: float32 [2560, 32, 3, 80], P('dp')
- output 4: float32 [32, 3, 80], P('dp')
- output 5: float32 [2560, 2560], P('dp')
- output 6: float32 [2560], P('dp')
- output 7: float32 [2560], P('dp')
- output 8: float32 [2560], P('dp')
All inputs are finite; a program needn't handle non-finite values.
Results may differ from a plain program's by a relative error of at most 0.00985173.
Values are sent between devices in bfloat16 or wider.
A program may use at most 768 MiB of HBM per device.

v0:
```python
import jax
import jax.numpy as jnp
from jax import lax
from jax.sharding import PartitionSpec as P

NORM_EPS = 1e-5
MASK_FILL = -1e30


def norm_forward(x_blk, ln_gain, ln_bias):
    x_f32 = x_blk.astype(jnp.float32)
    centered = x_f32 - jnp.mean(x_f32, axis=-1, keepdims=True)
    inv_std = lax.rsqrt(jnp.mean(centered * centered, axis=-1, keepdims=True) + NORM_EPS)
    x_hat = centered * inv_std
    x_norm = (x_hat * ln_gain + ln_bias).astype(jnp.bfloat16)
    return x_f32, x_hat, inv_std, x_norm


def norm_backward(d_norm, x_hat, inv_std, ln_gain):
    d_hat = d_norm * ln_gain
    d_mean = jnp.mean(d_hat, axis=-1, keepdims=True)
    d_proj = jnp.mean(d_hat * x_hat, axis=-1, keepdims=True)
    return inv_std * (d_hat - d_mean - x_hat * d_proj)


def attn_probs(q_part, k_part, q_pos, k_pos, k_keep, q_index, k_index, slopes, qk_scale):
    scores = jnp.einsum("bqnd,bknd->bnqk", q_part, k_part, preferred_element_type=jnp.float32) * qk_scale
    pos_gap = (q_pos[:, :, None] - k_pos[:, None, :]).astype(jnp.float32)
    scores = scores - slopes[None, :, None, None] * pos_gap[:, None, :, :]
    allowed = (k_index[None, :] <= q_index[:, None])[None, None] & (k_keep[:, None, None, :] > 0)
    return jax.nn.softmax(jnp.where(allowed, scores, MASK_FILL), axis=-1)


def attn_backward(attn_prob, prob_lo, q_part, k_part, v_part, o_part, do_part, qk_scale):
    dv_part = jnp.einsum("bnqk,bqnd->bknd", prob_lo, do_part, preferred_element_type=jnp.float32)
    grad_prob = jnp.einsum("bqnd,bknd->bnqk", do_part, v_part, preferred_element_type=jnp.float32)
    row_dot = jnp.einsum("bqnd,bqnd->bnq", do_part, o_part, preferred_element_type=jnp.float32)
    ds_lo = (attn_prob * (grad_prob - row_dot[:, :, :, None])).astype(jnp.bfloat16)
    dq_part = jnp.einsum("bnqk,bknd->bqnd", ds_lo, k_part, preferred_element_type=jnp.float32) * qk_scale
    dk_part = jnp.einsum("bnqk,bqnd->bknd", ds_lo, q_part, preferred_element_type=jnp.float32) * qk_scale
    return dq_part, dk_part, dv_part


def solution(mesh):
    sp_size = mesh.shape["sp"]

    def block_fn(x_blk, pos_blk, keep_blk, ln_gain, ln_bias, w_qkv, b_qkv, w_out, b_out, dy_blk):
        batch_loc, seq_loc, hidden = x_blk.shape
        num_heads = w_qkv.shape[1]
        head_dim = w_qkv.shape[3]
        heads_loc = num_heads // sp_size
        seq_len = seq_loc * sp_size
        qk_scale = head_dim ** -0.5
        sp_rank = lax.axis_index("sp")
        x_f32, x_hat, inv_std, x_norm = norm_forward(x_blk, ln_gain, ln_bias)
        qkv_loc = (jnp.einsum("bsh,hnct->bsnct", x_norm, w_qkv, preferred_element_type=jnp.float32) + b_qkv).astype(jnp.bfloat16)
        qkv_head = lax.all_to_all(qkv_loc, "sp", 2, 1, tiled=True)
        pos_full = lax.all_gather(pos_blk, "sp", axis=1, tiled=True)
        keep_full = lax.all_gather(keep_blk, "sp", axis=1, tiled=True)
        q_head = qkv_head[:, :, :, 0]
        k_head = qkv_head[:, :, :, 1]
        v_head = qkv_head[:, :, :, 2]
        head_ids = sp_rank * heads_loc + jnp.arange(heads_loc)
        slopes = jnp.exp2(-8.0 * (head_ids + 1).astype(jnp.float32) / num_heads)
        tok_index = jnp.arange(seq_len)
        attn_prob = attn_probs(q_head, k_head, pos_full, pos_full, keep_full, tok_index, tok_index, slopes, qk_scale)
        prob_lo = attn_prob.astype(jnp.bfloat16)
        o_head = jnp.einsum("bnqk,bknd->bqnd", prob_lo, v_head, preferred_element_type=jnp.float32).astype(jnp.bfloat16)
        o_loc = lax.all_to_all(o_head, "sp", 1, 2, tiled=True).reshape(batch_loc, seq_loc, hidden)
        y_blk = (x_f32 + jnp.einsum("bsh,hk->bsk", o_loc, w_out, preferred_element_type=jnp.float32) + b_out).astype(jnp.bfloat16)
        grad_b_out = jnp.sum(dy_blk.astype(jnp.float32), axis=(0, 1))
        grad_w_out = jnp.einsum("bsh,bsk->hk", o_loc, dy_blk, preferred_element_type=jnp.float32)
        do_loc = jnp.einsum("bsk,hk->bsh", dy_blk, w_out, preferred_element_type=jnp.float32).astype(jnp.bfloat16)
        do_head = lax.all_to_all(do_loc.reshape(batch_loc, seq_loc, num_heads, head_dim), "sp", 2, 1, tiled=True)
        dq_head, dk_head, dv_head = attn_backward(attn_prob, prob_lo, q_head, k_head, v_head, o_head, do_head, qk_scale)
        dqkv_head = jnp.stack([dq_head, dk_head, dv_head], axis=3).astype(jnp.bfloat16)
        dqkv_loc = lax.all_to_all(dqkv_head, "sp", 1, 2, tiled=True)
        grad_b_qkv = jnp.sum(dqkv_loc.astype(jnp.float32), axis=(0, 1))
        grad_w_qkv = jnp.einsum("bsh,bsnct->hnct", x_norm, dqkv_loc, preferred_element_type=jnp.float32)
        d_norm = jnp.einsum("bsnct,hnct->bsh", dqkv_loc, w_qkv, preferred_element_type=jnp.float32)
        grad_gain = jnp.sum(d_norm * x_hat, axis=(0, 1))
        grad_bias = jnp.sum(d_norm, axis=(0, 1))
        grad_x = (dy_blk.astype(jnp.float32) + norm_backward(d_norm, x_hat, inv_std, ln_gain)).astype(jnp.bfloat16)
        summed = lax.psum((grad_w_qkv, grad_b_qkv, grad_w_out, grad_b_out, grad_gain, grad_bias), "sp")
        return (y_blk, grad_x) + tuple(summed)

    act_spec = P("dp", "sp", None)
    tok_spec = P("dp", "sp")
    in_specs = (act_spec, tok_spec, tok_spec, P(), P(), P(), P(), P(), P(), act_spec)
    out_specs = (act_spec, act_spec, P("dp", None, None, None), P("dp", None, None), P("dp", None), P("dp"), P("dp"), P("dp"))
    return jax.shard_map(block_fn, mesh=mesh, in_specs=in_specs, out_specs=out_specs, check_vma=False)
```

profile of v0, /device:TPU:97, one launch (start us, length us, event | category | flops | bytes accessed | tf_op | source)
XLA Modules:
  0.0 1211.1 jit_solution(13564998903978787470)
XLA Ops:
  7.2 9.4 fusion.27
  20.4 9.1 all-to-all-start.2
  30.2 18.5 %add_convert_fusion = bf16[3,64,32,3,80]{4,1,3,2,0:T(8,128)(2,1)S(1)} fusion(f32[32,3,80]{2,1,0:T(4,128)S(1)} %copy.70, bf16[3,64,2560]{2,1,0:T(8,128)(2,1)S(1)} %copy-done, f32[2560]{0:T(1024)S(1)} %copy-done.13, f32[2560]{0:T(1024)S(1)} %copy-done.5, f32[3,64]{1,0:T(4,128)S(1)} %add_rsqrt_fusion, f32[3,64]{1,0:T(4,128)S(1)} %broadcast_multiply_fusion.2, ...), kind=kOutput, calls=%fused_computation.17 | convolution fusion | flops 7555645440 | bytes 43306496 | tf_op jit(solution)/shard_map/bsh,hnct->bsnct/dot_general | solution.py:56
  58.3 80.6 %all-gather.1 = s32[32,64,3]{1,2,0:T(4,128)S(1)} all-gather(s32[1,64,3]{1,2,0:T(4,128)S(1)} %bitcast.161), channel_id=1, replica_groups=mesh['dp'=1,'sp'=32] {'sp'}, dimensions={0}, use_global_device_ids=true | all-gather | bytes 25344 | tf_op jit(solution)/shard_map/all_gather | solution.py:58
  139.7 32.3 %all-gather = s32[32,64,3]{1,2,0:T(4,128)S(1)} all-gather(s32[1,64,3]{1,2,0:T(4,128)S(1)} %bitcast.162), channel_id=1, replica_groups=mesh['dp'=1,'sp'=32] {'sp'}, dimensions={0}, use_global_device_ids=true | all-gather | bytes 25344 | tf_op jit(solution)/shard_map/all_gather | solution.py:59
  181.8 11.4 copy.117
  201.3 33.7 %fusion.60 = (f32[3,2048]{1,0:T(4,128)S(1)}, f32[3,2048,2048]{1,2,0:T(8,128)}) fusion(s32[3,2048]{1,0:T(4,128)S(1)} %bitcast.159, f32[]{:T(128)S(6)} %exp2.9, pred[3,2048]{1,0:T(4,128)(4,1)S(1)} %bitcast.160, pred[2048,2048]{0,1:T(8,128)(4,1)} %iota_compare_fusion, bf16[3,2048,1,3,80]{1,4,0,3,2:T(8,128)(2,1)S(1)} %reshape.233), kind=kOutput, calls=%fused_computation.74 | convolution fusion | flops 2126514176 | bytes 56590340 | tf_op jit(solution)/shard_map/sub | solution.py:31
  235.0 27.3 %fusion.4 = bf16[3,2048,2048]{1,2,0:T(8,128)(2,1)} fusion(f32[3,2048,2048]{1,2,0:T(8,128)} %get-tuple-element.21, f32[3,2048]{1,0:T(4,128)S(1)} %get-tuple-element.20), kind=kLoop, calls=%fused_computation.9 | loop fusion | flops 25165824 | bytes 75522048 | tf_op jit(solution)/shard_map/convert_element_type | solution.py:67
  262.3 23.9 %fusion.32 = bf16[3,2048,1,1,80]{1,4,0,3,2:T(8,128)(2,1)} fusion(bf16[3,2048,80]{1,2,0:T(8,128)(2,1)} %reshape.215, bf16[3,2048,2048]{1,2,0:T(8,128)(2,1)} %fusion.4), kind=kOutput, calls=%fused_computation.38 | convolution fusion | flops 2013757440 | bytes 27131904 | tf_op jit(solution)/shard_map/bnqk,bqnd->bknd/dot_general | solution.py:35
  286.3 13.8 %fusion.51 = (f32[3,2048]{1,0:T(4,128)S(1)}, bf16[3,80,2048]{2,1,0:T(8,128)(2,1)}) fusion(bf16[3,2048,80]{1,2,0:T(8,128)(2,1)} %reshape.215, bf16[3,2048,2048]{1,2,0:T(8,128)(2,1)} %fusion.4, bf16[3,2048,1,3,80]{1,4,0,3,2:T(8,128)(2,1)S(1)} %reshape.233), kind=kOutput, calls=%fused_computation.57 | convolution fusion | flops 2015717376 | bytes 28139520 | tf_op jit(solution)/shard_map/bnqk,bknd->bqnd/dot_general | solution.py:68
  300.1 25.9 %multiply_convert_fusion = bf16[3,2048,2048]{1,2,0:T(8,128)(2,1)} fusion(f32[3,2048]{1,0:T(4,128)S(1)} %get-tuple-element.22, f32[3,2048,2048]{1,2,0:T(8,128)} %get-tuple-element.21, f32[3,2048]{1,0:T(4,128)S(1)} %get-tuple-element.20, bf16[3,2048,80]{1,2,0:T(8,128)(2,1)} %reshape.215, bf16[3,2048,1,3,80]{1,4,0,3,2:T(8,128)(2,1)S(1)} %reshape.233), kind=kOutput, calls=%fused_computation.1 | convolution fusion | flops 2063597568 | bytes 77529088 | tf_op jit(solution)/shard_map/bqnd,bknd->bnqk/dot_general | solution.py:36
  325.9 13.6 %fusion.33 = bf16[3,2048,1,1,80]{1,4,0,3,2:T(8,128)(2,1)} fusion(bf16[3,2048,2048]{1,2,0:T(8,128)(2,1)} %multiply_convert_fusion, bf16[3,2048,1,3,80]{1,4,0,3,2:T(8,128)(2,1)S(1)} %reshape.233), kind=kOutput, calls=%fused_computation.39 | convolution fusion | flops 2014248960 | bytes 27131904 | tf_op jit(solution)/shard_map/bnqk,bqnd->bknd/dot_general | solution.py:40
  349.3 10.3 all-to-all-start.1
  359.6 12.8 %fusion.34 = bf16[3,2048,1,1,80]{1,4,0,3,2:T(8,128)(2,1)S(1)} fusion(bf16[3,2048,2048]{1,2,0:T(8,128)(2,1)} %multiply_convert_fusion, bf16[3,2048,1,3,80]{1,4,0,3,2:T(8,128)(2,1)S(1)} %reshape.233), kind=kOutput, calls=%fused_computation.40 | convolution fusion | flops 2014248960 | bytes 27131904 | tf_op jit(solution)/shard_map/bnqk,bknd->bqnd/dot_general | solution.py:39
  379.6 14.3 %reshape.236 = bf16[32,2,23040]{2,1,0:T(2,128)(2,1)} reshape(bf16[2048,1,3,3,80]{4,3,2,1,0:T(4,128)(2,1)} %bitcast.153) | data formatting | bytes 5898240
  411.9 11.2 convolution_bitcast_fusion.1
  423.1 14.3 %all-to-all-done.3 = bf16[32,2,23040]{2,1,0:T(2,128)(2,1)} async-done(((bf16[32,2,23040]{2,1,0:T(2,128)(2,1)}), bf16[32,2,23040]{2,1,0:T(2,128)(2,1)}, u32[]{:S(2)}, u32[]{:S(2)}) %all-to-all-start.3) | async-done | bytes 2949152 | tf_op jit(solution)/shard_map/all_to_all | solution.py:77
  437.4 15.0 %reshape.237 = bf16[2048,1,3,3,80]{4,3,2,1,0:T(4,128)(2,1)} reshape(bf16[32,2,23040]{2,1,0:T(2,128)(2,1)} %all-to-all-done.3) | data formatting | bytes 5898240
  452.5 32.2 %convolution_bitcast_fusion = f32[2560,32,3,80]{0,3,2,1:T(8,128)} fusion(bf16[3,32,64,1,3,80]{5,0,4,2,1,3:T(4,128)(2,1)} %bitcast.150, bf16[3,64,2560]{2,1,0:T(8,128)(2,1)S(1)} %copy-done.1, f32[2560]{0:T(1024)S(1)} %copy-done.14, f32[2560]{0:T(1024)S(1)} %copy-done.6, f32[3,64]{1,0:T(4,128)S(1)} %copy-done.12, f32[3,64]{1,0:T(4,128)S(1)} %copy-done.9), kind=kOutput, calls=%fused_computation.6 | convolution fusion | flops 7552696320 | bytes 82597376 | tf_op jit(solution)/shard_map/bsh,bsnct->hnct/dot_general | solution.py:79
  493.8 18.3 %fusion.48 = (f32[2560]{0:T(1024)S(1)}, f32[3,64]{1,0:T(4,128)S(1)}, f32[3,64]{1,0:T(4,128)S(1)}, f32[2560]{0:T(1024)S(1)}, f32[3,64,2560]{2,1,0:T(8,128)S(1)}) fusion(bf16[3,64,2560]{2,1,0:T(8,128)(2,1)S(1)} %copy-done.1, f32[3,64]{1,0:T(4,128)S(1)} %copy-done.12, f32[3,64]{1,0:T(4,128)S(1)} %copy-done.9, f32[2560]{0:T(1024)S(1)} %copy-done.6, ...), kind=kOutput, calls=%fused_computation.53 | convolution fusion | flops 7554657280 | bytes 45253632 | tf_op jit(solution)/shard_map/bsnct,hnct->bsh/dot_general | solution.py:80
  519.4 49.0 %all-reduce = (f32[32,3,80]{2,0,1:T(8,128)}, f32[2560]{0:T(1024)}, f32[2560]{0:T(1024)}, f32[2560]{0:T(1024)}) all-reduce(f32[32,3,80]{2,0,1:T(8,128)S(1)} %convert_reduce_fusion, f32[2560]{0:T(1024)S(1)} %get-tuple-element.18, f32[2560]{0:T(1024)S(1)} %get-tuple-element.8, ...), channel_id=1, replica_groups=mesh['dp'=1,'sp'=32] {'sp'}, use_global_device_ids=true, to_apply=%region_8.9 | all-reduce | flops 15360 | bytes 122880 | tf_op jit(solution)/shard_map/psum | solution.py:84
  568.4 566.5 %all-reduce.4.cloned.1.call-done = (f32[2560,32,3,80]{0,3,2,1:T(8,128)}, f32[2560,2560]{1,0:T(8,128)}) async-done(((f32[2560,32,3,80]{0,3,2,1:T(8,128)}, f32[2560,2560]{1,0:T(8,128)}), (f32[2560,32,3,80]{0,3,2,1:T(8,128)}, f32[2560,2560]{1,0:T(8,128)})) %all-reduce.4.cloned.1.call-update) | async-done | bytes 104857616 | tf_op jit(solution)/shard_map/psum | solution.py:84
  1134.8 51.4 %copy.143 = f32[2560,32,3,80]{0,3,2,1:T(8,128)} copy(f32[2560,32,3,80]{0,3,2,1:T(8,128)} %get-tuple-element.29) | data formatting | bytes 157286400
  1186.2 17.6 %copy.144 = f32[2560,2560]{1,0:T(8,128)} copy(f32[2560,2560]{1,0:T(8,128)} %get-tuple-element.31) | data formatting | bytes 52428800
  (70 shorter events, 83.7 us)
Async XLA Ops:
  16.6 12.9 %copy-start = (bf16[3,64,2560]{2,1,0:T(8,128)(2,1)S(1)}, bf16[3,64,2560]{2,1,0:T(8,128)(2,1)}, u32[]{:S(2)}) copy-start(bf16[3,64,2560]{2,1,0:T(8,128)(2,1)} %param.10) | copy-start | bytes 2949124
  18.6 11.6 copy-start.5
  20.3 9.8 copy-start.7
  20.4 9.9 copy-start.13
  20.4 32.1 %all-to-all-start.2 = ((bf16[3,64,32,80]{3,1,0,2:T(8,128)(2,1)}), bf16[3,64,32,80]{3,1,0,2:T(8,128)(2,1)S(1)}, u32[]{:S(2)}, u32[]{:S(2)}) async-start(bf16[3,64,32,80]{3,1,0,2:T(8,128)(2,1)} %copy.82), calls=%async_computation.2 | async-start | bytes 3145728 | tf_op jit(solution)/shard_map/all_to_all | solution.py:74
  29.7 19.0 %copy-start.8 = (f32[3,64]{1,0:T(4,128)}, f32[3,64]{1,0:T(4,128)S(1)}, u32[]{:S(2)}) copy-start(f32[3,64]{1,0:T(4,128)S(1)} %broadcast_multiply_fusion.2) | copy-start | bytes 2308
  30.2 18.5 %copy-start.11 = (f32[3,64]{1,0:T(4,128)}, f32[3,64]{1,0:T(4,128)S(1)}, u32[]{:S(2)}) copy-start(f32[3,64]{1,0:T(4,128)S(1)} %add_rsqrt_fusion) | copy-start | bytes 2308
  52.0 6.3 copy-start.15
  52.0 87.7 %copy-start.16 = (s32[3,64]{1,0:T(4,128)S(1)}, s32[3,64]{1,0:T(4,128)}, u32[]{:S(2)}) copy-start(s32[3,64]{1,0:T(4,128)} %param.12) | copy-start | bytes 2308
  52.5 129.3 %all-to-all-start = ((bf16[3,64,32,3,80]{4,1,3,0,2:T(8,128)(2,1)}), bf16[3,64,32,3,80]{4,1,3,0,2:T(8,128)(2,1)}, u32[]{:S(2)}, u32[]{:S(2)}) async-start(bf16[3,64,32,3,80]{4,1,3,0,2:T(8,128)(2,1)} %copy.71), calls=%async_computation | async-start | bytes 9437184 | tf_op jit(solution)/shard_map/all_to_all | solution.py:57
  193.2 8.0 copy-start.10
  349.3 44.6 %all-to-all-start.1 = ((bf16[32,2,7680]{2,1,0:T(2,128)(2,1)}), bf16[32,2,7680]{2,1,0:T(2,128)(2,1)}, u32[]{:S(2)}, u32[]{:S(2)}) async-start(bf16[32,2,7680]{2,1,0:T(2,128)(2,1)} %reshape.234), calls=%async_computation.1 | async-start | bytes 1966080 | tf_op jit(solution)/shard_map/all_to_all | solution.py:69
  359.6 12.8 %copy-start.2 = (bf16[3,2048,1,1,80]{1,4,0,3,2:T(8,128)(2,1)S(1)}, bf16[3,2048,1,1,80]{1,4,0,3,2:T(8,128)(2,1)}, u32[]{:S(2)}) copy-start(bf16[3,2048,1,1,80]{1,4,0,3,2:T(8,128)(2,1)} %fusion.32) | copy-start | bytes 2949124
  359.6 12.8 %copy-start.3 = (bf16[3,2048,1,1,80]{1,4,0,3,2:T(8,128)(2,1)S(1)}, bf16[3,2048,1,1,80]{1,4,0,3,2:T(8,128)(2,1)}, u32[]{:S(2)}) copy-start(bf16[3,2048,1,1,80]{1,4,0,3,2:T(8,128)(2,1)} %fusion.33) | copy-start | bytes 2949124
  393.9 43.5 %all-to-all-start.3 = ((bf16[32,2,23040]{2,1,0:T(2,128)(2,1)}), bf16[32,2,23040]{2,1,0:T(2,128)(2,1)}, u32[]{:S(2)}, u32[]{:S(2)}) async-start(bf16[32,2,23040]{2,1,0:T(2,128)(2,1)} %reshape.236), calls=%async_computation.3 | async-start | bytes 5898240 | tf_op jit(solution)/shard_map/all_to_all | solution.py:77
  400.2 11.6 copy-start.4
  400.2 734.6 %all-reduce.4.cloned.1.call-start = ((), (), s32[]{:S(2)}) async-start(), calls=%async_computation.4 | async-start | bytes 209715200 | tf_op jit(solution)/shard_map/psum | solution.py:84
  423.1 29.4 %copy-start.1 = (bf16[3,64,2560]{2,1,0:T(8,128)(2,1)S(1)}, bf16[3,64,2560]{2,1,0:T(8,128)(2,1)}, u32[]{:S(2)}) copy-start(bf16[3,64,2560]{2,1,0:T(8,128)(2,1)} %param.10) | copy-start | bytes 2949124
  423.1 29.4 %copy-start.6 = (f32[2560]{0:T(1024)S(1)}, f32[2560]{0:T(1024)}, u32[]{:S(2)}) copy-start(f32[2560]{0:T(1024)} %param.13) | copy-start | bytes 30724
  423.1 29.4 %copy-start.9 = (f32[3,64]{1,0:T(4,128)S(1)}, f32[3,64]{1,0:T(4,128)}, u32[]{:S(2)}) copy-start(f32[3,64]{1,0:T(4,128)} %copy-done.8) | copy-start | bytes 2308
  423.1 29.4 %copy-start.12 = (f32[3,64]{1,0:T(4,128)S(1)}, f32[3,64]{1,0:T(4,128)}, u32[]{:S(2)}) copy-start(f32[3,64]{1,0:T(4,128)} %copy-done.11) | copy-start | bytes 2308
  423.1 29.4 %copy-start.14 = (f32[2560]{0:T(1024)S(1)}, f32[2560]{0:T(1024)}, u32[]{:S(2)}) copy-start(f32[2560]{0:T(1024)} %param.14) | copy-start | bytes 30724
  484.7 0.7 copy-start.17
Sparse Core Ops, SparseCore 0:
  484.9 649.9 all-reduce.3
where the time goes:
time: 1220 us; the launch traced here: 1210 us
  waiting for transfers between devices  581 us (48%)
  matrix products  222 us (18%)
  blocking collectives  162 us (13%)
  local copies, waits for them, and re-layouts  160 us (13%)
  other arithmetic  39.6 us (3%)
  starting transfers between devices  31.6 us (3%)
  between operations  14.9 us (1%)
    psum x1, waiting for transfers between devices, block_fn(): lax.psum((grad_w_qkv, grad_b_qkv, grad_w_out, grad_b_out, grad_gain, grad...  566 us
    unnamed x44, local copies, waits for them, and re-layouts  111 us
    all_gather x1, blocking collectives, block_fn(): pos_full = lax.all_gather(pos_blk, 'sp', axis=1, tiled=True)  80.6 us
    psum x1, blocking collectives, block_fn(): lax.psum((grad_w_qkv, grad_b_qkv, grad_w_out, grad_b_out, grad_gain, grad...  49 us
    sub x1, matrix products, attn_probs(): return jax.nn.softmax(jnp.where(allowed, scores, MASK_FILL), axis=-1)  33.7 us
    all_gather x1, blocking collectives, block_fn(): keep_full = lax.all_gather(keep_blk, 'sp', axis=1, tiled=True)  32.3 us
    dot_general x1, matrix products, block_fn(): jnp.einsum('bsh,bsnct->hnct', x_norm, dqkv_loc, preferred_element_type=jn...  32.2 us
    convert_element_type x1, other arithmetic, block_fn(): prob_lo = attn_prob.astype(jnp.bfloat16)  27.3 us
  transfers between devices with their start and end apart: 5, of which 3 were waited for; matrix products, arithmetic and copies ran while one was open for 10% of the time, Pallas kernels for 0%

commit v1 on v0

v1 whole, which is shorter than its diff:
```python
import functools

import jax
import jax.numpy as jnp
from jax import lax
from jax.experimental import pallas as pl
from jax.experimental.pallas import tpu as pltpu
from jax.sharding import PartitionSpec as P

NORM_EPS = 1e-5
MASK_FILL = -1e30
LANES = 128
MESH = pl.DeviceIdType.MESH
VMEM_LIMIT = 60 * 1024 * 1024


def dot(a, b, ca, cb):
    return lax.dot_general(a, b, (((ca,), (cb,)), ((), ())), preferred_element_type=jnp.float32)


def norm_forward(x_blk, ln_gain, ln_bias):
    x_f32 = x_blk.astype(jnp.float32)
    centered = x_f32 - jnp.mean(x_f32, axis=-1, keepdims=True)
    inv_std = lax.rsqrt(jnp.mean(centered * centered, axis=-1, keepdims=True) + NORM_EPS)
    return (centered * inv_std * ln_gain + ln_bias).astype(jnp.bfloat16)


def exchange_kernel(size, gather, in_ref, out_ref, send_sems, recv_sems, local_sem):
    me = lax.axis_index("sp")
    barrier = pltpu.get_barrier_semaphore()

    def greet(d, carry):
        pl.semaphore_signal(barrier, inc=1, device_id={"sp": lax.rem(me + d, size)}, device_id_type=MESH)
        return carry

    lax.fori_loop(1, size, greet, 0)
    pl.semaphore_wait(barrier, size - 1)

    def block(j):
        return in_ref if gather else in_ref.at[j]

    own = pltpu.make_async_copy(block(me), out_ref.at[me], local_sem)
    own.start()

    def copy_to(d):
        peer = lax.rem(me + d, size)
        return pltpu.make_async_remote_copy(
            src_ref=block(peer), dst_ref=out_ref.at[me], send_sem=send_sems.at[d], recv_sem=recv_sems.at[d],
            device_id={"sp": peer}, device_id_type=MESH)

    def send(d, carry):
        copy_to(d).start()
        return carry

    def arrive(d, carry):
        peer = lax.rem(me + size - d, size)
        pltpu.make_async_remote_copy(
            src_ref=block(peer), dst_ref=out_ref.at[peer], send_sem=send_sems.at[d], recv_sem=recv_sems.at[d],
            device_id={"sp": peer}, device_id_type=MESH).wait_recv()
        return carry

    def sent(d, carry):
        copy_to(d).wait_send()
        return carry

    lax.fori_loop(1, size, send, 0)
    own.wait()
    lax.fori_loop(1, size, arrive, 0)
    lax.fori_loop(1, size, sent, 0)


def exchange(x, size, collective_id, gather=False):
    out_shape = (size, *x.shape) if gather else x.shape
    nbytes = x.size * x.dtype.itemsize
    return pl.pallas_call(
        functools.partial(exchange_kernel, size, gather),
        out_shape=jax.ShapeDtypeStruct(out_shape, x.dtype),
        in_specs=[pl.BlockSpec(memory_space=pl.ANY)],
        out_specs=pl.BlockSpec(memory_space=pl.ANY),
        scratch_shapes=[pltpu.SemaphoreType.DMA((size,)), pltpu.SemaphoreType.DMA((size,)), pltpu.SemaphoreType.DMA],
        compiler_params=pltpu.CompilerParams(collective_id=collective_id, has_side_effects=True),
        cost_estimate=pl.CostEstimate(flops=10_000_000_000, bytes_accessed=2 * nbytes, transcendentals=0),
        name="gather_small" if gather else "all_to_all",
    )(x)


def attn_kernel(head_dim, q_block, slope_ref, qkv_ref, do_ref, pos_ref, keep_ref, out_ref, dk_acc, dv_acc):
    seq_len, pad_dim = dk_acc.shape
    blocks, _, tok, _ = qkv_ref.shape
    scale = head_dim ** -0.5
    slope = slope_ref[0]
    pos_row = pos_ref[0]
    keep_row = keep_ref[0]
    per = q_block // tok
    dk_acc[...] = jnp.zeros_like(dk_acc)
    dv_acc[...] = jnp.zeros_like(dv_acc)

    def rows(ref, lo, hi, part):
        return ref[lo * per:hi * per, 0, :, part * pad_dim:(part + 1) * pad_dim].reshape((hi - lo) * q_block, pad_dim)

    for i in range(seq_len // q_block):
        span = (i + 1) * q_block
        q = rows(qkv_ref, i, i + 1, 0)
        k = rows(qkv_ref, 0, i + 1, 1)
        v = rows(qkv_ref, 0, i + 1, 2)
        do = rows(do_ref, i, i + 1, 0)
        gap = (pos_row[:, span - 1:span] - pos_row[:, :span]).astype(jnp.float32)
        bias = jnp.where(keep_row[:, :span] > 0, -slope * gap, MASK_FILL)
        scores = dot(q, k, 1, 1) * scale + bias
        row_id = lax.broadcasted_iota(jnp.int32, (q_block, span), 0) + i * q_block
        col_id = lax.broadcasted_iota(jnp.int32, (q_block, span), 1)
        scores = jnp.where(col_id <= row_id, scores, MASK_FILL)
        expo = jnp.exp(scores - jnp.max(scores, axis=-1, keepdims=True))
        prob = expo * (1.0 / jnp.sum(expo, axis=-1, keepdims=True))
        prob_lo = prob.astype(jnp.bfloat16)
        o = dot(prob_lo, v, 1, 0).astype(jnp.bfloat16)
        row_dot = jnp.sum(do.astype(jnp.float32) * o.astype(jnp.float32), axis=-1, keepdims=True)
        ds_lo = (prob * (dot(do, v, 1, 1) - row_dot)).astype(jnp.bfloat16)
        dq = (dot(ds_lo, k, 1, 0) * scale).astype(jnp.bfloat16)
        dv_acc[:span, :] += dot(prob_lo, do, 0, 0)
        dk_acc[:span, :] += dot(ds_lo, q, 0, 0)
        both = jnp.concatenate([o[:, :head_dim], dq[:, :head_dim]], axis=1)
        out_ref[i * per:(i + 1) * per, 0, :, 0:2 * head_dim] = both.reshape(per, tok, 2 * head_dim)
    dk = (dk_acc[...] * scale).astype(jnp.bfloat16)
    dv = dv_acc[...].astype(jnp.bfloat16)
    both = jnp.concatenate([dk[:, :head_dim], dv[:, :head_dim]], axis=1)
    out_ref[:, 0, :, 2 * head_dim:4 * head_dim] = both.reshape(blocks, tok, 2 * head_dim)


def attention(slope, qkv, do, pos, keep, head_dim, q_block):
    blocks, batch, tok, wide = qkv.shape
    pad_dim = wide // 3
    seq_len = blocks * tok
    flops = 6 * batch * seq_len * seq_len * 256
    return pl.pallas_call(
        functools.partial(attn_kernel, head_dim, q_block),
        grid=(batch,),
        out_shape=jax.ShapeDtypeStruct((blocks, batch, tok, 4 * head_dim), jnp.bfloat16),
        in_specs=[
            pl.BlockSpec(memory_space=pltpu.SMEM),
            pl.BlockSpec((blocks, 1, tok, wide), lambda b: (0, b, 0, 0)),
            pl.BlockSpec((blocks, 1, tok, pad_dim), lambda b: (0, b, 0, 0)),
            pl.BlockSpec((1, 1, seq_len), lambda b: (b, 0, 0)),
            pl.BlockSpec((1, 1, seq_len), lambda b: (b, 0, 0)),
        ],
        out_specs=pl.BlockSpec((blocks, 1, tok, 4 * head_dim), lambda b: (0, b, 0, 0)),
        scratch_shapes=[pltpu.VMEM((seq_len, pad_dim), jnp.float32)] * 2,
        compiler_params=pltpu.CompilerParams(vmem_limit_bytes=VMEM_LIMIT),
        cost_estimate=pl.CostEstimate(flops=flops, bytes_accessed=20_000_000, transcendentals=batch * seq_len * seq_len // 2),
        name="attention",
    )(slope, qkv, do, pos, keep)


def token_kernel(head_dim, chunk, parts_ref, wq_ref, wo_ref, x_ref, dy_ref, gain_ref, bout_ref,
                 y_ref, gx_ref, bq_ref, sums_ref, dn_acc, y_acc):
    n = pl.program_id(0)
    parts = parts_ref[0]
    o = parts[:, :head_dim]
    dqkv = parts[:, head_dim:]
    bq_ref[0] = jnp.sum(dqkv.astype(jnp.float32), axis=0, keepdims=True)
    dn_term = dot(dqkv, wq_ref[0], 1, 0)
    y_term = dot(o, wo_ref[0], 1, 0)

    @pl.when(n == 0)
    def _():
        dn_acc[...] = dn_term
        y_acc[...] = y_term

    @pl.when(n > 0)
    def _():
        dn_acc[...] += dn_term
        y_acc[...] += y_term

    @pl.when(n == pl.num_programs(0) - 1)
    def _():
        sums_ref[...] = jnp.zeros_like(sums_ref)
        gain = gain_ref[...]
        bout = bout_ref[...]

        def body(c, carry):
            at = pl.ds(pl.multiple_of(c * chunk, chunk), chunk)
            x = x_ref[at, :].astype(jnp.float32)
            dy = dy_ref[at, :].astype(jnp.float32)
            centered = x - jnp.mean(x, axis=-1, keepdims=True)
            inv_std = lax.rsqrt(jnp.mean(centered * centered, axis=-1, keepdims=True) + NORM_EPS)
            x_hat = centered * inv_std
            d_norm = dn_acc[at, :]
            d_hat = d_norm * gain
            d_mean = jnp.mean(d_hat, axis=-1, keepdims=True)
            d_proj = jnp.mean(d_hat * x_hat, axis=-1, keepdims=True)
            gx_ref[at, :] = (dy + inv_std * (d_hat - d_mean - x_hat * d_proj)).astype(jnp.bfloat16)
            y_ref[at, :] = (x + y_acc[at, :] + bout).astype(jnp.bfloat16)
            sums_ref[0:1, :] += jnp.sum(d_norm * x_hat, axis=0, keepdims=True)
            sums_ref[1:2, :] += jnp.sum(d_norm, axis=0, keepdims=True)
            sums_ref[2:3, :] += jnp.sum(dy, axis=0, keepdims=True)
            return carry

        lax.fori_loop(0, x_ref.shape[0] // chunk, body, 0)


def token_side(parts, wq, wo, x, dy, gain, bout, head_dim):
    heads, tokens, _ = parts.shape
    hidden = x.shape[1]
    whole = lambda n: (0, 0)
    per_head = lambda n: (n, 0, 0)
    return pl.pallas_call(
        functools.partial(token_kernel, head_dim, 16),
        grid=(heads,),
        out_shape=(
            jax.ShapeDtypeStruct((tokens, hidden), jnp.bfloat16),
            jax.ShapeDtypeStruct((tokens, hidden), jnp.bfloat16),
            jax.ShapeDtypeStruct((heads, 1, 3 * head_dim), jnp.float32),
            jax.ShapeDtypeStruct((8, hidden), jnp.float32),
        ),
        in_specs=[
            pl.BlockSpec((1, tokens, 4 * head_dim), per_head),
            pl.BlockSpec((1, 3 * head_dim, hidden), per_head),
            pl.BlockSpec((1, head_dim, hidden), per_head),
            pl.BlockSpec((tokens, hidden), whole),
            pl.BlockSpec((tokens, hidden), whole),
            pl.BlockSpec((1, hidden), whole),
            pl.BlockSpec((1, hidden), whole),
        ],
        out_specs=(
            pl.BlockSpec((tokens, hidden), whole),
            pl.BlockSpec((tokens, hidden), whole),
            pl.BlockSpec((1, 1, 3 * head_dim), per_head),
            pl.BlockSpec((8, hidden), whole),
        ),
        scratch_shapes=[pltpu.VMEM((tokens, hidden), jnp.float32)] * 2,
        compiler_params=pltpu.CompilerParams(vmem_limit_bytes=VMEM_LIMIT),
        cost_estimate=pl.CostEstimate(
            flops=2 * tokens * hidden * 4 * heads * head_dim, bytes_accessed=8 * hidden * heads * head_dim, transcendentals=0),
        name="token_side",
    )(parts, wq, wo, x, dy, gain, bout)


def place_kernel(piece_ref, *refs):
    refs[-1][0, 0] = piece_ref[0]


def place(piece, slot, slots, into=None):
    heads, rows, cols = piece.shape
    shape = jax.ShapeDtypeStruct((heads, slots, rows, cols), piece.dtype)
    old = [] if into is None else [into]
    return pl.pallas_call(
        place_kernel,
        grid=(heads,),
        out_shape=shape,
        in_specs=[pl.BlockSpec((1, rows, cols), lambda n: (n, 0, 0))] + [pl.BlockSpec(memory_space=pl.ANY)] * len(old),
        out_specs=pl.BlockSpec((1, 1, rows, cols), lambda n: (n, slot, 0, 0)),
        input_output_aliases={} if into is None else {1: 0},
        cost_estimate=pl.CostEstimate(flops=5_000_000_000, bytes_accessed=8 * heads * rows * cols, transcendentals=0),
        name="place",
    )(piece, *old)


def solution(mesh):
    size = mesh.shape["sp"]

    def block_fn(x_blk, pos_blk, keep_blk, ln_gain, ln_bias, w_qkv, b_qkv, w_out, b_out, dy_blk):
        batch, tok, hidden = x_blk.shape
        heads, head_dim = w_qkv.shape[1], w_qkv.shape[3]
        tokens, seq_len = batch * tok, size * tok
        pad_dim = -(-head_dim // LANES) * LANES
        rank = lax.axis_index("sp")
        wq = jnp.transpose(w_qkv, (1, 2, 3, 0))
        wo = w_out.reshape(heads, head_dim, hidden)
        dy_flat = dy_blk.reshape(tokens, hidden)

        def gather(a):
            return lax.all_gather(a, "sp", axis=0, tiled=True)

        x_norm = norm_forward(x_blk, ln_gain, ln_bias).reshape(tokens, hidden)
        x_all = gather(x_norm)
        dy_all = gather(dy_flat)

        do_out = jnp.einsum("sk,nck->nsc", dy_flat, wo, preferred_element_type=jnp.float32).astype(jnp.bfloat16)
        do_in = exchange(do_out.reshape(heads, tokens * head_dim // LANES, LANES), size, 0)
        do_head = jnp.pad(do_in.reshape(size, batch, tok, head_dim), ((0, 0), (0, 0), (0, 0), (0, pad_dim - head_dim)))

        meta = jnp.pad(jnp.concatenate([pos_blk, keep_blk], axis=0), ((0, 8 - 2 * batch), (0, LANES - tok)))
        meta_all = jnp.transpose(exchange(meta, size, 1, gather=True)[:, :2 * batch, :tok], (1, 0, 2)).reshape(2 * batch, 1, seq_len)

        w_head = jnp.pad(lax.dynamic_slice_in_dim(wq, rank, 1, 0)[0], ((0, 0), (0, pad_dim - head_dim), (0, 0)))
        b_head = jnp.pad(lax.dynamic_slice_in_dim(b_qkv, rank, 1, 0)[0], ((0, 0), (0, pad_dim - head_dim)))
        qkv = (dot(x_all, w_head.reshape(3 * pad_dim, hidden), 1, 1) + b_head.reshape(-1)).astype(jnp.bfloat16)
        slope = jnp.exp2(-8.0 * (rank + 1).astype(jnp.float32) / heads).reshape(1)
        parts = attention(slope, qkv.reshape(size, batch, tok, 3 * pad_dim), do_head, meta_all[:batch], meta_all[batch:],
                          head_dim, min(256, seq_len))

        parts_flat = parts.reshape(size * tokens, 4 * head_dim)
        grad_head = dot(parts_flat, x_all, 0, 0)
        pieces = [grad_head[(c + 1) * head_dim:(c + 2) * head_dim] for c in range(3)]
        grad_wq = None
        for c in range(3):
            grad_wq = place(gather(pieces[c]).reshape(heads, head_dim, hidden), c, 3, grad_wq)
        grad_wo_head = dot(parts_flat[:, :head_dim], dy_all, 0, 0)
        grad_wo = place(gather(grad_wo_head).reshape(heads, head_dim, hidden), 0, 1)

        flat = parts.reshape(size, tokens * 4 * head_dim // LANES, LANES)
        parts_tok = exchange(flat, size, 2).reshape(heads, tokens, 4 * head_dim)
        y, grad_x, bq_part, sums = token_side(
            parts_tok, wq.reshape(heads, 3 * head_dim, hidden), wo, x_blk.reshape(tokens, hidden), dy_flat,
            ln_gain.reshape(1, hidden), b_out.reshape(1, hidden), head_dim)
        bq, gain, bias, bo = lax.psum((bq_part.reshape(-1), sums[0], sums[1], sums[2]), "sp")
        return (y.reshape(x_blk.shape), grad_x.reshape(x_blk.shape), jnp.transpose(grad_wq, (3, 0, 1, 2)),
                bq.reshape(heads, 3, head_dim), grad_wo.reshape(heads * head_dim, hidden), bo, gain, bias)

    act_spec = P("dp", "sp", None)
    tok_spec = P("dp", "sp")
    in_specs = (act_spec, tok_spec, tok_spec, P(), P(), P(), P(), P(), P(), act_spec)
    out_specs = (act_spec, act_spec, P("dp", None, None, None), P("dp", None, None), P("dp", None), P("dp"), P("dp"), P("dp"))
    return jax.shard_map(block_fn, mesh=mesh, in_specs=in_specs, out_specs=out_specs, check_vma=False)
```

time: 1220 us -> 689 us (0.56)
  waiting for transfers between devices: 581 us -> 161 us
  Pallas kernels: 0 us -> 346 us
  matrix products: 222 us -> 66.1 us
  local copies, waits for them, and re-layouts: 160 us -> 39.2 us
  blocking collectives: 162 us -> 47.7 us
  other arithmetic: 39.6 us -> 6.57 us
  starting transfers between devices: 31.6 us -> 0.38 us
    psum x1 -> x0, waiting for transfers between devices: 566 us -> none  [block_fn(): lax.psum((grad_w_qkv, grad_b_qkv, grad_w_out, grad_b_out, grad_gain, grad...]
    pallas_call x0 -> x9, Pallas kernels: none -> 346 us  [the longest x3 138 us: exchange(): pl.pallas_call(functools.partial(exchange_kernel, size, gather), out_shap...]
    all_gather x0 -> x6, waiting for transfers between devices: none -> 159 us  [gather(): return lax.all_gather(a, 'sp', axis=0, tiled=True)]
    dot_general x11 -> x4, matrix products: 188 us -> 66.1 us  [the longest x3 56.7 us: dot(): lax.dot_general(a, b, (((ca,), (cb,)), ((), ())), preferred_element_type=...]
    all_gather x2 -> x0, blocking collectives: 113 us -> none  [the longest x1 80.6 us: block_fn(): pos_full = lax.all_gather(pos_blk, 'sp', axis=1, tiled=True)]
    unnamed x44 -> x18, local copies, waits for them, and re-layouts: 111 us -> 0.68 us
    sub x1 -> x0, matrix products: 33.7 us -> none  [attn_probs(): return jax.nn.softmax(jnp.where(allowed, scores, MASK_FILL), axis=-1)]
    all_to_all x4 -> x0, starting transfers between devices: 31.5 us -> none  [the longest x1 10.3 us: block_fn(): lax.all_to_all(o_head, 'sp', 1, 2, tiled=True)]
  transfers between devices with their start and end apart: 5 -> 6, of which waited for: 3 -> 4; matrix products, arithmetic and copies ran while one was open for 10% -> 16% of each run, Pallas kernels for 0% -> 28%
where the time goes in v1:
time: 689 us; the launch traced here: 681 us
  Pallas kernels  346 us (50%)
  waiting for transfers between devices  161 us (23%)
  matrix products  66.1 us (10%)
  blocking collectives  47.7 us (7%)
  local copies, waits for them, and re-layouts  39.2 us (6%)
  between operations  14.6 us (2%)
    all_gather x6, waiting for transfers between devices, gather(): return lax.all_gather(a, 'sp', axis=0, tiled=True)  159 us
    pallas_call x3, Pallas kernels, exchange(): pl.pallas_call(functools.partial(exchange_kernel, size, gather), out_shap...  138 us
    pallas_call x4, Pallas kernels, place(): pl.pallas_call(place_kernel, grid=(heads,), out_shape=shape, in_specs=[pl...  121 us
    dot_general x3, matrix products, dot(): lax.dot_general(a, b, (((ca,), (cb,)), ((), ())), preferred_element_type=...  56.7 us
    pallas_call x1, Pallas kernels, token_side(): pl.pallas_call(functools.partial(token_kernel, head_dim, 16), grid=(heads...  49.1 us
    psum x1, blocking collectives, block_fn(): lax.psum((bq_part.reshape(-1), sums[0], sums[1], sums[2]), 'sp')  47.7 us
    pallas_call x1, Pallas kernels, attention(): pl.pallas_call(functools.partial(attn_kernel, head_dim, q_block), grid=(b...  38.1 us
  transfers between devices with their start and end apart: 6, of which 4 were waited for; matrix products, arithmetic and copies ran while one was open for 16% of the time, Pallas kernels for 28%

profile of v1, /device:TPU:97, one launch (start us, length us, event | category | flops | bytes accessed | tf_op | source)
XLA Modules:
  0.0 680.8 jit_solution(12171229420670496363)
XLA Ops:
  10.4 2.6 fusion.5
  14.1 9.4 %fusion.8 = bf16[32,192,80]{1,2,0:T(8,128)(2,1)} fusion(bf16[32,80,2560]{2,1,0:T(8,128)(2,1)} %bitcast.50, bf16[192,2560,1]{1,0,2:T(8,128)(2,1)S(1)} %bitcast.57), kind=kOutput, calls=%fused_computation.12 | convolution fusion | flops 2517073920 | bytes 15073280 | tf_op jit(solution)/shard_map/sk,nck->nsc/dot_general | solution.py:278
  23.4 2.2 copy.24
  25.6 3.5 reshape.112.in_ref
  29.0 28.5 %all_to_all.2 = bf16[32,120,128]{2,1,0:T(8,128)(2,1)} custom-call(bf16[32,120,128]{2,1,0:T(8,128)(2,1)} %reshape.112.in_ref), custom_call_target="tpu_custom_call" | custom-call | flops 10000000000 | bytes 1966080 | tf_op jit(solution)/shard_map/all_to_all/pallas_call | solution.py:75
  57.5 3.0 reshape.113
  65.6 10.2 %gather_small.1 = s32[32,8,128]{2,1,0:T(8,128)} custom-call(s32[8,128]{1,0:T(8,128)} %pad.19.in_ref), custom_call_target="tpu_custom_call" | custom-call | flops 10000000000 | bytes 8192 | tf_op jit(solution)/shard_map/gather_small/pallas_call | solution.py:75
  78.2 53.0 %all-gather.7.cloned.1.call-done = bf16[6144,2560]{1,0:T(8,128)(2,1)} async-done(((bf16[192,2560]{1,0:T(8,128)(2,1)}), bf16[6144,2560]{1,0:T(8,128)(2,1)}) %all-gather.7.cloned.1.call-update) | async-done | bytes 31457296 | tf_op jit(solution)/shard_map/all_gather | solution.py:272
  131.2 22.1 %add_convert_fusion = bf16[6144,384]{1,0:T(8,128)(2,1)} fusion(bf16[6144,2560]{1,0:T(8,128)(2,1)} %all-gather.7.cloned.1.call-done, bf16[384,2560]{1,0:T(8,128)(2,1)S(1)} %bitcast.58, f32[384]{0:T(512)S(1)} %pad_bitcast_fusion), kind=kOutput, calls=%fused_computation | convolution fusion | flops 12084314112 | bytes 38143488 | tf_op jit(solution)/shard_map/dot_general | solution.py:18
  153.3 38.1 %attention.1 = bf16[32,3,64,320]{3,2,1,0:T(8,128)(2,1)} custom-call(f32[1]{0:T(128)} %bitcast.slope_ref, bf16[32,3,64,384]{3,2,1,0:T(8,128)(2,1)} %bitcast.62, bf16[32,3,64,128]{3,2,1,0:T(8,128)(2,1)} %pad.18.do_ref, s32[3,1,2048]{2,1,0:T(1,128)} %slice.38.pos_ref, s32[3,1,2048]{2,1,0:T(1,128)} %slice.40.keep_ref), custom_call_target="tpu_custom_call" | custom-call | flops 19327352832 | bytes 20000000 | tf_op jit(solution)/shard_map/attention/pallas_call | solution.py:135
  191.4 17.7 %fusion.11 = f32[320,2560]{1,0:T(8,128)S(1)} fusion(bf16[6144,320]{1,0:T(8,128)(2,1)} %bitcast.52, bf16[6144,2560]{1,0:T(8,128)(2,1)} %all-gather.7.cloned.1.call-done), kind=kOutput, calls=%fused_computation.26 | convolution fusion | flops 10066329600 | bytes 38666240 | tf_op jit(solution)/shard_map/dot_general | solution.py:18
  210.7 24.7 %all-gather.15.cloned.1.call-done = bf16[6144,2560]{1,0:T(8,128)(2,1)} async-done(((bf16[192,2560]{1,0:T(8,128)(2,1)}), bf16[6144,2560]{1,0:T(8,128)(2,1)}) %all-gather.15.cloned.1.call-update) | async-done | bytes 31457296 | tf_op jit(solution)/shard_map/all_gather | solution.py:272
  235.4 17.0 %fusion.6 = f32[80,2560]{1,0:T(8,128)} fusion(bf16[6144,2560]{1,0:T(8,128)(2,1)} %all-gather.15.cloned.1.call-done, bf16[6144,320]{1,0:T(8,128)(2,1)} %bitcast.53), kind=kOutput, calls=%fused_computation.10 | convolution fusion | flops 2516582400 | bytes 33849344 | tf_op jit(solution)/shard_map/dot_general | solution.py:18
  254.9 9.8 %reshape.114.in_ref = bf16[32,480,128]{2,1,0:T(8,128)(2,1)} reshape(bf16[32,3,64,320]{3,2,1,0:T(8,128)(2,1)} %attention.1) | data formatting | bytes 7864320 | tf_op jit(solution)/shard_map/reshape | solution.py:301
  264.7 99.1 %all_to_all.3 = bf16[32,480,128]{2,1,0:T(8,128)(2,1)} custom-call(bf16[32,480,128]{2,1,0:T(8,128)(2,1)} %reshape.114.in_ref), custom_call_target="tpu_custom_call" | custom-call | flops 10000000000 | bytes 7864320 | tf_op jit(solution)/shard_map/all_to_all/pallas_call | solution.py:75
  363.8 8.7 %reshape.115.parts_ref = bf16[32,192,320]{2,1,0:T(8,128)(2,1)} reshape(bf16[32,480,128]{2,1,0:T(8,128)(2,1)} %all_to_all.3) | data formatting | bytes 7864320 | tf_op jit(solution)/shard_map/reshape | solution.py:302
  372.5 49.1 %token_side.1 = (bf16[192,2560]{1,0:T(8,128)(2,1)}, bf16[192,2560]{1,0:T(8,128)(2,1)}, f32[32,1,240]{2,1,0:T(1,128)}, f32[8,2560]{1,0:T(8,128)}) custom-call(bf16[32,192,320]{2,1,0:T(8,128)(2,1)} %reshape.115.parts_ref, bf16[32,240,2560]{2,1,0:T(8,128)(2,1)} %bitcast.43, bf16[32,80,2560]{2,1,0:T(8,128)(2,1)} %bitcast.51, bf16[192,2560]{1,0:T(8,128)(2,1)} %bitcast.49, ...), custom_call_target="tpu_custom_call" | custom-call | flops 10066329600 | bytes 52428800 | tf_op jit(solution)/shard_map/token_side/pallas_call | solution.py:206
  423.7 47.7 %all-reduce.4 = (f32[32,3,80]{2,1,0:T(4,128)S(1)}, f32[2560]{0:T(1024)}, f32[2560]{0:T(1024)}, f32[2560]{0:T(1024)}) all-reduce(f32[32,3,80]{2,1,0:T(4,128)S(1)} %reshape.127, f32[2560]{0:T(1024)S(1)} %get-tuple-element.26, f32[2560]{0:T(1024)S(1)} %get-tuple-element.25, ...), channel_id=1, replica_groups=mesh['dp'=1,'sp'=32] {'sp'}, use_global_device_ids=true, to_apply=%region_2.3 | all-reduce | flops 15360 | bytes 122880 | tf_op jit(solution)/shard_map/psum | solution.py:306
  472.0 30.2 %place.4.refs_0_ = f32[32,3,80,2560]{3,2,1,0:T(8,128)} custom-call(f32[32,80,2560]{2,1,0:T(8,128)} %bitcast.44), custom_call_target="tpu_custom_call" | custom-call | flops 5000000000 | bytes 52428800 | tf_op jit(solution)/shard_map/place/pallas_call | solution.py:246
  502.2 30.2 %place.7 = f32[32,1,80,2560]{3,2,1,0:T(8,128)} custom-call(f32[32,80,2560]{2,1,0:T(8,128)} %bitcast.45), custom_call_target="tpu_custom_call" | custom-call | flops 5000000000 | bytes 52428800 | tf_op jit(solution)/shard_map/place/pallas_call | solution.py:246
  532.4 20.6 %all-gather.11.cloned.1.call-done = f32[2560,2560]{1,0:T(8,128)} async-done(((f32[80,2560]{1,0:T(8,128)}), f32[2560,2560]{1,0:T(8,128)}) %all-gather.11.cloned.1.call-update) | async-done | bytes 26214416 | tf_op jit(solution)/shard_map/all_gather | solution.py:272
  553.0 30.2 %place.5.refs_0_ = f32[32,3,80,2560]{3,2,1,0:T(8,128)} custom-call(f32[32,80,2560]{2,1,0:T(8,128)} %bitcast.47, f32[32,3,80,2560]{3,2,1,0:T(8,128)} %place.4.refs_0_), custom_call_target="tpu_custom_call", output_to_operand_aliasing={{}: (1, {})} | custom-call | flops 5000000000 | bytes 52428800 | tf_op jit(solution)/shard_map/place/pallas_call | solution.py:246
  583.2 60.4 %all-gather.9.cloned.1.call-done = f32[2560,2560]{1,0:T(8,128)} async-done(((f32[80,2560]{1,0:T(8,128)}), f32[2560,2560]{1,0:T(8,128)}) %all-gather.9.cloned.1.call-update) | async-done | bytes 26214416 | tf_op jit(solution)/shard_map/all_gather | solution.py:272
  643.5 30.2 %place.6 = f32[32,3,80,2560]{3,2,1,0:T(8,128)} custom-call(f32[32,80,2560]{2,1,0:T(8,128)} %bitcast.48, f32[32,3,80,2560]{3,2,1,0:T(8,128)} %place.5.refs_0_), custom_call_target="tpu_custom_call", output_to_operand_aliasing={{}: (1, {})} | custom-call | flops 5000000000 | bytes 52428800 | tf_op jit(solution)/shard_map/place/pallas_call | solution.py:246
  (55 shorter events, 18.4 us)
Async XLA Ops:
  7.2 6.8 copy-start
  7.2 6.8 %copy-start.2 = (bf16[3,64,2560]{2,1,0:T(8,128)(2,1)S(1)}, bf16[3,64,2560]{2,1,0:T(8,128)(2,1)}, u32[]{:S(2)}) copy-start(bf16[3,64,2560]{2,1,0:T(8,128)(2,1)} %param.19) | copy-start | bytes 2949124
  7.2 124.0 %all-gather.7.cloned.1.call-start = ((), (), s32[]{:S(2)}) async-start(), calls=%async_computation | async-start | bytes 32440320 | tf_op jit(solution)/shard_map/all_gather | solution.py:272
  13.1 222.3 %all-gather.15.cloned.1.call-start = ((), (), s32[]{:S(2)}) async-start(), calls=%async_computation.4 | async-start | bytes 32440320 | tf_op jit(solution)/shard_map/all_gather | solution.py:272
  13.9 458.1 %all-gather.13.cloned.1.call-start = ((), (), s32[]{:S(2)}) async-start(), calls=%async_computation.3 | async-start | bytes 27033600 | tf_op jit(solution)/shard_map/all_gather | solution.py:272
  60.5 4.5 copy-start.6
  60.5 4.5 copy-start.7
  65.6 65.5 %copy-start.3 = (bf16[3,128,2560]{2,1,0:T(8,128)(2,1)S(1)}, bf16[3,128,2560]{2,1,0:T(8,128)(2,1)}, u32[]{:S(2)}) copy-start(bf16[3,128,2560]{2,1,0:T(8,128)(2,1)} %pad.16) | copy-start | bytes 5898244
  210.6 43.1 %copy-start.4 = (f32[2560]{0:T(1024)S(1)}, f32[2560]{0:T(1024)}, u32[]{:S(2)}) copy-start(f32[2560]{0:T(1024)} %param.13) | copy-start | bytes 30724
  210.6 43.7 %copy-start.5 = (f32[2560]{0:T(1024)S(1)}, f32[2560]{0:T(1024)}, u32[]{:S(2)}) copy-start(f32[2560]{0:T(1024)} %param.18) | copy-start | bytes 30724
  210.6 291.6 %all-gather.17.cloned.1.call-start = ((), (), s32[]{:S(2)}) async-start(), calls=%async_computation.5 | async-start | bytes 27033600 | tf_op jit(solution)/shard_map/all_gather | solution.py:272
  252.4 300.6 %all-gather.11.cloned.1.call-start = ((), (), s32[]{:S(2)}) async-start(), calls=%async_computation.2 | async-start | bytes 27033600 | tf_op jit(solution)/shard_map/all_gather | solution.py:272
  253.1 390.5 %all-gather.9.cloned.1.call-start = ((), (), s32[]{:S(2)}) async-start(), calls=%async_computation.1 | async-start | bytes 27033600 | tf_op jit(solution)/shard_map/all_gather | solution.py:272
  643.5 30.2 %copy-start.1 = (f32[32,3,80]{2,0,1:T(8,128)S(1)}, f32[32,3,80]{2,0,1:T(8,128)}, u32[]{:S(2)}) copy-start(f32[32,3,80]{2,0,1:T(8,128)} %param.16) | copy-start | bytes 92164
Sparse Core Ops, SparseCore 0:
  13.2 117.9 all-gather.6
  133.2 102.0 all-gather.14
  237.5 135.6 all-gather.12
  375.1 87.6 all-gather.16
  464.7 88.2 all-gather.10
  554.9 88.5 all-gather.8

commit v2 on v1

v2 whole, which is shorter than its diff:
```python
import functools
import math

import jax
import jax.numpy as jnp
from jax import lax
from jax.experimental import pallas as pl
from jax.experimental.pallas import tpu as pltpu
from jax.sharding import PartitionSpec as P

NORM_EPS = 1e-5
MASK_FILL = -1e30
LANES = 128
MESH = pl.DeviceIdType.MESH
VMEM_LIMIT = 61 * 1024 * 1024


def dot(a, b, ca, cb):
    return lax.dot_general(a, b, (((ca,), (cb,)), ((), ())), preferred_element_type=jnp.float32)


def norm_forward(x_blk, ln_gain, ln_bias):
    x_f32 = x_blk.astype(jnp.float32)
    centered = x_f32 - jnp.mean(x_f32, axis=-1, keepdims=True)
    inv_std = lax.rsqrt(jnp.mean(centered * centered, axis=-1, keepdims=True) + NORM_EPS)
    return (centered * inv_std * ln_gain + ln_bias).astype(jnp.bfloat16)


def greet_all(me, size):
    barrier = pltpu.get_barrier_semaphore()

    def greet(d, carry):
        pl.semaphore_signal(barrier, inc=1, device_id={"sp": lax.rem(me + d, size)}, device_id_type=MESH)
        return carry

    lax.fori_loop(1, size, greet, 0)
    pl.semaphore_wait(barrier, size - 1)


class Direct:
    def __init__(self, me, size, src, dst, send_sems, recv_sems):
        self.me, self.size, self.src, self.dst, self.send_sems, self.recv_sems = me, size, src, dst, send_sems, recv_sems

    def copy(self, d, peer, slot):
        return pltpu.make_async_remote_copy(
            src_ref=self.src(peer), dst_ref=self.dst(slot), send_sem=self.send_sems.at[d], recv_sem=self.recv_sems.at[d],
            device_id={"sp": peer}, device_id_type=MESH)

    def loop(self, step):
        def body(d, carry):
            step(d)
            return carry

        lax.fori_loop(1, self.size, body, 0)

    def start(self):
        self.loop(lambda d: self.copy(d, lax.rem(self.me + d, self.size), self.me).start())

    def wait_recv(self):
        def one(d):
            peer = lax.rem(self.me + self.size - d, self.size)
            self.copy(d, peer, peer).wait_recv()

        self.loop(one)

    def wait_send(self):
        self.loop(lambda d: self.copy(d, lax.rem(self.me + d, self.size), self.me).wait_send())


def exchange_kernel(size, in_ref, out_ref, send_sems, recv_sems, local_sem):
    me = lax.axis_index("sp")
    greet_all(me, size)
    own = pltpu.make_async_copy(in_ref.at[me], out_ref.at[me], local_sem)
    own.start()
    direct = Direct(me, size, lambda j: in_ref.at[j], lambda j: out_ref.at[j], send_sems, recv_sems)
    direct.start()
    own.wait()
    direct.wait_recv()
    direct.wait_send()


def exchange(x, size, collective_id):
    nbytes = x.size * x.dtype.itemsize
    return pl.pallas_call(
        functools.partial(exchange_kernel, size),
        out_shape=jax.ShapeDtypeStruct(x.shape, x.dtype),
        in_specs=[pl.BlockSpec(memory_space=pl.ANY)],
        out_specs=pl.BlockSpec(memory_space=pl.ANY),
        scratch_shapes=[pltpu.SemaphoreType.DMA((size,)), pltpu.SemaphoreType.DMA((size,)), pltpu.SemaphoreType.DMA],
        compiler_params=pltpu.CompilerParams(collective_id=collective_id, has_side_effects=True),
        cost_estimate=pl.CostEstimate(flops=40_000_000_000, bytes_accessed=2 * nbytes, transcendentals=0),
        name="all_to_all",
    )(x)


FIRST_OF = (2, 3, 0, 1)
SENDS = (("P", 0), ("Q", 0, 0), ("P", 1), ("Q", 0, 1), ("P", 2), ("Q", 1, 0), ("Q", 0, 2), ("Q", 1, 1),
         ("Q", 2, 0), ("Q", 3, 0), ("Q", 1, 2), ("Q", 2, 1), ("Q", 3, 1), ("Q", 2, 2), ("Q", 3, 2))
LAG = 2
COLOURS = 4
HEADS_STEP = 4


def gather_kernel(size, side, dims, xn_ref, dy_ref, wq_ref, bias_ref, wo_ref, meta_ref,
                  xall_ref, qkv_ref, do_ref, metaall_ref,
                  xbuf, wbuf, wobuf, dybuf, dosend, dorecv,
                  load_sems, wo_sems, out_sems, meta_sem, ici_send, ici_recv, d2d_send, d2d_recv, do_send, do_recv, meta_send, meta_recv):
    batch, tok, head_dim, pad_dim = dims
    me = lax.axis_index("sp")
    core = lax.rem(me, 2)
    chip = me // 2
    cx, cy = lax.rem(chip, side), chip // side
    sibling = me + 1 - 2 * core

    def chip_at(dx, dy):
        return lax.rem(cy + dy + side, side) * side + lax.rem(cx + dx + side, side)

    def device_at(dx, dy):
        return chip_at(dx, dy) * 2 + core

    step_of = ((1, 0), (-1, 0), (0, 1), (0, -1))

    def back_on(link, n, other=None, m=0):
        dx, dy = step_of[link][0] * -n, step_of[link][1] * -n
        if other is not None:
            dx, dy = dx - step_of[other][0] * m, dy - step_of[other][1] * m
        return device_at(dx, dy)

    def sent_chunk(link, slot, ahead=0):
        what = SENDS[slot]
        if what[0] == "P":
            return back_on(link, what[1] + ahead), link
        first = FIRST_OF[link]
        return back_on(link, what[2] + ahead, first, what[1]), first

    def ici_copy(link, slot, arriving):
        block, colour = sent_chunk(link, slot, 1 if arriving else 0)
        ref = xbuf.at[block, colour]
        return pltpu.make_async_remote_copy(
            src_ref=ref, dst_ref=ref, send_sem=ici_send.at[link, slot], recv_sem=ici_recv.at[link, slot],
            device_id={"sp": device_at(*step_of[link])}, device_id_type=MESH)

    def d2d_copy(link, slot, from_sibling):
        block, colour = sent_chunk(link, slot, 1)
        ref = xbuf.at[block + ((1 - 2 * core) if from_sibling else 0), colour]
        return pltpu.make_async_remote_copy(
            src_ref=ref, dst_ref=ref, send_sem=d2d_send.at[slot + 1, link], recv_sem=d2d_recv.at[slot + 1, link],
            device_id={"sp": sibling}, device_id_type=MESH)

    def d2d_own(block):
        return pltpu.make_async_remote_copy(
            src_ref=xbuf.at[block], dst_ref=xbuf.at[block], send_sem=d2d_send.at[0, 0], recv_sem=d2d_recv.at[0, 0],
            device_id={"sp": sibling}, device_id_type=MESH)

    rows = xbuf.shape[2]
    loads = [pltpu.make_async_copy(xn_ref.at[pl.ds(c * rows, rows)], xbuf.at[me, c], load_sems.at[c]) for c in range(COLOURS)]
    load_dy = pltpu.make_async_copy(dy_ref, dybuf, load_sems.at[COLOURS])
    load_w = pltpu.make_async_copy(wq_ref.at[me], wbuf, load_sems.at[COLOURS + 1])
    for load in loads:
        load.start()
    load_dy.start()
    load_w.start()
    heads = wo_ref.shape[0]
    groups = heads // HEADS_STEP

    def load_wo(g):
        return pltpu.make_async_copy(wo_ref.at[pl.ds(g * HEADS_STEP, HEADS_STEP)], wobuf.at[lax.rem(g, 2)], wo_sems.at[lax.rem(g, 2)])

    load_wo(0).start()
    meta = Direct(me, size, lambda j: meta_ref, lambda j: metaall_ref.at[j], meta_send, meta_recv)
    exch = Direct(me, size, lambda j: dosend.at[j], lambda j: dorecv.at[j], do_send, do_recv)
    greet_all(me, size)
    for load in loads:
        load.wait()
    for slot in range(LAG):
        for link in range(4):
            ici_copy(link, slot, False).start()
    d2d_own(me).start()
    own_meta = pltpu.make_async_copy(meta_ref, metaall_ref.at[me], meta_sem)
    own_meta.start()
    meta.start()
    load_dy.wait()

    def do_group(g, carry):
        @pl.when(g + 1 < groups)
        def _():
            load_wo(g + 1).start()

        load_wo(g).wait()
        w = wobuf[lax.rem(g, 2)].reshape(HEADS_STEP * head_dim, -1)
        d = dot(dybuf[...], w, 1, 1).astype(jnp.bfloat16)
        for h in range(HEADS_STEP):
            pieces = [d[b * tok:(b + 1) * tok, h * head_dim:(h + 1) * head_dim] for b in range(batch)]
            fill = dosend.shape[2] - batch * head_dim
            if fill:
                pieces.append(jnp.zeros((tok, fill), jnp.bfloat16))
            dosend[g * HEADS_STEP + h] = jnp.concatenate(pieces, axis=1)
        return carry

    lax.fori_loop(0, groups, do_group, 0)
    exch.start()
    dorecv[me] = dosend[me]
    load_w.wait()

    def store_out(pair):
        return pltpu.make_async_copy(
            xbuf.at[pl.ds(pair * 2, 2)], xall_ref.at[pl.ds(pair * 2, 2)], out_sems.at[pair])

    def multiply(pair):
        store_out(pair).start()
        x = xbuf[pl.ds(pair * 2, 2)].reshape(2 * COLOURS * rows, -1)
        r = (dot(x, wbuf[...], 1, 1) + bias_ref[...]).astype(jnp.bfloat16)
        zero = jnp.zeros((r.shape[0], pad_dim - head_dim), jnp.bfloat16)
        pieces = []
        for c in range(3):
            pieces += [r[:, c * head_dim:(c + 1) * head_dim], zero]
        qkv_ref[pl.ds(pair * 2, 2)] = jnp.concatenate(pieces, axis=1).reshape(2, COLOURS * rows, 3 * pad_dim)

    slots = len(SENDS)
    for step in range(LAG, slots + LAG + 1):
        for link in range(4):
            if step - LAG < slots:
                ici_copy(link, step - LAG, True).wait_recv()
                d2d_copy(link, step - LAG, False).start()
                if step < slots:
                    ici_copy(link, step, False).start()
        for link in range(4):
            if step == LAG:
                if link == 0:
                    d2d_own(sibling).wait_recv()
            else:
                d2d_copy(link, step - LAG - 1, True).wait_recv()
        if step == 12:
            def straight(i, carry):
                multiply(chip_at(jnp.where(i < side, i, 0), jnp.where(i < side, 0, i - side + 1)))
                return carry

            lax.fori_loop(0, 2 * side - 1, straight, 0)

    def cornered(i, carry):
        multiply(chip_at(1 + i // (side - 1), 1 + lax.rem(i, side - 1)))
        return carry

    lax.fori_loop(0, (side - 1) * (side - 1), cornered, 0)
    exch.wait_recv()

    def unpack(j, carry):
        d = dorecv[j]
        for b in range(batch):
            do_ref[j, b] = jnp.concatenate(
                [d[:, b * head_dim:(b + 1) * head_dim], jnp.zeros((tok, pad_dim - head_dim), jnp.bfloat16)], axis=1)
        return carry

    lax.fori_loop(0, size, unpack, 0)
    own_meta.wait()
    meta.wait_recv()
    meta.wait_send()
    exch.wait_send()
    d2d_own(me).wait_send()
    for slot in range(slots):
        for link in range(4):
            ici_copy(link, slot, False).wait_send()
            d2d_copy(link, slot, False).wait_send()

    def stored(i, carry):
        store_out(i).wait()
        return carry

    lax.fori_loop(0, side * side, stored, 0)


def gather_qkv(x_norm, dy, wq, bias, wo, meta, size, batch, collective_id):
    tokens, hidden = x_norm.shape
    heads, head_dim, _ = wo.shape
    pad_dim = -(-head_dim // LANES) * LANES
    tok = tokens // batch
    side = math.isqrt(size // 2)
    pack = -(-batch * head_dim // LANES) * LANES
    slots = len(SENDS)
    anywhere = pl.BlockSpec(memory_space=pl.ANY)
    vmem = pl.BlockSpec(memory_space=pltpu.VMEM)
    sem = pltpu.SemaphoreType.DMA
    xall, qkv, do, metaall = pl.pallas_call(
        functools.partial(gather_kernel, size, side, (batch, tok, head_dim, pad_dim)),
        out_shape=(
            jax.ShapeDtypeStruct((size, COLOURS, tokens // COLOURS, hidden), jnp.bfloat16),
            jax.ShapeDtypeStruct((size, tokens, 3 * pad_dim), jnp.bfloat16),
            jax.ShapeDtypeStruct((size, batch, tok, pad_dim), jnp.bfloat16),
            jax.ShapeDtypeStruct((size, *meta.shape), meta.dtype),
        ),
        in_specs=[anywhere, anywhere, anywhere, vmem, anywhere, anywhere],
        out_specs=(anywhere, vmem, vmem, anywhere),
        scratch_shapes=[
            pltpu.VMEM((size, COLOURS, tokens // COLOURS, hidden), jnp.bfloat16),
            pltpu.VMEM((3 * head_dim, hidden), jnp.bfloat16),
            pltpu.VMEM((2, HEADS_STEP, head_dim, hidden), jnp.bfloat16),
            pltpu.VMEM((tokens, hidden), jnp.bfloat16),
            pltpu.VMEM((size, tok, pack), jnp.bfloat16),
            pltpu.VMEM((size, tok, pack), jnp.bfloat16),
            sem((COLOURS + 2,)), sem((2,)), sem((side * side,)), sem,
            sem((4, slots)), sem((4, slots)), sem((slots + 1, 4)), sem((slots + 1, 4)),
            sem((size,)), sem((size,)), sem((size,)), sem((size,)),
        ],
        compiler_params=pltpu.CompilerParams(collective_id=collective_id, has_side_effects=True, vmem_limit_bytes=VMEM_LIMIT),
        cost_estimate=pl.CostEstimate(flops=80_000_000_000, bytes_accessed=60_000_000, transcendentals=0),
        name="gather_qkv",
    )(x_norm, dy, wq, bias, wo, meta)
    return xall.reshape(size, batch, tok, hidden), qkv.reshape(size, batch, tok, 3 * pad_dim), do, metaall


def attn_kernel(head_dim, q_block, slope_ref, qkv_ref, do_ref, pos_ref, keep_ref, x_ref, out_ref, gw_ref,
                dk_acc, dv_acc, dq_all, o_all, d_all, x_buf, x_sems):
    seq_len, pad_dim = dk_acc.shape
    blocks, _, tok, _ = qkv_ref.shape
    b = pl.program_id(0)
    batch = x_buf.shape[0]
    scale = head_dim ** -0.5
    slope = slope_ref[0]
    pos_row = pos_ref[0]
    keep_row = keep_ref[0]
    per = q_block // tok

    def load_x(i):
        return pltpu.make_async_copy(x_ref.at[:, i], x_buf.at[i], x_sems.at[i])

    @pl.when(b == 0)
    def _():
        for i in range(batch):
            load_x(i).start()

    dk_acc[...] = jnp.zeros_like(dk_acc)
    dv_acc[...] = jnp.zeros_like(dv_acc)

    def rows(ref, lo, hi, part):
        return ref[lo * per:hi * per, 0, :, part * pad_dim:(part + 1) * pad_dim].reshape((hi - lo) * q_block, pad_dim)

    for i in range(seq_len // q_block):
        span = (i + 1) * q_block
        q = rows(qkv_ref, i, i + 1, 0)
        k = rows(qkv_ref, 0, i + 1, 1)
        v = rows(qkv_ref, 0, i + 1, 2)
        do = rows(do_ref, i, i + 1, 0)
        gap = (pos_row[:, span - 1:span] - pos_row[:, :span]).astype(jnp.float32)
        bias = jnp.where(keep_row[:, :span] > 0, -slope * gap, MASK_FILL)
        scores = dot(q, k, 1, 1) * scale + bias
        row_id = lax.broadcasted_iota(jnp.int32, (q_block, span), 0) + i * q_block
        col_id = lax.broadcasted_iota(jnp.int32, (q_block, span), 1)
        scores = jnp.where(col_id <= row_id, scores, MASK_FILL)
        expo = jnp.exp(scores - jnp.max(scores, axis=-1, keepdims=True))
        prob = expo * (1.0 / jnp.sum(expo, axis=-1, keepdims=True))
        prob_lo = prob.astype(jnp.bfloat16)
        o = dot(prob_lo, v, 1, 0).astype(jnp.bfloat16)
        row_dot = jnp.sum(do.astype(jnp.float32) * o.astype(jnp.float32), axis=-1, keepdims=True)
        ds_lo = (prob * (dot(do, v, 1, 1) - row_dot)).astype(jnp.bfloat16)
        o_all[i * q_block:span, :] = o
        dq_all[i * q_block:span, :] = (dot(ds_lo, k, 1, 0) * scale).astype(jnp.bfloat16)
        dv_acc[:span, :] += dot(prob_lo, do, 0, 0)
        dk_acc[:span, :] += dot(ds_lo, q, 0, 0)
    dk = (dk_acc[...] * scale).astype(jnp.bfloat16)
    dv = dv_acc[...].astype(jnp.bfloat16)
    d_all[...] = jnp.concatenate([dq_all[:, :head_dim], dk[:, :head_dim], dv[:, :head_dim]], axis=1)
    whole = jnp.concatenate([d_all[...], o_all[:, :head_dim]], axis=1)
    out_ref[:, 0] = whole.reshape(blocks, tok, 4 * head_dim)
    load_x(b).wait()
    width = 512

    def columns(n, carry):
        at = pl.ds(pl.multiple_of(n * width, width), width)
        term = dot(d_all[...], x_buf[b, :, :, at].reshape(seq_len, width), 0, 0)

        @pl.when(b == 0)
        def _():
            gw_ref[:, at] = term

        @pl.when(b > 0)
        def _():
            gw_ref[:, at] += term

        return carry

    hidden = gw_ref.shape[1]
    if hidden % width:
        term = dot(d_all[...], x_buf[b].reshape(seq_len, hidden), 0, 0)
        gw_ref[...] = jnp.where(b == 0, term, gw_ref[...] + term)
    else:
        lax.fori_loop(0, hidden // width, columns, 0)


def attention(slope, qkv, do, pos, keep, x_all, head_dim, q_block):
    blocks, batch, tok, wide = qkv.shape
    hidden = x_all.shape[-1]
    pad_dim = wide // 3
    seq_len = blocks * tok
    flops = 6 * batch * seq_len * seq_len * 256 + 2 * batch * seq_len * 3 * head_dim * hidden
    return pl.pallas_call(
        functools.partial(attn_kernel, head_dim, q_block),
        grid=(batch,),
        out_shape=(jax.ShapeDtypeStruct((blocks, batch, tok, 4 * head_dim), jnp.bfloat16),
                   jax.ShapeDtypeStruct((3 * head_dim, hidden), jnp.float32)),
        in_specs=[
            pl.BlockSpec(memory_space=pltpu.SMEM),
            pl.BlockSpec((blocks, 1, tok, wide), lambda b: (0, b, 0, 0)),
            pl.BlockSpec((blocks, 1, tok, pad_dim), lambda b: (0, b, 0, 0)),
            pl.BlockSpec((1, 1, seq_len), lambda b: (b, 0, 0)),
            pl.BlockSpec((1, 1, seq_len), lambda b: (b, 0, 0)),
            pl.BlockSpec(memory_space=pl.ANY),
        ],
        out_specs=(pl.BlockSpec((blocks, 1, tok, 4 * head_dim), lambda b: (0, b, 0, 0)),
                   pl.BlockSpec((3 * head_dim, hidden), lambda b: (0, 0))),
        scratch_shapes=[pltpu.VMEM((seq_len, pad_dim), jnp.float32)] * 2 + [pltpu.VMEM((seq_len, pad_dim), jnp.bfloat16)] * 2 + [
            pltpu.VMEM((seq_len, 3 * head_dim), jnp.bfloat16),
            pltpu.VMEM((batch, blocks, tok, hidden), jnp.bfloat16),
            pltpu.SemaphoreType.DMA((batch,)),
        ],
        compiler_params=pltpu.CompilerParams(vmem_limit_bytes=VMEM_LIMIT),
        cost_estimate=pl.CostEstimate(flops=flops, bytes_accessed=50_000_000, transcendentals=batch * seq_len * seq_len // 2),
        name="attention",
    )(slope, qkv, do, pos, keep, x_all)


def outgrad_kernel(head_dim, parts_ref, dy_ref, after_ref, gw_ref):
    blocks, tokens, wide = parts_ref.shape
    o = parts_ref[...].reshape(blocks * tokens, wide)[:, wide - head_dim:]
    term = dot(o, dy_ref[...].reshape(blocks * tokens, -1), 0, 0)

    @pl.when(pl.program_id(0) == 0)
    def _():
        gw_ref[...] = term

    @pl.when(pl.program_id(0) > 0)
    def _():
        gw_ref[...] += term


def outgrad(parts, dy_all, after, head_dim):
    size, tokens, wide = parts.shape
    hidden = dy_all.shape[-1]
    step = 2
    return pl.pallas_call(
        functools.partial(outgrad_kernel, head_dim),
        grid=(size // step,),
        out_shape=jax.ShapeDtypeStruct((head_dim, hidden), jnp.float32),
        in_specs=[pl.BlockSpec((step, tokens, wide), lambda i: (i, 0, 0)),
                  pl.BlockSpec((step, tokens, hidden), lambda i: (i, 0, 0)),
                  pl.BlockSpec(memory_space=pl.ANY)],
        out_specs=pl.BlockSpec((head_dim, hidden), lambda i: (0, 0)),
        compiler_params=pltpu.CompilerParams(vmem_limit_bytes=VMEM_LIMIT),
        cost_estimate=pl.CostEstimate(flops=10_000_000_000, bytes_accessed=40_000_000, transcendentals=0),
        name="outgrad",
    )(parts, dy_all, after)


def token_kernel(head_dim, chunk, parts_ref, wq_ref, wo_ref, x_ref, dy_ref, gain_ref, bout_ref,
                 y_ref, gx_ref, bq_ref, sums_ref, dn_acc, y_acc):
    n = pl.program_id(0)
    parts = parts_ref[0]
    dqkv = parts[:, :3 * head_dim]
    o = parts[:, 3 * head_dim:]
    bq_ref[0] = jnp.sum(dqkv.astype(jnp.float32), axis=0, keepdims=True)
    dn_term = dot(dqkv, wq_ref[0], 1, 0)
    y_term = dot(o, wo_ref[0], 1, 0)

    @pl.when(n == 0)
    def _():
        dn_acc[...] = dn_term
        y_acc[...] = y_term

    @pl.when(n > 0)
    def _():
        dn_acc[...] += dn_term
        y_acc[...] += y_term

    @pl.when(n == pl.num_programs(0) - 1)
    def _():
        sums_ref[...] = jnp.zeros_like(sums_ref)
        gain = gain_ref[...]
        bout = bout_ref[...]

        def body(c, carry):
            at = pl.ds(pl.multiple_of(c * chunk, chunk), chunk)
            x = x_ref[at, :].astype(jnp.float32)
            dy = dy_ref[at, :].astype(jnp.float32)
            centered = x - jnp.mean(x, axis=-1, keepdims=True)
            inv_std = lax.rsqrt(jnp.mean(centered * centered, axis=-1, keepdims=True) + NORM_EPS)
            x_hat = centered * inv_std
            d_norm = dn_acc[at, :]
            d_hat = d_norm * gain
            d_mean = jnp.mean(d_hat, axis=-1, keepdims=True)
            d_proj = jnp.mean(d_hat * x_hat, axis=-1, keepdims=True)
            gx_ref[at, :] = (dy + inv_std * (d_hat - d_mean - x_hat * d_proj)).astype(jnp.bfloat16)
            y_ref[at, :] = (x + y_acc[at, :] + bout).astype(jnp.bfloat16)
            sums_ref[0:1, :] += jnp.sum(d_norm * x_hat, axis=0, keepdims=True)
            sums_ref[1:2, :] += jnp.sum(d_norm, axis=0, keepdims=True)
            sums_ref[2:3, :] += jnp.sum(dy, axis=0, keepdims=True)
            return carry

        lax.fori_loop(0, x_ref.shape[0] // chunk, body, 0)


def token_side(parts, wq, wo, x, dy, gain, bout, head_dim):
    heads, tokens, _ = parts.shape
    hidden = x.shape[1]
    whole = lambda n: (0, 0)
    per_head = lambda n: (n, 0, 0)
    return pl.pallas_call(
        functools.partial(token_kernel, head_dim, 16),
        grid=(heads,),
        out_shape=(
            jax.ShapeDtypeStruct((tokens, hidden), jnp.bfloat16),
            jax.ShapeDtypeStruct((tokens, hidden), jnp.bfloat16),
            jax.ShapeDtypeStruct((heads, 1, 3 * head_dim), jnp.float32),
            jax.ShapeDtypeStruct((8, hidden), jnp.float32),
        ),
        in_specs=[
            pl.BlockSpec((1, tokens, 4 * head_dim), per_head),
            pl.BlockSpec((1, 3 * head_dim, hidden), per_head),
            pl.BlockSpec((1, head_dim, hidden), per_head),
            pl.BlockSpec((tokens, hidden), whole),
            pl.BlockSpec((tokens, hidden), whole),
            pl.BlockSpec((1, hidden), whole),
            pl.BlockSpec((1, hidden), whole),
        ],
        out_specs=(
            pl.BlockSpec((tokens, hidden), whole),
            pl.BlockSpec((tokens, hidden), whole),
            pl.BlockSpec((1, 1, 3 * head_dim), per_head),
            pl.BlockSpec((8, hidden), whole),
        ),
        scratch_shapes=[pltpu.VMEM((tokens, hidden), jnp.float32)] * 2,
        compiler_params=pltpu.CompilerParams(vmem_limit_bytes=VMEM_LIMIT),
        cost_estimate=pl.CostEstimate(
            flops=2 * tokens * hidden * 4 * heads * head_dim, bytes_accessed=8 * hidden * heads * head_dim, transcendentals=0),
        name="token_side",
    )(parts, wq, wo, x, dy, gain, bout)


def settle_kernel(block, depth, ahead, src_ref, *refs):
    dst_ref, buf, read_sems, write_sems = refs[-4:]
    count = src_ref.shape[0] // block

    def at(i):
        return pl.ds(pl.multiple_of(i * block, block), block)

    def read(i):
        return pltpu.make_async_copy(src_ref.at[at(i)], buf.at[lax.rem(i, depth)], read_sems.at[lax.rem(i, depth)])

    def write(i):
        return pltpu.make_async_copy(buf.at[lax.rem(i, depth)], dst_ref.at[at(i)], write_sems.at[lax.rem(i, depth)])

    def step(i, carry):
        @pl.when(jnp.logical_and(i >= depth, i < count))
        def _():
            write(i - depth).wait()

        @pl.when(i < count)
        def _():
            read(i).start()

        @pl.when(i >= ahead)
        def _():
            read(i - ahead).wait()
            write(i - ahead).start()

        return carry

    lax.fori_loop(0, count + ahead, step, 0)

    def drain(i, carry):
        write(i).wait()
        return carry

    lax.fori_loop(max(0, count - depth), count, drain, 0)


def settle(x, block, after=()):
    depth, ahead = 12, 6
    rows, cols = x.shape
    sem = pltpu.SemaphoreType.DMA((depth,))
    return pl.pallas_call(
        functools.partial(settle_kernel, block, depth, ahead),
        out_shape=jax.ShapeDtypeStruct(x.shape, x.dtype),
        in_specs=[pl.BlockSpec(memory_space=pl.ANY)] * (1 + len(after)),
        out_specs=pl.BlockSpec(memory_space=pl.ANY),
        scratch_shapes=[pltpu.VMEM((depth, block, cols), x.dtype), sem, sem],
        cost_estimate=pl.CostEstimate(flops=10_000_000_000, bytes_accessed=8 * rows * cols, transcendentals=0),
        name="settle",
    )(x, *after)


def solution(mesh):
    size = mesh.shape["sp"]

    def block_fn(x_blk, pos_blk, keep_blk, ln_gain, ln_bias, w_qkv, b_qkv, w_out, b_out, dy_blk):
        batch, tok, hidden = x_blk.shape
        heads, head_dim = w_qkv.shape[1], w_qkv.shape[3]
        tokens, seq_len = batch * tok, size * tok
        rank = lax.axis_index("sp")
        wq = jnp.transpose(w_qkv, (1, 2, 3, 0)).reshape(heads, 3 * head_dim, hidden)
        wo = w_out.reshape(heads, head_dim, hidden)
        dy_flat = dy_blk.reshape(tokens, hidden)

        def gather(a):
            return lax.all_gather(a, "sp", axis=0, tiled=True)

        x_norm = norm_forward(x_blk, ln_gain, ln_bias).reshape(tokens, hidden)
        meta = jnp.pad(jnp.concatenate([pos_blk, keep_blk], axis=0), ((0, 8 - 2 * batch), (0, LANES - tok)))
        bias = lax.dynamic_slice_in_dim(b_qkv, rank, 1, 0).reshape(1, 3 * head_dim)
        x_all, qkv, do_head, meta_all = gather_qkv(x_norm, dy_flat, wq, bias, wo, meta, size, batch, 0)
        dy_later, meta_all = lax.optimization_barrier((dy_flat, meta_all))
        dy_all = gather(dy_later)

        meta_all = jnp.transpose(meta_all[:, :2 * batch, :tok], (1, 0, 2)).reshape(2 * batch, 1, seq_len)
        slope = jnp.exp2(-8.0 * (rank + 1).astype(jnp.float32) / heads).reshape(1)
        parts, grad_head = attention(slope, qkv, do_head, meta_all[:batch], meta_all[batch:], x_all, head_dim, min(256, seq_len))

        flat = parts.reshape(size, tokens * 4 * head_dim // LANES, LANES)
        parts_tok = exchange(flat, size, 1).reshape(heads, tokens, 4 * head_dim)
        y, grad_x, bq_part, sums = token_side(
            parts_tok, wq, wo, x_blk.reshape(tokens, hidden), dy_flat, ln_gain.reshape(1, hidden), b_out.reshape(1, hidden), head_dim)
        grad_wq = settle(gather(grad_head), head_dim)
        grad_out = outgrad(parts.reshape(size, tokens, 4 * head_dim), dy_all.reshape(size, tokens, hidden), parts_tok, head_dim)
        grad_wo = settle(gather(grad_out), head_dim, after=(grad_wq,))
        bq, gain, bias_sum, bo = lax.psum((bq_part.reshape(-1), sums[0], sums[1], sums[2]), "sp")
        grad_wq = jnp.transpose(grad_wq.reshape(heads, 3, head_dim, hidden), (3, 0, 1, 2))
        return (y.reshape(x_blk.shape), grad_x.reshape(x_blk.shape), grad_wq, bq.reshape(heads, 3, head_dim), grad_wo,
                bo, gain, bias_sum)

    act_spec = P("dp", "sp", None)
    tok_spec = P("dp", "sp")
    in_specs = (act_spec, tok_spec, tok_spec, P(), P(), P(), P(), P(), P(), act_spec)
    out_specs = (act_spec, act_spec, P("dp", None, None, None), P("dp", None, None), P("dp", None), P("dp"), P("dp"), P("dp"))
    return jax.shard_map(block_fn, mesh=mesh, in_specs=in_specs, out_specs=out_specs, check_vma=False)
```

time: 689 us -> 626 us (0.909)
  matrix products: 66.1 us -> 0 us
  Pallas kernels: 346 us -> 400 us
  waiting for transfers between devices: 161 us -> 131 us
  local copies, waits for them, and re-layouts: 39.2 us -> 25.1 us
    dot_general x4 -> x0, matrix products: 66.1 us -> none  [the longest x3 56.7 us: dot(): lax.dot_general(a, b, (((ca,), (cb,)), ((), ())), preferred_element_type=...]
    pallas_call x7 -> x5, Pallas kernels: 258 us -> 299 us  [the longest x1 124 us: gather_qkv(): pl.pallas_call(functools.partial(gather_kernel, size, side, (batch, tok,...]
    all_gather x6 -> x3, waiting for transfers between devices: 159 us -> 131 us  [gather(): return lax.all_gather(a, 'sp', axis=0, tiled=True)]
    pallas_call x1, Pallas kernels: 38.1 us -> 52.4 us  [attention(): pl.pallas_call(functools.partial(attn_kernel, head_dim, q_block), grid=(b...]
    reshape x3 -> x2, local copies, waits for them, and re-layouts: 15.2 us -> 9.4 us  [the longest x1 8.75 us: block_fn(): parts_tok = exchange(flat, size, 1).reshape(heads, tokens, 4 * head_dim)]
  transfers between devices with their start and end apart: 6 -> 3, of which waited for: 4 -> 2; matrix products, arithmetic and copies ran while one was open for 16% -> 4% of each run, Pallas kernels for 28% -> 28%
where the time goes in v2:
time: 626 us; the launch traced here: 624 us
  Pallas kernels  400 us (64%)
  waiting for transfers between devices  131 us (21%)
  blocking collectives  48.7 us (8%)
  local copies, waits for them, and re-layouts  25.1 us (4%)
  between operations  14 us (2%)
    all_gather x3, waiting for transfers between devices, gather(): return lax.all_gather(a, 'sp', axis=0, tiled=True)  131 us
    pallas_call x1, Pallas kernels, gather_qkv(): pl.pallas_call(functools.partial(gather_kernel, size, side, (batch, tok,...  124 us
    pallas_call x1, Pallas kernels, exchange(): pl.pallas_call(functools.partial(exchange_kernel, size), out_shape=jax.Sh...  85.7 us
    pallas_call x2, Pallas kernels, settle(): pl.pallas_call(functools.partial(settle_kernel, block, depth, ahead), out...  68.6 us
    pallas_call x1, Pallas kernels, attention(): pl.pallas_call(functools.partial(attn_kernel, head_dim, q_block), grid=(b...  52.4 us
    psum x1, blocking collectives, block_fn(): lax.psum((bq_part.reshape(-1), sums[0], sums[1], sums[2]), 'sp')  48.7 us
    pallas_call x1, Pallas kernels, token_side(): pl.pallas_call(functools.partial(token_kernel, head_dim, 16), grid=(heads...  48.4 us
    pallas_call x1, Pallas kernels, outgrad(): pl.pallas_call(functools.partial(outgrad_kernel, head_dim), grid=(size //...  21.1 us
  transfers between devices with their start and end apart: 3, of which 2 were waited for; matrix products, arithmetic and copies ran while one was open for 4% of the time, Pallas kernels for 28%

profile of v2, /device:TPU:97, one launch (start us, length us, event | category | flops | bytes accessed | tf_op | source)
XLA Modules:
  0.0 624.3 jit_solution(17770441935711813708)
XLA Ops:
  7.3 1.5 convert_reduce_fusion
  8.9 1.6 fusion.2
  10.5 0.6 reshape.97.bias_ref
  11.8 1.4 fusion.5
  13.2 123.6 %gather_qkv.1 = (bf16[32,4,48,2560]{3,2,1,0:T(8,128)(2,1)}, bf16[32,192,384]{2,1,0:T(8,128)(2,1)}, bf16[32,3,64,128]{3,2,1,0:T(8,128)(2,1)}, s32[32,8,128]{2,1,0:T(8,128)}) custom-call(bf16[192,2560]{1,0:T(8,128)(2,1)} %bitcast.31, bf16[192,2560]{1,0:T(8,128)(2,1)} %bitcast.28, bf16[32,240,2560]{2,1,0:T(8,128)(2,1)} %bitcast.21, f32[1,240]{1,0:T(1,128)} %reshape.97.bias_ref, ...), custom_call_target="tpu_custom_call" | custom-call | flops 80000000000 | bytes 60000000 | tf_op jit(solution)/shard_map/gather_qkv/pallas_call | solution.py:283
  137.1 0.9 slice_bitcast_fusion
  138.1 0.7 slice.26.pos_ref
  138.8 0.7 slice.28.keep_ref
  139.5 52.4 %attention.1 = (bf16[32,3,64,320]{3,2,1,0:T(8,128)(2,1)}, f32[240,2560]{1,0:T(8,128)}) custom-call(f32[1]{0:T(128)} %bitcast.slope_ref, bf16[32,3,64,384]{3,2,1,0:T(8,128)(2,1)} %bitcast.35, bf16[32,3,64,128]{3,2,1,0:T(8,128)(2,1)} %get-tuple-element.21.do_ref, s32[3,1,2048]{2,1,0:T(1,128)} %slice.26.pos_ref, s32[3,1,2048]{2,1,0:T(1,128)} %slice.28.keep_ref, ...), custom_call_target="tpu_custom_call" | custom-call | flops 26877100032 | bytes 50000000 | tf_op jit(solution)/shard_map/attention/pallas_call | solution.py:395
  192.2 9.6 %reshape.101.in_ref = bf16[32,480,128]{2,1,0:T(8,128)(2,1)} reshape(bf16[32,3,64,320]{3,2,1,0:T(8,128)(2,1)} %get-tuple-element.25) | data formatting | bytes 7864320 | tf_op jit(solution)/shard_map/reshape | solution.py:616
  201.8 85.7 %all_to_all.1 = bf16[32,480,128]{2,1,0:T(8,128)(2,1)} custom-call(bf16[32,480,128]{2,1,0:T(8,128)(2,1)} %reshape.101.in_ref), custom_call_target="tpu_custom_call" | custom-call | flops 40000000000 | bytes 7864320 | tf_op jit(solution)/shard_map/all_to_all/pallas_call | solution.py:84
  287.5 8.7 %reshape.102.parts_ref.after_ref = bf16[32,192,320]{2,1,0:T(8,128)(2,1)} reshape(bf16[32,480,128]{2,1,0:T(8,128)(2,1)} %all_to_all.1) | data formatting | bytes 7864320 | tf_op jit(solution)/shard_map/reshape | solution.py:617
  296.3 21.1 %outgrad.1 = f32[80,2560]{1,0:T(8,128)} custom-call(bf16[32,192,320]{2,1,0:T(8,128)(2,1)} %bitcast.24, bf16[32,192,2560]{2,1,0:T(8,128)(2,1)} %bitcast.23, bf16[32,192,320]{2,1,0:T(8,128)(2,1)} %reshape.102.parts_ref.after_ref), custom_call_target="tpu_custom_call" | custom-call | flops 10000000000 | bytes 40000000 | tf_op jit(solution)/shard_map/outgrad/pallas_call | solution.py:439
  317.5 0.6 reshape.104.gain_ref
  318.1 0.6 reshape.105.bout_ref
  318.7 48.4 %token_side.1 = (bf16[192,2560]{1,0:T(8,128)(2,1)}, bf16[192,2560]{1,0:T(8,128)(2,1)}, f32[32,1,240]{2,1,0:T(1,128)}, f32[8,2560]{1,0:T(8,128)}) custom-call(bf16[32,192,320]{2,1,0:T(8,128)(2,1)} %reshape.102.parts_ref.after_ref, bf16[32,240,2560]{2,1,0:T(8,128)(2,1)} %bitcast.22, bf16[32,80,2560]{2,1,0:T(8,128)(2,1)} %bitcast.27, ...), custom_call_target="tpu_custom_call" | custom-call | flops 10066329600 | bytes 52428800 | tf_op jit(solution)/shard_map/token_side/pallas_call | solution.py:505
  367.1 0.8 reduce.1
  368.0 1.1 slice_reduce_fusion
  369.2 48.7 %all-reduce.1 = (f32[32,3,80]{2,1,0:T(4,128)S(1)}, f32[2560]{0:T(1024)}, f32[2560]{0:T(1024)}, f32[2560]{0:T(1024)}) all-reduce(f32[32,3,80]{2,1,0:T(4,128)S(1)} %reshape.110, f32[2560]{0:T(1024)S(1)} %get-tuple-element.42, f32[2560]{0:T(1024)S(1)} %get-tuple-element.41, ...), channel_id=1, replica_groups=mesh['dp'=1,'sp'=32] {'sp'}, use_global_device_ids=true, to_apply=%region_2.3 | all-reduce | flops 15360 | bytes 122880 | tf_op jit(solution)/shard_map/psum | solution.py:623
  417.9 0.6 copy.23
  418.5 91.0 %all-gather.4.cloned.1.call-done.src_ref = f32[7680,2560]{1,0:T(8,128)} async-done(((f32[240,2560]{1,0:T(8,128)}), f32[7680,2560]{1,0:T(8,128)}) %all-gather.4.cloned.1.call-update) | async-done | bytes 78643216 | tf_op jit(solution)/shard_map/all_gather | solution.py:603
  509.5 50.8 %settle.2.refs_0_ = f32[7680,2560]{1,0:T(8,128)} custom-call(f32[7680,2560]{1,0:T(8,128)} %all-gather.4.cloned.1.call-done.src_ref), custom_call_target="tpu_custom_call" | custom-call | flops 10000000000 | bytes 157286400 | tf_op jit(solution)/shard_map/settle/pallas_call | solution.py:579
  560.3 39.5 %all-gather.8.cloned.1.call-done.src_ref = f32[2560,2560]{1,0:T(8,128)} async-done(((f32[80,2560]{1,0:T(8,128)}), f32[2560,2560]{1,0:T(8,128)}) %all-gather.8.cloned.1.call-update) | async-done | bytes 26214416 | tf_op jit(solution)/shard_map/all_gather | solution.py:603
  599.9 17.8 %settle.3 = f32[2560,2560]{1,0:T(8,128)} custom-call(f32[2560,2560]{1,0:T(8,128)} %all-gather.8.cloned.1.call-done.src_ref, f32[7680,2560]{1,0:T(8,128)} %settle.2.refs_0_), custom_call_target="tpu_custom_call" | custom-call | flops 10000000000 | bytes 52428800 | tf_op jit(solution)/shard_map/settle/pallas_call | solution.py:579
  (34 shorter events, 1.6 us)
Async XLA Ops:
  7.2 3.3 copy-start
  7.2 4.6 copy-start.2
  7.2 3.9 copy-start.7
  7.2 3.9 copy-start.8
  7.2 4.5 copy-start.5
  7.2 4.5 copy-start.3
  7.3 289.0 %all-gather.6.cloned.1.call-start = ((), (), s32[]{:S(2)}) async-start(), calls=%async_computation.1 | async-start | bytes 32440320 | tf_op jit(solution)/shard_map/all_gather | solution.py:603
  136.8 372.7 %all-gather.4.cloned.1.call-start = ((), (), s32[]{:S(2)}) async-start(), calls=%async_computation | async-start | bytes 81100800 | tf_op jit(solution)/shard_map/all_gather | solution.py:603
  191.9 407.9 %all-gather.8.cloned.1.call-start = ((), (), s32[]{:S(2)}) async-start(), calls=%async_computation.2 | async-start | bytes 27033600 | tf_op jit(solution)/shard_map/all_gather | solution.py:603
  296.3 21.2 %copy-start.4 = (f32[2560]{0:T(1024)S(1)}, f32[2560]{0:T(1024)}, u32[]{:S(2)}) copy-start(f32[2560]{0:T(1024)} %param.13) | copy-start | bytes 30724
  296.3 21.8 %copy-start.6 = (f32[2560]{0:T(1024)S(1)}, f32[2560]{0:T(1024)}, u32[]{:S(2)}) copy-start(f32[2560]{0:T(1024)} %param.18) | copy-start | bytes 30724
  599.9 17.9 %copy-start.1 = (f32[32,3,80]{2,0,1:T(8,128)S(1)}, f32[32,3,80]{2,0,1:T(8,128)}, u32[]{:S(2)}) copy-start(f32[32,3,80]{2,0,1:T(8,128)} %param.16) | copy-start | bytes 92164
Sparse Core Ops, SparseCore 0:
  137.0 142.9 all-gather.5
  282.0 227.5 all-gather.3
  511.6 88.2 all-gather.7

commit v3 on v1

v3 whole, which is shorter than its diff:
```python
import functools
import math

import jax
import jax.numpy as jnp
from jax import lax
from jax.experimental import pallas as pl
from jax.experimental.pallas import tpu as pltpu
from jax.sharding import PartitionSpec as P

NORM_EPS = 1e-5
MASK_FILL = -1e30
LANES = 128
MESH = pl.DeviceIdType.MESH
VMEM_LIMIT = 61 * 1024 * 1024


def dot(a, b, ca, cb):
    return lax.dot_general(a, b, (((ca,), (cb,)), ((), ())), preferred_element_type=jnp.float32)


def norm_forward(x_blk, ln_gain, ln_bias):
    x_f32 = x_blk.astype(jnp.float32)
    centered = x_f32 - jnp.mean(x_f32, axis=-1, keepdims=True)
    inv_std = lax.rsqrt(jnp.mean(centered * centered, axis=-1, keepdims=True) + NORM_EPS)
    return (centered * inv_std * ln_gain + ln_bias).astype(jnp.bfloat16)


def greet_all(me, size):
    barrier = pltpu.get_barrier_semaphore()

    def greet(d, carry):
        pl.semaphore_signal(barrier, inc=1, device_id={"sp": lax.rem(me + d, size)}, device_id_type=MESH)
        return carry

    lax.fori_loop(1, size, greet, 0)
    pl.semaphore_wait(barrier, size - 1)


class Direct:
    def __init__(self, me, size, src, dst, send_sems, recv_sems):
        self.me, self.size, self.src, self.dst, self.send_sems, self.recv_sems = me, size, src, dst, send_sems, recv_sems

    def copy(self, d, peer, slot):
        return pltpu.make_async_remote_copy(
            src_ref=self.src(peer), dst_ref=self.dst(slot), send_sem=self.send_sems.at[d], recv_sem=self.recv_sems.at[d],
            device_id={"sp": peer}, device_id_type=MESH)

    def loop(self, step):
        def body(d, carry):
            step(d)
            return carry

        lax.fori_loop(1, self.size, body, 0)

    def start(self):
        self.loop(lambda d: self.copy(d, lax.rem(self.me + d, self.size), self.me).start())

    def wait_recv(self):
        def one(d):
            peer = lax.rem(self.me + self.size - d, self.size)
            self.copy(d, peer, peer).wait_recv()

        self.loop(one)

    def wait_send(self):
        self.loop(lambda d: self.copy(d, lax.rem(self.me + d, self.size), self.me).wait_send())


def exchange_kernel(size, in_ref, out_ref, send_sems, recv_sems, local_sem):
    me = lax.axis_index("sp")
    greet_all(me, size)
    own = pltpu.make_async_copy(in_ref.at[me], out_ref.at[me], local_sem)
    own.start()
    direct = Direct(me, size, lambda j: in_ref.at[j], lambda j: out_ref.at[j], send_sems, recv_sems)
    direct.start()
    own.wait()
    direct.wait_recv()
    direct.wait_send()


def exchange(x, size, collective_id):
    nbytes = x.size * x.dtype.itemsize
    return pl.pallas_call(
        functools.partial(exchange_kernel, size),
        out_shape=jax.ShapeDtypeStruct(x.shape, x.dtype),
        in_specs=[pl.BlockSpec(memory_space=pl.ANY)],
        out_specs=pl.BlockSpec(memory_space=pl.ANY),
        scratch_shapes=[pltpu.SemaphoreType.DMA((size,)), pltpu.SemaphoreType.DMA((size,)), pltpu.SemaphoreType.DMA],
        compiler_params=pltpu.CompilerParams(collective_id=collective_id, has_side_effects=True),
        cost_estimate=pl.CostEstimate(flops=40_000_000_000, bytes_accessed=2 * nbytes, transcendentals=0),
        name="all_to_all",
    )(x)


FIRST_OF = (2, 3, 0, 1)
CYCLE = (("P", 0), ("Q", 0, 0), ("Q", 3, 2), ("P", 1), ("Q", 0, 1), ("Q", 1, 0), ("Q", 2, 0), ("P", 2), ("Q", 1, 1),
         ("Q", 2, 1), ("Q", 3, 0), ("Q", 1, 2), ("Q", 2, 2), ("Q", 3, 1), ("Q", 0, 2))
LATE = 2
LAG = 3
COLOURS = 4
READY = 6
STEP_OF = ((1, 0), (-1, 0), (0, 1), (0, -1))


def block_kernel(size, side, dims, own_ref, wq_ref, bias_ref, wo_ref, meta_ref, slope_ref,
                 gat_ref, parts_ref, partstok_ref, gwq_ref, gwo_ref,
                 stage, wbuf, wobuf, metabuf, rowbuf, sbuf, qkvb, dob, dk_acc, dv_acc, dq_all, o_all, d_all, pbuf,
                 load_sems, own_sems, piece_sems, parts_sem, ici_send, ici_recv, d2d_send, d2d_recv, own_send, own_recv,
                 meta_send, meta_recv, part_send, part_recv):
    batch, tok, head_dim, pad_dim, hidden, q_block = dims
    seq_len = size * tok
    me = lax.axis_index("sp")
    core = lax.rem(me, 2)
    chip = me // 2
    cx, cy = lax.rem(chip, side), chip // side
    flip = 1 - 2 * core
    sibling = me + flip
    places = len(CYCLE)
    scale = head_dim ** -0.5
    slope = slope_ref[0]

    def device_at(dx, dy):
        return (lax.rem(cy + dy + side, side) * side + lax.rem(cx + dx + side, side)) * 2 + core

    def chunk(link, place, ahead):
        what = CYCLE[place]
        if what[0] == "P":
            first, n, m = link, what[1] + ahead, 0
        else:
            first, n, m = FIRST_OF[link], what[2] + ahead, what[1]
        dx = -STEP_OF[link][0] * n - STEP_OF[first][0] * m
        dy = -STEP_OF[link][1] * n - STEP_OF[first][1] * m
        return device_at(dx, dy), first

    def send(b, link, place):
        block, colour = chunk(link, place, 0)
        dst = gat_ref.at[b, block, colour]
        return pltpu.make_async_remote_copy(
            src_ref=stage.at[b, colour] if CYCLE[place] in (("P", 0), ("Q", 0, 0)) else dst, dst_ref=dst,
            send_sem=ici_send.at[b, link, place], recv_sem=ici_recv.at[b, link, place],
            device_id={"sp": device_at(*STEP_OF[link])}, device_id_type=MESH)

    def arrival(b, link, place):
        block, colour = chunk(link, place, 1)
        ref = gat_ref.at[b, block, colour]
        return pltpu.make_async_remote_copy(
            src_ref=ref, dst_ref=ref, send_sem=ici_send.at[b, link, place], recv_sem=ici_recv.at[b, link, place],
            device_id={"sp": me}, device_id_type=MESH)

    def share(b, link, place, shift):
        block, colour = chunk(link, place, 1)
        ref = gat_ref.at[b, block + shift, colour]
        return pltpu.make_async_remote_copy(
            src_ref=ref, dst_ref=ref, send_sem=d2d_send.at[b, link, place], recv_sem=d2d_recv.at[b, link, place],
            device_id={"sp": sibling}, device_id_type=MESH)

    def share_own(b, block):
        return pltpu.make_async_remote_copy(
            src_ref=stage.at[b], dst_ref=gat_ref.at[b, block], send_sem=own_send.at[b], recv_sem=own_recv.at[b],
            device_id={"sp": sibling}, device_id_type=MESH)

    def keep_own(b):
        return pltpu.make_async_copy(stage.at[b], gat_ref.at[b, me], own_sems.at[b])

    load_own = pltpu.make_async_copy(own_ref, stage, load_sems.at[0])
    load_wq = pltpu.make_async_copy(wq_ref.at[me], wbuf, load_sems.at[1])
    load_wo = pltpu.make_async_copy(wo_ref.at[me], wobuf, load_sems.at[2])
    own_meta = pltpu.make_async_copy(meta_ref, metabuf.at[me], load_sems.at[3])
    for load in (load_own, load_wq, load_wo, own_meta):
        load.start()
    meta = Direct(me, size, lambda j: meta_ref, lambda j: metabuf.at[j], meta_send, meta_recv)
    early = batch - 1
    trades = [Direct(me, size, lambda j, b=b: parts_ref.at[b, j], lambda j, b=b: partstok_ref.at[j, b], part_send.at[b], part_recv.at[b])
              for b in range(early)]
    own_parts = [pltpu.make_async_copy(parts_ref.at[b, me], partstok_ref.at[me, b], load_sems.at[4 + b]) for b in range(early)]
    greet_all(me, size)
    load_own.wait()

    group = sbuf.shape[1]
    pieces = size // group
    piece_rows = group * tok

    def load_piece(b, p):
        return pltpu.make_async_copy(gat_ref.at[b, pl.ds(p * group, group)], sbuf.at[lax.rem(p, 2)], piece_sems.at[lax.rem(p, 2)])

    def rows_of(p, which, at=slice(None)):
        return sbuf[lax.rem(p, 2), :, :, which, :, at].reshape(piece_rows, -1)

    def stream(b, lo, hi, use):
        def body(p, carry):
            @pl.when(p + 1 < pieces)
            def _():
                load_piece(b, p + 1).start()

            load_piece(b, p).wait()
            use(p)
            return carry

        lax.fori_loop(lo, hi, body, 0)

    def pad_lanes(a):
        return jnp.concatenate([a, jnp.zeros((a.shape[0], pad_dim - head_dim), a.dtype)], axis=1)

    def project(p):
        at = pl.ds(pl.multiple_of(p * piece_rows, piece_rows), piece_rows)
        r = (dot(rows_of(p, 1), wbuf[...], 1, 1) + bias_ref[...]).astype(jnp.bfloat16)
        for c in range(3):
            qkvb[at, c * pad_dim:(c + 1) * pad_dim] = pad_lanes(r[:, c * head_dim:(c + 1) * head_dim])
        dob[at, :] = pad_lanes(dot(rows_of(p, 0), wobuf[...], 1, 1).astype(jnp.bfloat16))

    def attend(b, i):
        span = (i + 1) * q_block
        mine = slice(i * q_block, span)
        q, k, v = qkvb[mine, :pad_dim], qkvb[:span, pad_dim:2 * pad_dim], qkvb[:span, 2 * pad_dim:]
        do = dob[mine, :]
        pos = rowbuf[pl.ds(b, 1), :span]
        keep = rowbuf[pl.ds(b + batch, 1), :span]
        bias = jnp.where(keep > 0, -slope * (pos[:, span - 1:] - pos).astype(jnp.float32), MASK_FILL)
        scores = dot(q, k, 1, 1) * scale + bias
        row_id = lax.broadcasted_iota(jnp.int32, (q_block, span), 0) + i * q_block
        col_id = lax.broadcasted_iota(jnp.int32, (q_block, span), 1)
        scores = jnp.where(col_id <= row_id, scores, MASK_FILL)
        expo = jnp.exp(scores - jnp.max(scores, axis=-1, keepdims=True))
        prob = expo * (1.0 / jnp.sum(expo, axis=-1, keepdims=True))
        prob_lo = prob.astype(jnp.bfloat16)
        o = dot(prob_lo, v, 1, 0).astype(jnp.bfloat16)
        row_dot = jnp.sum(do.astype(jnp.float32) * o.astype(jnp.float32), axis=-1, keepdims=True)
        ds_lo = (prob * (dot(do, v, 1, 1) - row_dot)).astype(jnp.bfloat16)
        o_all[mine, :] = o
        dq_all[mine, :] = (dot(ds_lo, k, 1, 0) * scale).astype(jnp.bfloat16)
        dv_acc[:span, :] += dot(prob_lo, do, 0, 0)
        dk_acc[:span, :] += dot(ds_lo, q, 0, 0)

    def store_parts(b):
        return pltpu.make_async_copy(pbuf, parts_ref.at[b], parts_sem)

    def finish(b):
        dk = (dk_acc[...] * scale).astype(jnp.bfloat16)
        dv = dv_acc[...].astype(jnp.bfloat16)
        d_all[...] = jnp.concatenate([dq_all[:, :head_dim], dk[:, :head_dim], dv[:, :head_dim]], axis=1)
        whole = jnp.concatenate([d_all[...], o_all[:, :head_dim]], axis=1).reshape(size, tok, 4 * head_dim)
        pbuf[...] = jnp.concatenate([whole[:, :tok // 2], whole[:, tok // 2:]], axis=2)
        store_parts(b).start()

    width = min(512, hidden)

    def gradient(p):
        rows = pl.ds(pl.multiple_of(p * piece_rows, piece_rows), piece_rows)

        def columns(n, carry):
            at = pl.ds(pl.multiple_of(n * width, width), width)
            gwq_ref[:, at] += dot(d_all[rows, :], rows_of(p, 1, at), 0, 0)
            gwo_ref[:, at] += dot(o_all[rows, :head_dim], rows_of(p, 0, at), 0, 0)
            return carry

        lax.fori_loop(0, hidden // width, columns, 0)

    count = seq_len // q_block
    todo = [list(range(min(3, count)))] + [[i] for i in range(3, count)]

    def work_front(b, place):
        place -= READY + 1
        if place == 0:
            load_piece(b, 0).start()
            dk_acc[...] = jnp.zeros_like(dk_acc)
            dv_acc[...] = jnp.zeros_like(dv_acc)
            stream(b, 0, pieces // 2, project)
        elif place == 1:
            stream(b, pieces // 2, pieces, project)
        elif place - 2 < len(todo):
            for i in todo[place - 2]:
                attend(b, i)

    def work_back(b, place):
        if place == 0:
            load_piece(b, 0).start()
            finish(b)
        elif place == 2:
            stream(b, 0, pieces // 2, gradient)
        elif place == 4:
            stream(b, pieces // 2, pieces, gradient)
            store_parts(b).wait()

    gwq_ref[...] = jnp.zeros_like(gwq_ref)
    gwo_ref[...] = jnp.zeros_like(gwo_ref)

    def phase_of(i, place):
        return i - 1 if place == LATE else i

    def among(b):
        return jnp.logical_and(b >= 0, b < batch)

    def turn(i, carry):
        for place in range(places):
            came = (place - LAG) % places
            b_came = phase_of(i if place >= LAG else i - 1, came)

            @pl.when(among(b_came))
            def _():
                for link in range(4):
                    arrival(b_came, link, came).wait_recv()
                    share(b_came, link, came, 0).start()

            b_send = phase_of(i, place)

            @pl.when(among(b_send))
            def _():
                for link in range(4):
                    send(b_send, link, place).start()

            shared = (place - LAG - 1) % places
            b_shared = phase_of(i if place >= LAG + 1 else i - 1, shared)

            @pl.when(among(b_shared))
            def _():
                for link in range(4):
                    share(b_shared, link, shared, flip).wait_recv()

            if place == 1:
                @pl.when(i == 0)
                def _():
                    for b in range(batch):
                        share_own(b, me).start()
                        keep_own(b).start()
                    meta.start()

            if place == READY:
                @pl.when(i == 1)
                def _():
                    for load in (load_wq, load_wo, own_meta):
                        load.wait()
                    meta.wait_recv()
                    for j in range(size):
                        rowbuf[:, j * tok:(j + 1) * tok] = metabuf[j, :, :tok]
                    for b in range(batch):
                        share_own(b, sibling).wait_recv()
                        keep_own(b).wait()

                @pl.when(i == batch)
                def _():
                    for b in range(early):
                        own_parts[b].start()
                        trades[b].start()

            if place > READY:
                @pl.when(among(i - 1))
                def _():
                    work_front(i - 1, place)
            else:
                @pl.when(among(i - 2))
                def _():
                    work_back(i - 2, place)
        return carry

    lax.fori_loop(0, batch + 2, turn, 0)
    for b in range(early):
        own_parts[b].wait()
        trades[b].wait_recv()
        trades[b].wait_send()
    meta.wait_send()

    def sent(n, carry):
        b = n // (4 * places)
        link = lax.rem(n, 4 * places) // places
        place = lax.rem(n, places)
        ref = gat_ref.at[0, 0, 0]
        for sem in (ici_send, d2d_send):
            pltpu.make_async_remote_copy(
                src_ref=ref, dst_ref=ref, send_sem=sem.at[b, link, place], recv_sem=ici_recv.at[b, link, place],
                device_id={"sp": sibling}, device_id_type=MESH).wait_send()
        return carry

    lax.fori_loop(0, batch * 4 * places, sent, 0)
    for b in range(batch):
        share_own(b, me).wait_send()


def block_call(own, wq, bias, wo, meta, slope, size, q_block, collective_id):
    batch, _, _, rows, hidden = own.shape
    tok = COLOURS * rows
    heads, head_dim, _ = wo.shape
    pad_dim = -(-head_dim // LANES) * LANES
    seq_len = size * tok
    side = math.isqrt(size // 2)
    group = size // 4
    places = len(CYCLE)
    anywhere = pl.BlockSpec(memory_space=pl.ANY)
    vmem = pl.BlockSpec(memory_space=pltpu.VMEM)
    sem = pltpu.SemaphoreType.DMA
    bf16, f32 = jnp.bfloat16, jnp.float32
    flops = batch * (6 * seq_len * seq_len * 256 + 4 * seq_len * 4 * head_dim * hidden) + 80_000_000_000
    return pl.pallas_call(
        functools.partial(block_kernel, size, side, (batch, tok, head_dim, pad_dim, hidden, min(q_block, seq_len))),
        out_shape=(
            jax.ShapeDtypeStruct((batch, size, COLOURS, 2, rows, hidden), bf16),
            jax.ShapeDtypeStruct((batch, size, tok // 2, 8 * head_dim), bf16),
            jax.ShapeDtypeStruct((size, batch - 1, tok // 2, 8 * head_dim), bf16),
            jax.ShapeDtypeStruct((3 * head_dim, hidden), f32),
            jax.ShapeDtypeStruct((head_dim, hidden), f32),
        ),
        in_specs=[anywhere, anywhere, vmem, anywhere, anywhere, pl.BlockSpec(memory_space=pltpu.SMEM)],
        out_specs=(anywhere, anywhere, anywhere, vmem, vmem),
        scratch_shapes=[
            pltpu.VMEM((batch, COLOURS, 2, rows, hidden), bf16),
            pltpu.VMEM((3 * head_dim, hidden), bf16),
            pltpu.VMEM((head_dim, hidden), bf16),
            pltpu.VMEM((size, *meta.shape), meta.dtype),
            pltpu.VMEM((meta.shape[0], seq_len), meta.dtype),
            pltpu.VMEM((2, group, COLOURS, 2, rows, hidden), bf16),
            pltpu.VMEM((seq_len, 3 * pad_dim), bf16),
            pltpu.VMEM((seq_len, pad_dim), bf16),
            pltpu.VMEM((seq_len, pad_dim), f32),
            pltpu.VMEM((seq_len, pad_dim), f32),
            pltpu.VMEM((seq_len, pad_dim), bf16),
            pltpu.VMEM((seq_len, pad_dim), bf16),
            pltpu.VMEM((seq_len, 3 * head_dim), bf16),
            pltpu.VMEM((size, tok // 2, 8 * head_dim), bf16),
            sem((4 + batch,)), sem((batch,)), sem((2,)), sem,
            sem((batch, 4, places)), sem((batch, 4, places)), sem((batch, 4, places)), sem((batch, 4, places)),
            sem((batch,)), sem((batch,)), sem((size,)), sem((size,)), sem((batch - 1, size)), sem((batch - 1, size)),
        ],
        compiler_params=pltpu.CompilerParams(collective_id=collective_id, has_side_effects=True, vmem_limit_bytes=VMEM_LIMIT),
        cost_estimate=pl.CostEstimate(flops=flops, bytes_accessed=60_000_000, transcendentals=batch * seq_len * seq_len // 2),
        name="block",
    )(own, wq, bias, wo, meta, slope)


def token_kernel(head_dim, chunk, early_ref, last_ref, wq_ref, wo_ref, x_ref, dy_ref, gain_ref, bout_ref,
                 y_ref, gx_ref, bq_ref, sums_ref, dn_acc, y_acc):
    n = pl.program_id(0)
    parts = []
    for b in range(early_ref.shape[1] + 1):
        pair = early_ref[0, b] if b < early_ref.shape[1] else last_ref[0]
        parts += [pair[:, :4 * head_dim], pair[:, 4 * head_dim:]]
    parts = jnp.concatenate(parts, axis=0)
    dqkv = parts[:, :3 * head_dim]
    o = parts[:, 3 * head_dim:]
    bq_ref[0] = jnp.sum(dqkv.astype(jnp.float32), axis=0, keepdims=True)
    dn_term = dot(dqkv, wq_ref[0], 1, 0)
    y_term = dot(o, wo_ref[0], 1, 0)

    @pl.when(n == 0)
    def _():
        dn_acc[...] = dn_term
        y_acc[...] = y_term

    @pl.when(n > 0)
    def _():
        dn_acc[...] += dn_term
        y_acc[...] += y_term

    @pl.when(n == pl.num_programs(0) - 1)
    def _():
        sums_ref[...] = jnp.zeros_like(sums_ref)
        gain = gain_ref[...]
        bout = bout_ref[...]

        def body(c, carry):
            at = pl.ds(pl.multiple_of(c * chunk, chunk), chunk)
            x = x_ref[at, :].astype(jnp.float32)
            dy = dy_ref[at, :].astype(jnp.float32)
            centered = x - jnp.mean(x, axis=-1, keepdims=True)
            inv_std = lax.rsqrt(jnp.mean(centered * centered, axis=-1, keepdims=True) + NORM_EPS)
            x_hat = centered * inv_std
            d_norm = dn_acc[at, :]
            d_hat = d_norm * gain
            d_mean = jnp.mean(d_hat, axis=-1, keepdims=True)
            d_proj = jnp.mean(d_hat * x_hat, axis=-1, keepdims=True)
            gx_ref[at, :] = (dy + inv_std * (d_hat - d_mean - x_hat * d_proj)).astype(jnp.bfloat16)
            y_ref[at, :] = (x + y_acc[at, :] + bout).astype(jnp.bfloat16)
            sums_ref[0:1, :] += jnp.sum(d_norm * x_hat, axis=0, keepdims=True)
            sums_ref[1:2, :] += jnp.sum(d_norm, axis=0, keepdims=True)
            sums_ref[2:3, :] += jnp.sum(dy, axis=0, keepdims=True)
            return carry

        lax.fori_loop(0, x_ref.shape[0] // chunk, body, 0)


def token_side(early, last, wq, wo, x, dy, gain, bout, head_dim):
    heads = early.shape[0]
    tokens, hidden = x.shape
    whole = lambda n: (0, 0)
    per_head = lambda n: (n, 0, 0)
    return pl.pallas_call(
        functools.partial(token_kernel, head_dim, 16),
        grid=(heads,),
        out_shape=(
            jax.ShapeDtypeStruct((tokens, hidden), jnp.bfloat16),
            jax.ShapeDtypeStruct((tokens, hidden), jnp.bfloat16),
            jax.ShapeDtypeStruct((heads, 1, 3 * head_dim), jnp.float32),
            jax.ShapeDtypeStruct((8, hidden), jnp.float32),
        ),
        in_specs=[
            pl.BlockSpec((1, *early.shape[1:]), lambda n: (n, 0, 0, 0)),
            pl.BlockSpec((1, *last.shape[1:]), per_head),
            pl.BlockSpec((1, 3 * head_dim, hidden), per_head),
            pl.BlockSpec((1, head_dim, hidden), per_head),
            pl.BlockSpec((tokens, hidden), whole),
            pl.BlockSpec((tokens, hidden), whole),
            pl.BlockSpec((1, hidden), whole),
            pl.BlockSpec((1, hidden), whole),
        ],
        out_specs=(
            pl.BlockSpec((tokens, hidden), whole),
            pl.BlockSpec((tokens, hidden), whole),
            pl.BlockSpec((1, 1, 3 * head_dim), per_head),
            pl.BlockSpec((8, hidden), whole),
        ),
        scratch_shapes=[pltpu.VMEM((tokens, hidden), jnp.float32)] * 2,
        compiler_params=pltpu.CompilerParams(vmem_limit_bytes=VMEM_LIMIT),
        cost_estimate=pl.CostEstimate(
            flops=2 * tokens * hidden * 4 * heads * head_dim, bytes_accessed=8 * hidden * heads * head_dim, transcendentals=0),
        name="token_side",
    )(early, last, wq, wo, x, dy, gain, bout)


def settle_kernel(block, depth, ahead, src_ref, *refs):
    dst_ref, buf, read_sems, write_sems = refs[-4:]
    count = src_ref.shape[0] // block

    def at(i):
        return pl.ds(pl.multiple_of(i * block, block), block)

    def read(i):
        return pltpu.make_async_copy(src_ref.at[at(i)], buf.at[lax.rem(i, depth)], read_sems.at[lax.rem(i, depth)])

    def write(i):
        return pltpu.make_async_copy(buf.at[lax.rem(i, depth)], dst_ref.at[at(i)], write_sems.at[lax.rem(i, depth)])

    def step(i, carry):
        @pl.when(jnp.logical_and(i >= depth, i < count))
        def _():
            write(i - depth).wait()

        @pl.when(i < count)
        def _():
            read(i).start()

        @pl.when(i >= ahead)
        def _():
            read(i - ahead).wait()
            write(i - ahead).start()

        return carry

    lax.fori_loop(0, count + ahead, step, 0)

    def drain(i, carry):
        write(i).wait()
        return carry

    lax.fori_loop(max(0, count - depth), count, drain, 0)


def settle(x, block, after=()):
    depth, ahead = 12, 6
    rows, cols = x.shape
    sem = pltpu.SemaphoreType.DMA((depth,))
    return pl.pallas_call(
        functools.partial(settle_kernel, block, depth, ahead),
        out_shape=jax.ShapeDtypeStruct(x.shape, x.dtype),
        in_specs=[pl.BlockSpec(memory_space=pl.ANY)] * (1 + len(after)),
        out_specs=pl.BlockSpec(memory_space=pl.ANY),
        scratch_shapes=[pltpu.VMEM((depth, block, cols), x.dtype), sem, sem],
        cost_estimate=pl.CostEstimate(flops=10_000_000_000, bytes_accessed=8 * rows * cols, transcendentals=0),
        name="settle",
    )(x, *after)


def solution(mesh):
    size = mesh.shape["sp"]

    def block_fn(x_blk, pos_blk, keep_blk, ln_gain, ln_bias, w_qkv, b_qkv, w_out, b_out, dy_blk):
        batch, tok, hidden = x_blk.shape
        heads, head_dim = w_qkv.shape[1], w_qkv.shape[3]
        tokens = batch * tok
        rank = lax.axis_index("sp")
        wq = jnp.transpose(w_qkv, (1, 2, 3, 0)).reshape(heads, 3 * head_dim, hidden)
        wo = w_out.reshape(heads, head_dim, hidden)
        dy_flat = dy_blk.reshape(tokens, hidden)

        def gather(a):
            return lax.all_gather(a, "sp", axis=0, tiled=True)

        x_norm = norm_forward(x_blk, ln_gain, ln_bias)
        own = jnp.stack([dy_blk, x_norm], axis=0).reshape(2, batch, COLOURS, tok // COLOURS, hidden).transpose(1, 2, 0, 3, 4)
        meta = jnp.pad(jnp.concatenate([pos_blk, keep_blk], axis=0), ((0, 8 - 2 * batch), (0, LANES - tok)))
        bias = lax.dynamic_slice_in_dim(b_qkv, rank, 1, 0).reshape(1, 3 * head_dim)
        slope = jnp.exp2(-8.0 * (rank + 1).astype(jnp.float32) / heads).reshape(1)
        _, parts, early, grad_head, grad_out = block_call(own, wq, bias, wo, meta, slope, size, 256, 0)

        grad_wq = settle(gather(grad_head), head_dim)
        grad_wo = settle(gather(grad_out), head_dim, after=(grad_wq,))

        last = exchange(parts[batch - 1], size, 1)
        y, grad_x, bq_part, sums = token_side(
            early, last, wq, wo, x_blk.reshape(tokens, hidden), dy_flat, ln_gain.reshape(1, hidden), b_out.reshape(1, hidden), head_dim)
        bq, gain, bias_sum, bo = lax.psum((bq_part.reshape(-1), sums[0], sums[1], sums[2]), "sp")
        grad_wq = jnp.transpose(grad_wq.reshape(heads, 3, head_dim, hidden), (3, 0, 1, 2))
        return (y.reshape(x_blk.shape), grad_x.reshape(x_blk.shape), grad_wq, bq.reshape(heads, 3, head_dim), grad_wo,
                bo, gain, bias_sum)

    act_spec = P("dp", "sp", None)
    tok_spec = P("dp", "sp")
    in_specs = (act_spec, tok_spec, tok_spec, P(), P(), P(), P(), P(), P(), act_spec)
    out_specs = (act_spec, act_spec, P("dp", None, None, None), P("dp", None, None), P("dp", None), P("dp"), P("dp"), P("dp"))
    return jax.shard_map(block_fn, mesh=mesh, in_specs=in_specs, out_specs=out_specs, check_vma=False)
```

time: 689 us -> 597 us (0.87); the launches traced: 681 us -> 596 us
  matrix products: 66.1 us -> 0 us
  Pallas kernels: 346 us -> 380 us
  local copies, waits for them, and re-layouts: 39.2 us -> 7.52 us
  waiting for transfers between devices: 161 us -> 141 us
    dot_general x4 -> x0, matrix products: 66.1 us -> none  [the longest x3 56.7 us: dot(): lax.dot_general(a, b, (((ca,), (cb,)), ((), ())), preferred_element_type=...]
    pallas_call x8 -> x4, Pallas kernels: 297 us -> 331 us  [the longest x1 229 us: block_call(): pl.pallas_call(functools.partial(block_kernel, size, side, (batch, tok, h...]
    reshape x4 -> x1, local copies, waits for them, and re-layouts: 25 us -> 0.65 us  [block_fn(): bias = lax.dynamic_slice_in_dim(b_qkv, rank, 1, 0).reshape(1, 3 * head_dim)]
    all_gather x6 -> x2, waiting for transfers between devices: 159 us -> 140 us  [gather(): return lax.all_gather(a, 'sp', axis=0, tiled=True)]
  transfers between devices with their start and end apart: 6 -> 2, of which waited for: 4 -> 2; matrix products, arithmetic and copies ran while one was open for 16% -> 1% of each run, Pallas kernels for 28% -> 17%
where the time goes in v3:
time: 597 us; the launch traced here: 596 us
  Pallas kernels  380 us (64%)
  waiting for transfers between devices  141 us (24%)
  blocking collectives  47.1 us (8%)
  between operations  14.3 us (2%)
  local copies, waits for them, and re-layouts  7.52 us (1%)
    pallas_call x1, Pallas kernels, block_call(): pl.pallas_call(functools.partial(block_kernel, size, side, (batch, tok, h...  229 us
    all_gather x2, waiting for transfers between devices, gather(): return lax.all_gather(a, 'sp', axis=0, tiled=True)  140 us
    pallas_call x2, Pallas kernels, settle(): pl.pallas_call(functools.partial(settle_kernel, block, depth, ahead), out...  68.6 us
    pallas_call x1, Pallas kernels, token_side(): pl.pallas_call(functools.partial(token_kernel, head_dim, 16), grid=(heads...  48.8 us
    psum x1, blocking collectives, block_fn(): lax.psum((bq_part.reshape(-1), sums[0], sums[1], sums[2]), 'sp')  47.1 us
    pallas_call x1, Pallas kernels, exchange(): pl.pallas_call(functools.partial(exchange_kernel, size), out_shape=jax.Sh...  33.5 us
  transfers between devices with their start and end apart: 2, of which 2 were waited for; matrix products, arithmetic and copies ran while one was open for 1% of the time, Pallas kernels for 17%

profile of v3, /device:TPU:97, one launch (start us, length us, event | category | flops | bytes accessed | tf_op | source)
XLA Modules:
  0.0 596.0 jit_solution(8777917543129953945)
XLA Ops:
  7.3 0.7 copy-done
  8.0 0.6 reshape.75.bias_ref
  8.7 1.5 convert_reduce_fusion
  10.2 1.6 fusion.2
  11.9 0.6 pad.4.meta_ref
  12.5 0.5 fusion.5
  13.0 1.4 maximum_bitcast_fusion.own_ref
  14.4 229.0 %block.1 = (bf16[3,32,4,2,16,2560]{5,4,3,2,1,0:T(8,128)(2,1)}, bf16[3,32,32,640]{3,2,1,0:T(8,128)(2,1)}, bf16[32,2,32,640]{3,2,1,0:T(8,128)(2,1)}, f32[240,2560]{1,0:T(8,128)}, f32[80,2560]{1,0:T(8,128)}) custom-call(bf16[3,4,2,16,2560]{4,3,2,1,0:T(8,128)(2,1)} %maximum_bitcast_fusion.own_ref, bf16[32,240,2560]{2,1,0:T(8,128)(2,1)} %bitcast.18, ...), custom_call_target="tpu_custom_call" | custom-call | flops 119460012032 | bytes 60000000 | tf_op jit(solution)/shard_map/block/pallas_call | solution.py:393
  243.5 0.1 all-gather.5.cloned.1.call-start
  243.6 0.7 all-gather.5.cloned.1.call-update
  244.3 0.6 reshape.80.gain_ref
  244.9 0.6 reshape.81.bout_ref
  245.5 2.5 slice_bitcast_fusion.in_ref
  248.0 33.5 %all_to_all.1.last_ref = bf16[32,32,640]{2,1,0:T(8,128)(2,1)} custom-call(bf16[32,32,640]{2,1,0:T(8,128)(2,1)} %slice_bitcast_fusion.in_ref), custom_call_target="tpu_custom_call" | custom-call | flops 40000000000 | bytes 2621440 | tf_op jit(solution)/shard_map/all_to_all/pallas_call | solution.py:84
  281.6 48.8 %token_side.1 = (bf16[192,2560]{1,0:T(8,128)(2,1)}, bf16[192,2560]{1,0:T(8,128)(2,1)}, f32[32,1,240]{2,1,0:T(1,128)}, f32[8,2560]{1,0:T(8,128)}) custom-call(bf16[32,2,32,640]{3,2,1,0:T(8,128)(2,1)} %get-tuple-element.16.early_ref, bf16[32,32,640]{2,1,0:T(8,128)(2,1)} %all_to_all.1.last_ref, bf16[32,240,2560]{2,1,0:T(8,128)(2,1)} %bitcast.19, ...), custom_call_target="tpu_custom_call" | custom-call | flops 10066329600 | bytes 52428800 | tf_op jit(solution)/shard_map/token_side/pallas_call | solution.py:485
  330.4 0.8 reduce.1
  331.2 0.1 reshape.86
  331.3 1.1 slice_reduce_fusion
  332.5 47.1 %all-reduce.1 = (f32[32,3,80]{2,1,0:T(4,128)S(1)}, f32[2560]{0:T(1024)}, f32[2560]{0:T(1024)}, f32[2560]{0:T(1024)}) all-reduce(f32[32,3,80]{2,1,0:T(4,128)S(1)} %reshape.86, f32[2560]{0:T(1024)S(1)} %get-tuple-element.34, f32[2560]{0:T(1024)S(1)} %get-tuple-element.33, ...), channel_id=1, replica_groups=mesh['dp'=1,'sp'=32] {'sp'}, use_global_device_ids=true, to_apply=%region_2.3 | all-reduce | flops 15360 | bytes 122880 | tf_op jit(solution)/shard_map/psum | solution.py:599
  379.6 0.6 copy.19
  380.2 100.7 %all-gather.3.cloned.1.call-done.src_ref = f32[7680,2560]{1,0:T(8,128)} async-done(((f32[240,2560]{1,0:T(8,128)}), f32[7680,2560]{1,0:T(8,128)}) %all-gather.3.cloned.1.call-update) | async-done | bytes 78643216 | tf_op jit(solution)/shard_map/all_gather | solution.py:584
  480.9 50.8 %settle.2.refs_0_ = f32[7680,2560]{1,0:T(8,128)} custom-call(f32[7680,2560]{1,0:T(8,128)} %all-gather.3.cloned.1.call-done.src_ref), custom_call_target="tpu_custom_call" | custom-call | flops 10000000000 | bytes 157286400 | tf_op jit(solution)/shard_map/settle/pallas_call | solution.py:560
  531.7 39.5 %all-gather.5.cloned.1.call-done.src_ref = f32[2560,2560]{1,0:T(8,128)} async-done(((f32[80,2560]{1,0:T(8,128)}), f32[2560,2560]{1,0:T(8,128)}) %all-gather.5.cloned.1.call-update) | async-done | bytes 26214416 | tf_op jit(solution)/shard_map/all_gather | solution.py:584
  571.2 17.8 %settle.3 = f32[2560,2560]{1,0:T(8,128)} custom-call(f32[2560,2560]{1,0:T(8,128)} %all-gather.5.cloned.1.call-done.src_ref, f32[7680,2560]{1,0:T(8,128)} %settle.2.refs_0_), custom_call_target="tpu_custom_call" | custom-call | flops 10000000000 | bytes 52428800 | tf_op jit(solution)/shard_map/settle/pallas_call | solution.py:560
  (23 shorter events, 0.2 us)
Async XLA Ops:
  7.2 0.8 copy-start
  7.2 5.3 copy-start.2
  7.2 4.6 copy-start.8
  7.2 4.6 copy-start.7
  7.2 5.2 copy-start.4
  7.2 5.2 copy-start.5
  7.3 473.6 %all-gather.3.cloned.1.call-start = ((), (), s32[]{:S(2)}) async-start(), calls=%async_computation | async-start | bytes 81100800 | tf_op jit(solution)/shard_map/all_gather | solution.py:584
  8.7 4.3 copy-start.3
  243.4 1.5 copy-start.6
  243.5 327.7 %all-gather.5.cloned.1.call-start = ((), (), s32[]{:S(2)}) async-start(), calls=%async_computation.1 | async-start | bytes 27033600 | tf_op jit(solution)/shard_map/all_gather | solution.py:584
  571.2 17.9 %copy-start.1 = (f32[32,3,80]{2,0,1:T(8,128)S(1)}, f32[32,3,80]{2,0,1:T(8,128)}, u32[]{:S(2)}) copy-start(f32[32,3,80]{2,0,1:T(8,128)} %param.16) | copy-start | bytes 92164
Sparse Core Ops, SparseCore 0:
  243.6 237.1 all-gather.2
  483.0 88.2 all-gather.4

commit v4 on v3

--- a/solution.py
+++ b/solution.py
@@ -65,32 +65,6 @@
 
     def wait_send(self):
         self.loop(lambda d: self.copy(d, lax.rem(self.me + d, self.size), self.me).wait_send())
-
-
-def exchange_kernel(size, in_ref, out_ref, send_sems, recv_sems, local_sem):
-    me = lax.axis_index("sp")
-    greet_all(me, size)
-    own = pltpu.make_async_copy(in_ref.at[me], out_ref.at[me], local_sem)
-    own.start()
-    direct = Direct(me, size, lambda j: in_ref.at[j], lambda j: out_ref.at[j], send_sems, recv_sems)
-    direct.start()
-    own.wait()
-    direct.wait_recv()
-    direct.wait_send()
-
-
-def exchange(x, size, collective_id):
-    nbytes = x.size * x.dtype.itemsize
-    return pl.pallas_call(
-        functools.partial(exchange_kernel, size),
-        out_shape=jax.ShapeDtypeStruct(x.shape, x.dtype),
-        in_specs=[pl.BlockSpec(memory_space=pl.ANY)],
-        out_specs=pl.BlockSpec(memory_space=pl.ANY),
-        scratch_shapes=[pltpu.SemaphoreType.DMA((size,)), pltpu.SemaphoreType.DMA((size,)), pltpu.SemaphoreType.DMA],
-        compiler_params=pltpu.CompilerParams(collective_id=collective_id, has_side_effects=True),
-        cost_estimate=pl.CostEstimate(flops=40_000_000_000, bytes_accessed=2 * nbytes, transcendentals=0),
-        name="all_to_all",
-    )(x)
 
 
 FIRST_OF = (2, 3, 0, 1)
@@ -100,30 +74,29 @@
 LAG = 3
 COLOURS = 4
 READY = 6
+TAIL_ROWS = 32
 STEP_OF = ((1, 0), (-1, 0), (0, 1), (0, -1))
-
-
-def block_kernel(size, side, dims, own_ref, wq_ref, bias_ref, wo_ref, meta_ref, slope_ref,
-                 gat_ref, parts_ref, partstok_ref, gwq_ref, gwo_ref,
-                 stage, wbuf, wobuf, metabuf, rowbuf, sbuf, qkvb, dob, dk_acc, dv_acc, dq_all, o_all, d_all, pbuf,
-                 load_sems, own_sems, piece_sems, parts_sem, ici_send, ici_recv, d2d_send, d2d_recv, own_send, own_recv,
-                 meta_send, meta_recv, part_send, part_recv):
-    batch, tok, head_dim, pad_dim, hidden, q_block = dims
-    seq_len = size * tok
-    me = lax.axis_index("sp")
-    core = lax.rem(me, 2)
-    chip = me // 2
-    cx, cy = lax.rem(chip, side), chip // side
-    flip = 1 - 2 * core
-    sibling = me + flip
-    places = len(CYCLE)
-    scale = head_dim ** -0.5
-    slope = slope_ref[0]
-
-    def device_at(dx, dy):
-        return (lax.rem(cy + dy + side, side) * side + lax.rem(cx + dx + side, side)) * 2 + core
-
-    def chunk(link, place, ahead):
+PLACES = len(CYCLE)
+
+
+class Torus:
+    def __init__(self, size):
+        self.side = math.isqrt(size // 2)
+        self.me = lax.axis_index("sp")
+        self.core = lax.rem(self.me, 2)
+        chip = self.me // 2
+        self.cx, self.cy = lax.rem(chip, self.side), chip // self.side
+        self.flip = 1 - 2 * self.core
+        self.sibling = self.me + self.flip
+
+    def device_at(self, dx, dy):
+        side = self.side
+        return (lax.rem(self.cy + dy + side, side) * side + lax.rem(self.cx + dx + side, side)) * 2 + self.core
+
+    def neighbour(self, link):
+        return self.device_at(*STEP_OF[link])
+
+    def chunk(self, link, place, ahead):
         what = CYCLE[place]
         if what[0] == "P":
             first, n, m = link, what[1] + ahead, 0
@@ -131,25 +104,43 @@
             first, n, m = FIRST_OF[link], what[2] + ahead, what[1]
         dx = -STEP_OF[link][0] * n - STEP_OF[first][0] * m
         dy = -STEP_OF[link][1] * n - STEP_OF[first][1] * m
-        return device_at(dx, dy), first
+        return self.device_at(dx, dy), first
+
+
+def is_own(place):
+    return CYCLE[place] in (("P", 0), ("Q", 0, 0))
+
+
+def block_kernel(size, dims, own_ref, wq_ref, bias_ref, wo_ref, meta_ref, slope_ref,
+                 gat_ref, parts_ref, partstok_ref, gwq_ref, gwtail_ref, gwo_ref,
+                 stage, wbuf, wobuf, metabuf, rowbuf, sbuf, qkvb, dob, dk_acc, dv_acc, dq_all, o_all, d_all, pbuf,
+                 load_sems, own_sems, piece_sems, parts_sem, ici_send, ici_recv, d2d_send, d2d_recv, own_send, own_recv,
+                 meta_send, meta_recv, part_send, part_recv):
+    batch, tok, head_dim, pad_dim, hidden, q_block = dims
+    seq_len = size * tok
+    torus = Torus(size)
+    me, flip, sibling = torus.me, torus.flip, torus.sibling
+    places = PLACES
+    scale = head_dim ** -0.5
+    slope = slope_ref[0]
 
     def send(b, link, place):
-        block, colour = chunk(link, place, 0)
+        block, colour = torus.chunk(link, place, 0)
         dst = gat_ref.at[b, block, colour]
         return pltpu.make_async_remote_copy(
-            src_ref=stage.at[b, colour] if CYCLE[place] in (("P", 0), ("Q", 0, 0)) else dst, dst_ref=dst,
+            src_ref=stage.at[b, colour] if is_own(place) else dst, dst_ref=dst,
             send_sem=ici_send.at[b, link, place], recv_sem=ici_recv.at[b, link, place],
-            device_id={"sp": device_at(*STEP_OF[link])}, device_id_type=MESH)
+            device_id={"sp": torus.neighbour(link)}, device_id_type=MESH)
 
     def arrival(b, link, place):
-        block, colour = chunk(link, place, 1)
+        block, colour = torus.chunk(link, place, 1)
         ref = gat_ref.at[b, block, colour]
         return pltpu.make_async_remote_copy(
             src_ref=ref, dst_ref=ref, send_sem=ici_send.at[b, link, place], recv_sem=ici_recv.at[b, link, place],
             device_id={"sp": me}, device_id_type=MESH)
 
     def share(b, link, place, shift):
-        block, colour = chunk(link, place, 1)
+        block, colour = torus.chunk(link, place, 1)
         ref = gat_ref.at[b, block + shift, colour]
         return pltpu.make_async_remote_copy(
             src_ref=ref, dst_ref=ref, send_sem=d2d_send.at[b, link, place], recv_sem=d2d_recv.at[b, link, place],
@@ -177,23 +168,17 @@
     greet_all(me, size)
     load_own.wait()
 
-    group = sbuf.shape[1]
-    pieces = size // group
+    pieces, group = sbuf.shape[0], sbuf.shape[1]
     piece_rows = group * tok
 
     def load_piece(b, p):
-        return pltpu.make_async_copy(gat_ref.at[b, pl.ds(p * group, group)], sbuf.at[lax.rem(p, 2)], piece_sems.at[lax.rem(p, 2)])
+        return pltpu.make_async_copy(gat_ref.at[b, pl.ds(p * group, group)], sbuf.at[p], piece_sems.at[p])
 
     def rows_of(p, which, at=slice(None)):
-        return sbuf[lax.rem(p, 2), :, :, which, :, at].reshape(piece_rows, -1)
-
-    def stream(b, lo, hi, use):
+        return sbuf[p, :, :, which, :, at].reshape(piece_rows, -1)
+
+    def each(lo, hi, use):
         def body(p, carry):
-            @pl.when(p + 1 < pieces)
-            def _():
-                load_piece(b, p + 1).start()
-
-            load_piece(b, p).wait()
             use(p)
             return carry
 
@@ -202,7 +187,8 @@
     def pad_lanes(a):
         return jnp.concatenate([a, jnp.zeros((a.shape[0], pad_dim - head_dim), a.dtype)], axis=1)
 
-    def project(p):
+    def project(b, p):
+        load_piece(b, p).wait()
         at = pl.ds(pl.multiple_of(p * piece_rows, piece_rows), piece_rows)
         r = (dot(rows_of(p, 1), wbuf[...], 1, 1) + bias_ref[...]).astype(jnp.bfloat16)
         for c in range(3):
@@ -212,6 +198,9 @@
     def attend(b, i):
         span = (i + 1) * q_block
         mine = slice(i * q_block, span)
+        if i == 0:
+            dk_acc[...] = jnp.zeros_like(dk_acc)
+            dv_acc[...] = jnp.zeros_like(dv_acc)
         q, k, v = qkvb[mine, :pad_dim], qkvb[:span, pad_dim:2 * pad_dim], qkvb[:span, 2 * pad_dim:]
         do = dob[mine, :]
         pos = rowbuf[pl.ds(b, 1), :span]
@@ -250,40 +239,28 @@
 
         def columns(n, carry):
             at = pl.ds(pl.multiple_of(n * width, width), width)
-            gwq_ref[:, at] += dot(d_all[rows, :], rows_of(p, 1, at), 0, 0)
+            term = dot(d_all[rows, :], rows_of(p, 1, at), 0, 0)
+            gwq_ref[:, at] += term[:gwq_ref.shape[0]]
+            gwtail_ref[:, at] += term[gwq_ref.shape[0]:]
             gwo_ref[:, at] += dot(o_all[rows, :head_dim], rows_of(p, 0, at), 0, 0)
             return carry
 
         lax.fori_loop(0, hidden // width, columns, 0)
 
     count = seq_len // q_block
-    todo = [list(range(min(3, count)))] + [[i] for i in range(3, count)]
-
-    def work_front(b, place):
-        place -= READY + 1
-        if place == 0:
-            load_piece(b, 0).start()
-            dk_acc[...] = jnp.zeros_like(dk_acc)
-            dv_acc[...] = jnp.zeros_like(dv_acc)
-            stream(b, 0, pieces // 2, project)
-        elif place == 1:
-            stream(b, pieces // 2, pieces, project)
-        elif place - 2 < len(todo):
-            for i in todo[place - 2]:
-                attend(b, i)
-
-    def work_back(b, place):
-        if place == 0:
-            load_piece(b, 0).start()
-            finish(b)
-        elif place == 2:
-            stream(b, 0, pieces // 2, gradient)
-        elif place == 4:
-            stream(b, pieces // 2, pieces, gradient)
-            store_parts(b).wait()
-
-    gwq_ref[...] = jnp.zeros_like(gwq_ref)
-    gwo_ref[...] = jnp.zeros_like(gwo_ref)
+    half = pieces // 2
+    tasks = {(0, READY): [lambda b: each(0, pieces, lambda p: load_piece(b, p).start())],
+             (0, READY + 2): [lambda b: each(0, half, lambda p: project(b, p))],
+             (0, READY + 3): [lambda b: each(half, pieces, lambda p: project(b, p))],
+             (1, 1): [finish],
+             (1, 3): [lambda b: each(0, half, gradient)],
+             (1, 5): [lambda b: each(half, pieces, gradient), lambda b: store_parts(b).wait()]}
+    spots = [(0, place) for place in range(READY + 4, places)] + [(1, 0)]
+    for i in range(count):
+        tasks.setdefault(spots[min(max(0, i - 2), len(spots) - 1)], []).append(lambda b, i=i: attend(b, i))
+
+    for ref in (gwq_ref, gwtail_ref, gwo_ref):
+        ref[...] = jnp.zeros_like(ref)
 
     def phase_of(i, place):
         return i - 1 if place == LATE else i
@@ -343,14 +320,12 @@
                         own_parts[b].start()
                         trades[b].start()
 
-            if place > READY:
-                @pl.when(among(i - 1))
-                def _():
-                    work_front(i - 1, place)
-            else:
-                @pl.when(among(i - 2))
-                def _():
-                    work_back(i - 2, place)
+            for later in (0, 1):
+                if (later, place) in tasks:
+                    @pl.when(among(i - 1 - later))
+                    def _():
+                        for task in tasks[later, place]:
+                            task(i - 1 - later)
         return carry
 
     lax.fori_loop(0, batch + 2, turn, 0)
@@ -382,32 +357,32 @@
     heads, head_dim, _ = wo.shape
     pad_dim = -(-head_dim // LANES) * LANES
     seq_len = size * tok
-    side = math.isqrt(size // 2)
-    group = size // 4
-    places = len(CYCLE)
+    pieces = 4
+    places = PLACES
     anywhere = pl.BlockSpec(memory_space=pl.ANY)
     vmem = pl.BlockSpec(memory_space=pltpu.VMEM)
     sem = pltpu.SemaphoreType.DMA
     bf16, f32 = jnp.bfloat16, jnp.float32
     flops = batch * (6 * seq_len * seq_len * 256 + 4 * seq_len * 4 * head_dim * hidden) + 80_000_000_000
     return pl.pallas_call(
-        functools.partial(block_kernel, size, side, (batch, tok, head_dim, pad_dim, hidden, min(q_block, seq_len))),
+        functools.partial(block_kernel, size, (batch, tok, head_dim, pad_dim, hidden, min(q_block, seq_len))),
         out_shape=(
             jax.ShapeDtypeStruct((batch, size, COLOURS, 2, rows, hidden), bf16),
             jax.ShapeDtypeStruct((batch, size, tok // 2, 8 * head_dim), bf16),
             jax.ShapeDtypeStruct((size, batch - 1, tok // 2, 8 * head_dim), bf16),
-            jax.ShapeDtypeStruct((3 * head_dim, hidden), f32),
+            jax.ShapeDtypeStruct((3 * head_dim - TAIL_ROWS, hidden), f32),
+            jax.ShapeDtypeStruct((TAIL_ROWS, hidden), f32),
             jax.ShapeDtypeStruct((head_dim, hidden), f32),
         ),
         in_specs=[anywhere, anywhere, vmem, anywhere, anywhere, pl.BlockSpec(memory_space=pltpu.SMEM)],
-        out_specs=(anywhere, anywhere, anywhere, vmem, vmem),
+        out_specs=(anywhere, anywhere, anywhere, vmem, vmem, vmem),
         scratch_shapes=[
             pltpu.VMEM((batch, COLOURS, 2, rows, hidden), bf16),
             pltpu.VMEM((3 * head_dim, hidden), bf16),
             pltpu.VMEM((head_dim, hidden), bf16),
             pltpu.VMEM((size, *meta.shape), meta.dtype),
             pltpu.VMEM((meta.shape[0], seq_len), meta.dtype),
-            pltpu.VMEM((2, group, COLOURS, 2, rows, hidden), bf16),
+            pltpu.VMEM((pieces, size // pieces, COLOURS, 2, rows, hidden), bf16),
             pltpu.VMEM((seq_len, 3 * pad_dim), bf16),
             pltpu.VMEM((seq_len, pad_dim), bf16),
             pltpu.VMEM((seq_len, pad_dim), f32),
@@ -416,7 +391,7 @@
             pltpu.VMEM((seq_len, pad_dim), bf16),
             pltpu.VMEM((seq_len, 3 * head_dim), bf16),
             pltpu.VMEM((size, tok // 2, 8 * head_dim), bf16),
-            sem((4 + batch,)), sem((batch,)), sem((2,)), sem,
+            sem((4 + batch,)), sem((batch,)), sem((pieces,)), sem,
             sem((batch, 4, places)), sem((batch, 4, places)), sem((batch, 4, places)), sem((batch, 4, places)),
             sem((batch,)), sem((batch,)), sem((size,)), sem((size,)), sem((batch - 1, size)), sem((batch - 1, size)),
         ],
@@ -424,6 +399,102 @@
         cost_estimate=pl.CostEstimate(flops=flops, bytes_accessed=60_000_000, transcendentals=batch * seq_len * seq_len // 2),
         name="block",
     )(own, wq, bias, wo, meta, slope)
+
+
+def spread_kernel(size, own_ref, parts_ref, gat_ref, last_ref, stage, load_sem, keep_sem, part_sem,
+                  ici_send, ici_recv, d2d_send, d2d_recv, own_send, own_recv, part_send, part_recv):
+    torus = Torus(size)
+    me, sibling = torus.me, torus.sibling
+    b = parts_ref.shape[0] - 1
+    part = own_ref.shape[1] // COLOURS
+
+    def view(block, colour):
+        return gat_ref.at[block, :, pl.ds(colour * part, part)]
+
+    def send(link, place):
+        block, colour = torus.chunk(link, place, 0)
+        dst = view(block, colour)
+        return pltpu.make_async_remote_copy(
+            src_ref=stage.at[:, pl.ds(colour * part, part)] if is_own(place) else dst, dst_ref=dst,
+            send_sem=ici_send.at[link, place], recv_sem=ici_recv.at[link, place],
+            device_id={"sp": torus.neighbour(link)}, device_id_type=MESH)
+
+    def arrival(link, place):
+        ref = view(*torus.chunk(link, place, 1))
+        return pltpu.make_async_remote_copy(
+            src_ref=ref, dst_ref=ref, send_sem=ici_send.at[link, place], recv_sem=ici_recv.at[link, place],
+            device_id={"sp": me}, device_id_type=MESH)
+
+    def share(link, place, shift):
+        block, colour = torus.chunk(link, place, 1)
+        ref = view(block + shift, colour)
+        return pltpu.make_async_remote_copy(
+            src_ref=ref, dst_ref=ref, send_sem=d2d_send.at[link, place], recv_sem=d2d_recv.at[link, place],
+            device_id={"sp": sibling}, device_id_type=MESH)
+
+    def share_own(block):
+        return pltpu.make_async_remote_copy(
+            src_ref=stage, dst_ref=gat_ref.at[block], send_sem=own_send, recv_sem=own_recv,
+            device_id={"sp": sibling}, device_id_type=MESH)
+
+    load = pltpu.make_async_copy(own_ref, stage, load_sem)
+    load.start()
+    keep = pltpu.make_async_copy(stage, gat_ref.at[me], keep_sem)
+    trade = Direct(me, size, lambda j: parts_ref.at[b, j], lambda j: last_ref.at[j], part_send, part_recv)
+    own_part = pltpu.make_async_copy(parts_ref.at[b, me], last_ref.at[me], part_sem)
+    greet_all(me, size)
+    load.wait()
+
+    def place_of(g):
+        place = g % PLACES
+        return place if g >= 0 and g // PLACES == (1 if place == LATE else 0) else None
+
+    for g in range(PLACES + LATE + LAG + 2):
+        came, now, shared = place_of(g - LAG), place_of(g), place_of(g - LAG - 1)
+        for link in range(4):
+            if came is not None:
+                arrival(link, came).wait_recv()
+                share(link, came, 0).start()
+        for link in range(4):
+            if now is not None:
+                send(link, now).start()
+        for link in range(4):
+            if shared is not None:
+                share(link, shared, torus.flip).wait_recv()
+        if g == 1:
+            trade.start()
+            own_part.start()
+            share_own(me).start()
+            keep.start()
+    share_own(sibling).wait_recv()
+    own_part.wait()
+    keep.wait()
+    trade.wait_recv()
+    trade.wait_send()
+    share_own(me).wait_send()
+    for place in range(PLACES):
+        for link in range(4):
+            send(link, place).wait_send()
+            share(link, place, 0).wait_send()
+
+
+def spread(block, parts, size, collective_id):
+    rows, cols = block.shape
+    anywhere = pl.BlockSpec(memory_space=pl.ANY)
+    sem = pltpu.SemaphoreType.DMA
+    return pl.pallas_call(
+        functools.partial(spread_kernel, size),
+        out_shape=(jax.ShapeDtypeStruct((size, rows, cols), block.dtype), jax.ShapeDtypeStruct(parts.shape[1:], parts.dtype)),
+        in_specs=[anywhere, anywhere],
+        out_specs=(anywhere, anywhere),
+        scratch_shapes=[
+            pltpu.VMEM((rows, cols), block.dtype), sem, sem, sem,
+            sem((4, PLACES)), sem((4, PLACES)), sem((4, PLACES)), sem((4, PLACES)), sem, sem, sem((size,)), sem((size,)),
+        ],
+        compiler_params=pltpu.CompilerParams(collective_id=collective_id, has_side_effects=True),
+        cost_estimate=pl.CostEstimate(flops=100_000_000_000, bytes_accessed=8 * size * rows * cols, transcendentals=0),
+        name="spread",
+    )(block, parts)
 
 
 def token_kernel(head_dim, chunk, early_ref, last_ref, wq_ref, wo_ref, x_ref, dy_ref, gain_ref, bout_ref,
@@ -515,18 +586,19 @@
     )(early, last, wq, wo, x, dy, gain, bout)
 
 
-def settle_kernel(block, depth, ahead, src_ref, *refs):
+def settle_kernel(block, depth, ahead, first, src_ref, *refs):
     dst_ref, buf, read_sems, write_sems = refs[-4:]
-    count = src_ref.shape[0] // block
-
-    def at(i):
-        return pl.ds(pl.multiple_of(i * block, block), block)
+    per = src_ref.shape[1] // block
+    count = src_ref.shape[0] * per
+
+    def slab(ref, i, start):
+        return ref.at[i // per, pl.ds(pl.multiple_of(start + lax.rem(i, per) * block, 8), block)]
 
     def read(i):
-        return pltpu.make_async_copy(src_ref.at[at(i)], buf.at[lax.rem(i, depth)], read_sems.at[lax.rem(i, depth)])
+        return pltpu.make_async_copy(slab(src_ref, i, 0), buf.at[lax.rem(i, depth)], read_sems.at[lax.rem(i, depth)])
 
     def write(i):
-        return pltpu.make_async_copy(buf.at[lax.rem(i, depth)], dst_ref.at[at(i)], write_sems.at[lax.rem(i, depth)])
+        return pltpu.make_async_copy(buf.at[lax.rem(i, depth)], slab(dst_ref, i, first), write_sems.at[lax.rem(i, depth)])
 
     def step(i, carry):
         @pl.when(jnp.logical_and(i >= depth, i < count))
@@ -553,19 +625,22 @@
     lax.fori_loop(max(0, count - depth), count, drain, 0)
 
 
-def settle(x, block, after=()):
+def settle(x, first, total, block, into=None):
     depth, ahead = 12, 6
-    rows, cols = x.shape
+    count, _, cols = x.shape
     sem = pltpu.SemaphoreType.DMA((depth,))
+    old = [] if into is None else [into]
     return pl.pallas_call(
-        functools.partial(settle_kernel, block, depth, ahead),
-        out_shape=jax.ShapeDtypeStruct(x.shape, x.dtype),
-        in_specs=[pl.BlockSpec(memory_space=pl.ANY)] * (1 + len(after)),
+        functools.partial(settle_kernel, block, depth, ahead, first),
+        out_shape=jax.ShapeDtypeStruct((count, total, cols), x.dtype),
+        in_specs=[pl.BlockSpec(memory_space=pl.ANY)] * (1 + len(old)),
         out_specs=pl.BlockSpec(memory_space=pl.ANY),
         scratch_shapes=[pltpu.VMEM((depth, block, cols), x.dtype), sem, sem],
-        cost_estimate=pl.CostEstimate(flops=10_000_000_000, bytes_accessed=8 * rows * cols, transcendentals=0),
+        input_output_aliases={1: 0} if old else {},
+        compiler_params=pltpu.CompilerParams(vmem_limit_bytes=VMEM_LIMIT),
+        cost_estimate=pl.CostEstimate(flops=10_000_000_000, bytes_accessed=8 * x.size, transcendentals=0),
         name="settle",
-    )(x, *after)
+    )(x, *old)
 
 
 def solution(mesh):
@@ -588,17 +663,20 @@
         meta = jnp.pad(jnp.concatenate([pos_blk, keep_blk], axis=0), ((0, 8 - 2 * batch), (0, LANES - tok)))
         bias = lax.dynamic_slice_in_dim(b_qkv, rank, 1, 0).reshape(1, 3 * head_dim)
         slope = jnp.exp2(-8.0 * (rank + 1).astype(jnp.float32) / heads).reshape(1)
-        _, parts, early, grad_head, grad_out = block_call(own, wq, bias, wo, meta, slope, size, 256, 0)
-
-        grad_wq = settle(gather(grad_head), head_dim)
-        grad_wo = settle(gather(grad_out), head_dim, after=(grad_wq,))
-
-        last = exchange(parts[batch - 1], size, 1)
+        _, parts, early, grad_head, grad_tail, grad_out = block_call(own, wq, bias, wo, meta, slope, size, 256, 0)
+
+        rows, split = 3 * head_dim, 3 * head_dim - TAIL_ROWS
+        grad_wq = settle(gather(grad_head).reshape(heads, split, hidden), 0, rows, split // 2)
+        grad_wq = settle(gather(grad_tail).reshape(heads, TAIL_ROWS, hidden), split, rows, TAIL_ROWS, grad_wq)
+        out_all, last = spread(grad_out, parts, size, 1)
+        grad_wo = settle(out_all, 0, head_dim, head_dim)
+
         y, grad_x, bq_part, sums = token_side(
             early, last, wq, wo, x_blk.reshape(tokens, hidden), dy_flat, ln_gain.reshape(1, hidden), b_out.reshape(1, hidden), head_dim)
         bq, gain, bias_sum, bo = lax.psum((bq_part.reshape(-1), sums[0], sums[1], sums[2]), "sp")
         grad_wq = jnp.transpose(grad_wq.reshape(heads, 3, head_dim, hidden), (3, 0, 1, 2))
-        return (y.reshape(x_blk.shape), grad_x.reshape(x_blk.shape), grad_wq, bq.reshape(heads, 3, head_dim), grad_wo,
+        return (y.reshape(x_blk.shape), grad_x.reshape(x_blk.shape), grad_wq, bq.reshape(heads, 3, head_dim),
+                grad_wo.reshape(heads * head_dim, hidden),
                 bo, gain, bias_sum)
 
     act_spec = P("dp", "sp", None)

time: 597 us -> 578 us (0.968)
  waiting for transfers between devices: 141 us -> 5.02 us
  Pallas kernels: 380 us -> 499 us
    all_gather x2, waiting for transfers between devices: 140 us -> 4.23 us  [gather(): return lax.all_gather(a, 'sp', axis=0, tiled=True)]
    pallas_call x4 -> x5, Pallas kernels: 331 us -> 450 us  [the longest x1 229 us: block_call(): pl.pallas_call(functools.partial(block_kernel, size, (batch, tok, head_di...]
  transfers between devices with their start and end apart: 2 -> 2, of which waited for: 2 -> 1; matrix products, arithmetic and copies ran while one was open for 1% -> 1% of each run, Pallas kernels for 17% -> 45%
where the time goes in v4:
time: 578 us; the launch traced here: 576 us
  Pallas kernels  499 us (86%)
  blocking collectives  47.2 us (8%)
  between operations  14.3 us (2%)
  other arithmetic  5.89 us (1%)
    pallas_call x1, Pallas kernels, block_call(): pl.pallas_call(functools.partial(block_kernel, size, (batch, tok, head_di...  229 us
    pallas_call x1, Pallas kernels, spread(): pl.pallas_call(functools.partial(spread_kernel, size), out_shape=(jax.Sha...  151 us
    pallas_call x3, Pallas kernels, settle(): pl.pallas_call(functools.partial(settle_kernel, block, depth, ahead, firs...  70.1 us
    pallas_call x1, Pallas kernels, token_side(): pl.pallas_call(functools.partial(token_kernel, head_dim, 16), grid=(heads...  48.8 us
    psum x1, blocking collectives, block_fn(): lax.psum((bq_part.reshape(-1), sums[0], sums[1], sums[2]), 'sp')  47.2 us
  transfers between devices with their start and end apart: 2, of which 1 were waited for; matrix products, arithmetic and copies ran while one was open for 1% of the time, Pallas kernels for 45%

profile of v4, /device:TPU:97, one launch (start us, length us, event | category | flops | bytes accessed | tf_op | source)
XLA Modules:
  0.0 576.3 jit_solution(14709550364510928135)
XLA Ops:
  7.3 0.1 all-gather.5.cloned.1.call-start
  7.4 0.6 copy-done
  8.0 0.6 reshape.84.bias_ref
  8.7 1.5 convert_reduce_fusion
  10.2 1.6 fusion.2
  11.8 0.6 pad.4.meta_ref
  12.4 0.5 fusion.5
  12.9 1.4 maximum_bitcast_fusion.own_ref
  14.4 229.2 %block.1 = (bf16[3,32,4,2,16,2560]{5,4,3,2,1,0:T(8,128)(2,1)}, bf16[3,32,32,640]{3,2,1,0:T(8,128)(2,1)}, bf16[32,2,32,640]{3,2,1,0:T(8,128)(2,1)}, f32[208,2560]...) custom-call(bf16[3,4,2,16,2560]{4,3,2,1,0:T(8,128)(2,1)} %maximum_bitcast_fusion.own_ref, ...), custom_call_target="tpu_custom_call" | custom-call | flops 119460012032 | bytes 60000000 | tf_op jit(solution)/shard_map/block/pallas_call | solution.py:367
  243.7 0.1 all-gather.3.cloned.1.call-start
  243.7 0.7 all-gather.3.cloned.1.call-update
  244.5 0.6 reshape.89.gain_ref
  245.1 0.6 reshape.90.bout_ref
  245.7 150.6 %spread.1 = (f32[32,80,2560]{2,1,0:T(8,128)}, bf16[32,32,640]{2,1,0:T(8,128)(2,1)}) custom-call(f32[80,2560]{1,0:T(8,128)} %get-tuple-element.20.own_ref, bf16[3,32,32,640]{3,2,1,0:T(8,128)(2,1)} %get-tuple-element.21.parts_ref), custom_call_target="tpu_custom_call" | custom-call | flops 99999997952 | bytes 52428800 | tf_op jit(solution)/shard_map/spread/pallas_call | solution.py:485
  396.3 48.8 %token_side.1 = (bf16[192,2560]{1,0:T(8,128)(2,1)}, bf16[192,2560]{1,0:T(8,128)(2,1)}, f32[32,1,240]{2,1,0:T(1,128)}, f32[8,2560]{1,0:T(8,128)}) custom-call(bf16[32,2,32,640]{3,2,1,0:T(8,128)(2,1)} %get-tuple-element.19.early_ref, bf16[32,32,640]{2,1,0:T(8,128)(2,1)} %get-tuple-element.22.last_ref, bf16[32,240,2560]{2,1,0:T(8,128)(2,1)} %bitcast.20, ...), custom_call_target="tpu_custom_call" | custom-call | flops 10066329600 | bytes 52428800 | tf_op jit(solution)/shard_map/token_side/pallas_call | solution.py:556
  445.1 0.8 reduce.1
  446.0 0.1 reshape.97
  446.1 1.1 slice_reduce_fusion
  447.2 47.2 %all-reduce.1 = (f32[32,3,80]{2,1,0:T(4,128)S(1)}, f32[2560]{0:T(1024)}, f32[2560]{0:T(1024)}, f32[2560]{0:T(1024)}) all-reduce(f32[32,3,80]{2,1,0:T(4,128)S(1)} %reshape.97, f32[2560]{0:T(1024)S(1)} %get-tuple-element.40, f32[2560]{0:T(1024)S(1)} %get-tuple-element.39, ...), channel_id=1, replica_groups=mesh['dp'=1,'sp'=32] {'sp'}, use_global_device_ids=true, to_apply=%region_2.3 | all-reduce | flops 15360 | bytes 122880 | tf_op jit(solution)/shard_map/psum | solution.py:676
  494.4 0.6 copy.20
  495.0 17.9 %settle.5 = f32[32,80,2560]{2,1,0:T(8,128)} custom-call(f32[32,80,2560]{2,1,0:T(8,128)} %get-tuple-element.28.src_ref), custom_call_target="tpu_custom_call" | custom-call | flops 10000000000 | bytes 52428800 | tf_op jit(solution)/shard_map/settle/pallas_call | solution.py:633
  512.9 43.8 %settle.3.refs_0_ = f32[32,240,2560]{2,1,0:T(8,128)} custom-call(f32[32,208,2560]{2,1,0:T(8,128)} %bitcast.12.src_ref), custom_call_target="tpu_custom_call" | custom-call | flops 10000000000 | bytes 136314880 | tf_op jit(solution)/shard_map/settle/pallas_call | solution.py:633
  556.8 4.2 all-gather.3.cloned.1.call-done
  561.0 8.4 %settle.4 = f32[32,240,2560]{2,1,0:T(8,128)} custom-call(f32[32,32,2560]{2,1,0:T(8,128)} %bitcast.25, f32[32,240,2560]{2,1,0:T(8,128)} %settle.3.refs_0_), custom_call_target="tpu_custom_call", output_to_operand_aliasing={{}: (1, {})} | custom-call | flops 10000000000 | bytes 20971520 | tf_op jit(solution)/shard_map/settle/pallas_call | solution.py:633
  (23 shorter events, 0.2 us)
Async XLA Ops:
  7.2 0.8 copy-start
  7.2 5.2 copy-start.2
  7.2 4.6 copy-start.7
  7.2 4.6 copy-start.8
  7.2 5.2 copy-start.4
  7.2 5.2 copy-start.5
  7.3 505.7 %all-gather.5.cloned.1.call-start = ((), (), s32[]{:S(2)}) async-start(), calls=%async_computation.1 | async-start | bytes 70287360 | tf_op jit(solution)/shard_map/all_gather | solution.py:659
  8.7 4.2 copy-start.3
  243.6 1.5 copy-start.6
  243.7 317.3 %all-gather.3.cloned.1.call-start = ((), (), s32[]{:S(2)}) async-start(), calls=%async_computation | async-start | bytes 10813440 | tf_op jit(solution)/shard_map/all_gather | solution.py:659
  561.0 8.5 %copy-start.1 = (f32[32,3,80]{2,0,1:T(8,128)S(1)}, f32[32,3,80]{2,0,1:T(8,128)}, u32[]{:S(2)}) copy-start(f32[32,3,80]{2,0,1:T(8,128)} %param.16) | copy-start | bytes 92164
Sparse Core Ops, SparseCore 0:
  243.8 264.8 all-gather.4
  510.7 50.1 all-gather.2

commit v5 on v4

--- a/solution.py
+++ b/solution.py
@@ -19,14 +19,7 @@
     return lax.dot_general(a, b, (((ca,), (cb,)), ((), ())), preferred_element_type=jnp.float32)
 
 
-def norm_forward(x_blk, ln_gain, ln_bias):
-    x_f32 = x_blk.astype(jnp.float32)
-    centered = x_f32 - jnp.mean(x_f32, axis=-1, keepdims=True)
-    inv_std = lax.rsqrt(jnp.mean(centered * centered, axis=-1, keepdims=True) + NORM_EPS)
-    return (centered * inv_std * ln_gain + ln_bias).astype(jnp.bfloat16)
-
-
-def greet_all(me, size):
+def greet_all(me, size, meanwhile=lambda: None):
     barrier = pltpu.get_barrier_semaphore()
 
     def greet(d, carry):
@@ -34,6 +27,7 @@
         return carry
 
     lax.fori_loop(1, size, greet, 0)
+    meanwhile()
     pl.semaphore_wait(barrier, size - 1)
 
 
@@ -74,7 +68,6 @@
 LAG = 3
 COLOURS = 4
 READY = 6
-TAIL_ROWS = 32
 STEP_OF = ((1, 0), (-1, 0), (0, 1), (0, -1))
 PLACES = len(CYCLE)
 
@@ -111,18 +104,19 @@
     return CYCLE[place] in (("P", 0), ("Q", 0, 0))
 
 
-def block_kernel(size, dims, own_ref, wq_ref, bias_ref, wo_ref, meta_ref, slope_ref,
-                 gat_ref, parts_ref, partstok_ref, gwq_ref, gwtail_ref, gwo_ref,
-                 stage, wbuf, wobuf, metabuf, rowbuf, sbuf, qkvb, dob, dk_acc, dv_acc, dq_all, o_all, d_all, pbuf,
+def block_kernel(size, dims, x_ref, dy_ref, gain_ref, shift_ref, pos_ref, keep_ref, wq_ref, bias_ref, wo_ref,
+                 gat_ref, parts_ref, partstok_ref, gwa_ref, gwb_ref, gwc_ref, gwo_ref,
+                 xin, stage, wbuf, wobuf, metatile, metabuf, rowbuf, sbuf, qkvb, dob, dk_acc, dv_acc, dq_all, o_all, d_all, pbuf,
                  load_sems, own_sems, piece_sems, parts_sem, ici_send, ici_recv, d2d_send, d2d_recv, own_send, own_recv,
                  meta_send, meta_recv, part_send, part_recv):
     batch, tok, head_dim, pad_dim, hidden, q_block = dims
     seq_len = size * tok
     torus = Torus(size)
-    me, flip, sibling = torus.me, torus.flip, torus.sibling
+    me, flip, sibling, side = torus.me, torus.flip, torus.sibling, torus.side
     places = PLACES
     scale = head_dim ** -0.5
-    slope = slope_ref[0]
+    heads = wo_ref.shape[0]
+    slope = jnp.exp2(jnp.full((1, 1), -8.0 / heads, jnp.float32) * (me + 1).astype(jnp.float32))
 
     def send(b, link, place):
         block, colour = torus.chunk(link, place, 0)
@@ -154,28 +148,56 @@
     def keep_own(b):
         return pltpu.make_async_copy(stage.at[b], gat_ref.at[b, me], own_sems.at[b])
 
-    load_own = pltpu.make_async_copy(own_ref, stage, load_sems.at[0])
-    load_wq = pltpu.make_async_copy(wq_ref.at[me], wbuf, load_sems.at[1])
-    load_wo = pltpu.make_async_copy(wo_ref.at[me], wobuf, load_sems.at[2])
-    own_meta = pltpu.make_async_copy(meta_ref, metabuf.at[me], load_sems.at[3])
-    for load in (load_own, load_wq, load_wo, own_meta):
+    load_x = pltpu.make_async_copy(x_ref, xin, load_sems.at[0])
+    load_dy = pltpu.make_async_copy(dy_ref, stage.at[:, :, 0], load_sems.at[1])
+    load_wq = pltpu.make_async_copy(wq_ref.at[me], wbuf, load_sems.at[2])
+    load_wo = pltpu.make_async_copy(wo_ref.at[me], wobuf, load_sems.at[3])
+    for load in (load_x, load_dy, load_wq, load_wo):
         load.start()
-    meta = Direct(me, size, lambda j: meta_ref, lambda j: metabuf.at[j], meta_send, meta_recv)
+    meta = Direct(me, size, lambda j: metatile, lambda j: metabuf.at[j], meta_send, meta_recv)
     early = batch - 1
     trades = [Direct(me, size, lambda j, b=b: parts_ref.at[b, j], lambda j, b=b: partstok_ref.at[j, b], part_send.at[b], part_recv.at[b])
               for b in range(early)]
     own_parts = [pltpu.make_async_copy(parts_ref.at[b, me], partstok_ref.at[me, b], load_sems.at[4 + b]) for b in range(early)]
-    greet_all(me, size)
-    load_own.wait()
-
-    pieces, group = sbuf.shape[0], sbuf.shape[1]
-    piece_rows = group * tok
+
+    def prepare():
+        metatile[...] = jnp.zeros_like(metatile)
+        metatile[0:batch, 0:tok] = pos_ref[...]
+        metatile[batch:2 * batch, 0:tok] = keep_ref[...]
+        metabuf[me] = metatile[...]
+        load_x.wait()
+
+        def normalise(n, carry):
+            b, c = n // COLOURS, lax.rem(n, COLOURS)
+            x = xin[b, c].astype(jnp.float32)
+            centered = x - jnp.mean(x, axis=-1, keepdims=True)
+            inv_std = lax.rsqrt(jnp.mean(centered * centered, axis=-1, keepdims=True) + NORM_EPS)
+            stage[b, c, 1] = (centered * inv_std * gain_ref[...] + shift_ref[...]).astype(jnp.bfloat16)
+            return carry
+
+        lax.fori_loop(0, batch * COLOURS, normalise, 0)
+        load_dy.wait()
+
+    greet_all(me, size, prepare)
+
+    pieces = sbuf.shape[0]
+    chip_rows = 2 * tok
+
+    def chip_of(p, e):
+        return torus.device_at(lax.rem(p + 1 + e, side), e) // 2
+
+    def rows_at(p, e):
+        return pl.ds(pl.multiple_of(chip_of(p, e) * chip_rows, chip_rows), chip_rows)
 
     def load_piece(b, p):
-        return pltpu.make_async_copy(gat_ref.at[b, pl.ds(p * group, group)], sbuf.at[p], piece_sems.at[p])
+        return [pltpu.make_async_copy(gat_ref.at[b, pl.ds(chip_of(p, e) * 2, 2)], sbuf.at[p, e], piece_sems.at[p, e]) for e in range(side)]
+
+    def start_piece(b, p):
+        for load in load_piece(b, p):
+            load.start()
 
     def rows_of(p, which, at=slice(None)):
-        return sbuf[p, :, :, which, :, at].reshape(piece_rows, -1)
+        return sbuf[p, :, :, :, which, :, at].reshape(side * chip_rows, -1)
 
     def each(lo, hi, use):
         def body(p, carry):
@@ -188,12 +210,18 @@
         return jnp.concatenate([a, jnp.zeros((a.shape[0], pad_dim - head_dim), a.dtype)], axis=1)
 
     def project(b, p):
-        load_piece(b, p).wait()
-        at = pl.ds(pl.multiple_of(p * piece_rows, piece_rows), piece_rows)
-        r = (dot(rows_of(p, 1), wbuf[...], 1, 1) + bias_ref[...]).astype(jnp.bfloat16)
-        for c in range(3):
-            qkvb[at, c * pad_dim:(c + 1) * pad_dim] = pad_lanes(r[:, c * head_dim:(c + 1) * head_dim])
-        dob[at, :] = pad_lanes(dot(rows_of(p, 0), wobuf[...], 1, 1).astype(jnp.bfloat16))
+        for load in load_piece(b, p):
+            load.wait()
+        bias = jnp.concatenate([bias_ref[c, pl.ds(me, 1), :] for c in range(3)], axis=1)
+        r = (dot(rows_of(p, 1), wbuf[...], 1, 1) + bias).astype(jnp.bfloat16)
+        d = pad_lanes(dot(rows_of(p, 0), wobuf[...], 1, 1).astype(jnp.bfloat16))
+        q, k, v = (pad_lanes(r[:, c * head_dim:(c + 1) * head_dim]) for c in range(3))
+        for e in range(side):
+            mine = slice(e * chip_rows, (e + 1) * chip_rows)
+            at = rows_at(p, e)
+            for c, part in enumerate((q, k, v)):
+                qkvb[at, c * pad_dim:(c + 1) * pad_dim] = part[mine]
+            dob[at, :] = d[mine]
 
     def attend(b, i):
         span = (i + 1) * q_block
@@ -235,31 +263,37 @@
     width = min(512, hidden)
 
     def gradient(p):
-        rows = pl.ds(pl.multiple_of(p * piece_rows, piece_rows), piece_rows)
+        d = jnp.concatenate([d_all[rows_at(p, e), :] for e in range(side)], axis=0)
+        o = jnp.concatenate([o_all[rows_at(p, e), :] for e in range(side)], axis=0)[:, :head_dim]
 
         def columns(n, carry):
             at = pl.ds(pl.multiple_of(n * width, width), width)
-            term = dot(d_all[rows, :], rows_of(p, 1, at), 0, 0)
-            gwq_ref[:, at] += term[:gwq_ref.shape[0]]
-            gwtail_ref[:, at] += term[gwq_ref.shape[0]:]
-            gwo_ref[:, at] += dot(o_all[rows, :head_dim], rows_of(p, 0, at), 0, 0)
+            term = dot(d, rows_of(p, 1, at), 0, 0)
+            row = 0
+            for ref in (gwa_ref, gwb_ref, gwc_ref):
+                ref[:, at] += term[row:row + ref.shape[0]]
+                row += ref.shape[0]
+            gwo_ref[:, at] += dot(o, rows_of(p, 0, at), 0, 0)
             return carry
 
         lax.fori_loop(0, hidden // width, columns, 0)
 
     count = seq_len // q_block
-    half = pieces // 2
-    tasks = {(0, READY): [lambda b: each(0, pieces, lambda p: load_piece(b, p).start())],
-             (0, READY + 2): [lambda b: each(0, half, lambda p: project(b, p))],
-             (0, READY + 3): [lambda b: each(half, pieces, lambda p: project(b, p))],
-             (1, 1): [finish],
-             (1, 3): [lambda b: each(0, half, gradient)],
-             (1, 5): [lambda b: each(half, pieces, gradient), lambda b: store_parts(b).wait()]}
-    spots = [(0, place) for place in range(READY + 4, places)] + [(1, 0)]
+    last = pieces - 1
+    tasks = {(0, READY - 3): [lambda b: each(0, last, lambda p: start_piece(b, p))],
+             (0, READY - 2): [lambda b: each(0, last - 1, lambda p: project(b, p))],
+             (0, READY - 1): [lambda b: project(b, last - 1)],
+             (0, READY): [lambda b: start_piece(b, last)],
+             (0, READY + 1): [lambda b: project(b, last)],
+             (0, READY + 7): [finish],
+             (0, READY + 8): [lambda b: each(0, pieces // 2, gradient)],
+             (1, 0): [lambda b: each(pieces // 2, pieces, gradient)],
+             (1, 1): [lambda b: store_parts(b).wait()]}
+    spot = (2, 2, 2, 3, 3, 4, 5, 6)
     for i in range(count):
-        tasks.setdefault(spots[min(max(0, i - 2), len(spots) - 1)], []).append(lambda b, i=i: attend(b, i))
-
-    for ref in (gwq_ref, gwtail_ref, gwo_ref):
+        tasks.setdefault((0, READY + spot[i]), []).append(lambda b, i=i: attend(b, i))
+
+    for ref in (gwa_ref, gwb_ref, gwc_ref, gwo_ref):
         ref[...] = jnp.zeros_like(ref)
 
     def phase_of(i, place):
@@ -293,6 +327,9 @@
             def _():
                 for link in range(4):
                     share(b_shared, link, shared, flip).wait_recv()
+                for link in range(4):
+                    share(b_shared, link, shared, 0).wait_send()
+                    send(b_shared, link, shared).wait_send()
 
             if place == 1:
                 @pl.when(i == 0)
@@ -302,10 +339,10 @@
                         keep_own(b).start()
                     meta.start()
 
-            if place == READY:
+            if place == READY - 3:
                 @pl.when(i == 1)
                 def _():
-                    for load in (load_wq, load_wo, own_meta):
+                    for load in (load_wq, load_wo):
                         load.wait()
                     meta.wait_recv()
                     for j in range(size):
@@ -313,7 +350,11 @@
                     for b in range(batch):
                         share_own(b, sibling).wait_recv()
                         keep_own(b).wait()
-
+                    meta.wait_send()
+                    for b in range(batch):
+                        share_own(b, me).wait_send()
+
+            if place == READY:
                 @pl.when(i == batch)
                 def _():
                     for b in range(early):
@@ -333,56 +374,47 @@
         own_parts[b].wait()
         trades[b].wait_recv()
         trades[b].wait_send()
-    meta.wait_send()
-
-    def sent(n, carry):
-        b = n // (4 * places)
-        link = lax.rem(n, 4 * places) // places
-        place = lax.rem(n, places)
-        ref = gat_ref.at[0, 0, 0]
-        for sem in (ici_send, d2d_send):
-            pltpu.make_async_remote_copy(
-                src_ref=ref, dst_ref=ref, send_sem=sem.at[b, link, place], recv_sem=ici_recv.at[b, link, place],
-                device_id={"sp": sibling}, device_id_type=MESH).wait_send()
-        return carry
-
-    lax.fori_loop(0, batch * 4 * places, sent, 0)
-    for b in range(batch):
-        share_own(b, me).wait_send()
-
-
-def block_call(own, wq, bias, wo, meta, slope, size, q_block, collective_id):
-    batch, _, _, rows, hidden = own.shape
-    tok = COLOURS * rows
+
+
+def split_rows(rows):
+    first = 8 * (rows * 3 // 80)
+    return first, rows - first - 8, 8
+
+
+def block_call(x, dy, gain, shift, pos, keep, wq, bias, wo, size, q_block, collective_id):
+    batch, tok, hidden = x.shape
+    rows = tok // COLOURS
     heads, head_dim, _ = wo.shape
     pad_dim = -(-head_dim // LANES) * LANES
     seq_len = size * tok
-    pieces = 4
+    side = math.isqrt(size // 2)
     places = PLACES
     anywhere = pl.BlockSpec(memory_space=pl.ANY)
     vmem = pl.BlockSpec(memory_space=pltpu.VMEM)
     sem = pltpu.SemaphoreType.DMA
     bf16, f32 = jnp.bfloat16, jnp.float32
     flops = batch * (6 * seq_len * seq_len * 256 + 4 * seq_len * 4 * head_dim * hidden) + 80_000_000_000
+    cut = (batch, COLOURS, rows, hidden)
     return pl.pallas_call(
         functools.partial(block_kernel, size, (batch, tok, head_dim, pad_dim, hidden, min(q_block, seq_len))),
         out_shape=(
             jax.ShapeDtypeStruct((batch, size, COLOURS, 2, rows, hidden), bf16),
             jax.ShapeDtypeStruct((batch, size, tok // 2, 8 * head_dim), bf16),
             jax.ShapeDtypeStruct((size, batch - 1, tok // 2, 8 * head_dim), bf16),
-            jax.ShapeDtypeStruct((3 * head_dim - TAIL_ROWS, hidden), f32),
-            jax.ShapeDtypeStruct((TAIL_ROWS, hidden), f32),
+            *(jax.ShapeDtypeStruct((n, hidden), f32) for n in split_rows(3 * head_dim)),
             jax.ShapeDtypeStruct((head_dim, hidden), f32),
         ),
-        in_specs=[anywhere, anywhere, vmem, anywhere, anywhere, pl.BlockSpec(memory_space=pltpu.SMEM)],
-        out_specs=(anywhere, anywhere, anywhere, vmem, vmem, vmem),
+        in_specs=[anywhere, anywhere, vmem, vmem, vmem, vmem, anywhere, vmem, anywhere],
+        out_specs=(anywhere, anywhere, anywhere, vmem, vmem, vmem, vmem),
         scratch_shapes=[
+            pltpu.VMEM(cut, bf16),
             pltpu.VMEM((batch, COLOURS, 2, rows, hidden), bf16),
             pltpu.VMEM((3 * head_dim, hidden), bf16),
             pltpu.VMEM((head_dim, hidden), bf16),
-            pltpu.VMEM((size, *meta.shape), meta.dtype),
-            pltpu.VMEM((meta.shape[0], seq_len), meta.dtype),
-            pltpu.VMEM((pieces, size // pieces, COLOURS, 2, rows, hidden), bf16),
+            pltpu.VMEM((8, LANES), jnp.int32),
+            pltpu.VMEM((size, 8, LANES), jnp.int32),
+            pltpu.VMEM((8, seq_len), jnp.int32),
+            pltpu.VMEM((side, side, 2, COLOURS, 2, rows, hidden), bf16),
             pltpu.VMEM((seq_len, 3 * pad_dim), bf16),
             pltpu.VMEM((seq_len, pad_dim), bf16),
             pltpu.VMEM((seq_len, pad_dim), f32),
@@ -391,14 +423,14 @@
             pltpu.VMEM((seq_len, pad_dim), bf16),
             pltpu.VMEM((seq_len, 3 * head_dim), bf16),
             pltpu.VMEM((size, tok // 2, 8 * head_dim), bf16),
-            sem((4 + batch,)), sem((batch,)), sem((pieces,)), sem,
+            sem((4 + batch,)), sem((batch,)), sem((side, side)), sem,
             sem((batch, 4, places)), sem((batch, 4, places)), sem((batch, 4, places)), sem((batch, 4, places)),
             sem((batch,)), sem((batch,)), sem((size,)), sem((size,)), sem((batch - 1, size)), sem((batch - 1, size)),
         ],
         compiler_params=pltpu.CompilerParams(collective_id=collective_id, has_side_effects=True, vmem_limit_bytes=VMEM_LIMIT),
         cost_estimate=pl.CostEstimate(flops=flops, bytes_accessed=60_000_000, transcendentals=batch * seq_len * seq_len // 2),
         name="block",
-    )(own, wq, bias, wo, meta, slope)
+    )(x.reshape(cut), dy.reshape(cut), gain, shift, pos, keep, wq, bias, wo)
 
 
 def spread_kernel(size, own_ref, parts_ref, gat_ref, last_ref, stage, load_sem, keep_sem, part_sem,
@@ -498,18 +530,27 @@
 
 
 def token_kernel(head_dim, chunk, early_ref, last_ref, wq_ref, wo_ref, x_ref, dy_ref, gain_ref, bout_ref,
-                 y_ref, gx_ref, bq_ref, sums_ref, dn_acc, y_acc):
+                 y_ref, gx_ref, tiles_ref, dn_acc, y_acc, sums):
     n = pl.program_id(0)
-    parts = []
-    for b in range(early_ref.shape[1] + 1):
-        pair = early_ref[0, b] if b < early_ref.shape[1] else last_ref[0]
-        parts += [pair[:, :4 * head_dim], pair[:, 4 * head_dim:]]
-    parts = jnp.concatenate(parts, axis=0)
-    dqkv = parts[:, :3 * head_dim]
-    o = parts[:, 3 * head_dim:]
-    bq_ref[0] = jnp.sum(dqkv.astype(jnp.float32), axis=0, keepdims=True)
-    dn_term = dot(dqkv, wq_ref[0], 1, 0)
-    y_term = dot(o, wo_ref[0], 1, 0)
+    step = wq_ref.shape[0]
+
+    @pl.when(n == 0)
+    def _():
+        tiles_ref[...] = jnp.zeros_like(tiles_ref)
+
+    dn_term = y_term = 0.0
+    for h in range(step):
+        parts = []
+        for b in range(early_ref.shape[1] + 1):
+            pair = early_ref[h, b] if b < early_ref.shape[1] else last_ref[h]
+            parts += [pair[:, :4 * head_dim], pair[:, 4 * head_dim:]]
+        parts = jnp.concatenate(parts, axis=0)
+        dqkv = parts[:, :3 * head_dim]
+        total = jnp.sum(dqkv.astype(jnp.float32), axis=0, keepdims=True)
+        for c in range(3):
+            tiles_ref[n * step + h, 3 + c:4 + c, 0:head_dim] = total[:, c * head_dim:(c + 1) * head_dim]
+        dn_term += dot(dqkv, wq_ref[h], 1, 0)
+        y_term += dot(parts[:, 3 * head_dim:], wo_ref[h], 1, 0)
 
     @pl.when(n == 0)
     def _():
@@ -523,7 +564,7 @@
 
     @pl.when(n == pl.num_programs(0) - 1)
     def _():
-        sums_ref[...] = jnp.zeros_like(sums_ref)
+        sums[...] = jnp.zeros_like(sums)
         gain = gain_ref[...]
         bout = bout_ref[...]
 
@@ -540,33 +581,35 @@
             d_proj = jnp.mean(d_hat * x_hat, axis=-1, keepdims=True)
             gx_ref[at, :] = (dy + inv_std * (d_hat - d_mean - x_hat * d_proj)).astype(jnp.bfloat16)
             y_ref[at, :] = (x + y_acc[at, :] + bout).astype(jnp.bfloat16)
-            sums_ref[0:1, :] += jnp.sum(d_norm * x_hat, axis=0, keepdims=True)
-            sums_ref[1:2, :] += jnp.sum(d_norm, axis=0, keepdims=True)
-            sums_ref[2:3, :] += jnp.sum(dy, axis=0, keepdims=True)
+            sums[0:1, :] += jnp.sum(d_norm * x_hat, axis=0, keepdims=True)
+            sums[1:2, :] += jnp.sum(d_norm, axis=0, keepdims=True)
+            sums[2:3, :] += jnp.sum(dy, axis=0, keepdims=True)
             return carry
 
         lax.fori_loop(0, x_ref.shape[0] // chunk, body, 0)
+        for j in range(tiles_ref.shape[0]):
+            tiles_ref[j, 0:3, 0:head_dim] = sums[0:3, j * head_dim:(j + 1) * head_dim]
 
 
 def token_side(early, last, wq, wo, x, dy, gain, bout, head_dim):
     heads = early.shape[0]
     tokens, hidden = x.shape
+    step = 4
     whole = lambda n: (0, 0)
     per_head = lambda n: (n, 0, 0)
     return pl.pallas_call(
         functools.partial(token_kernel, head_dim, 16),
-        grid=(heads,),
+        grid=(heads // step,),
         out_shape=(
             jax.ShapeDtypeStruct((tokens, hidden), jnp.bfloat16),
             jax.ShapeDtypeStruct((tokens, hidden), jnp.bfloat16),
-            jax.ShapeDtypeStruct((heads, 1, 3 * head_dim), jnp.float32),
-            jax.ShapeDtypeStruct((8, hidden), jnp.float32),
+            jax.ShapeDtypeStruct((heads, 8, LANES), jnp.float32),
         ),
         in_specs=[
-            pl.BlockSpec((1, *early.shape[1:]), lambda n: (n, 0, 0, 0)),
-            pl.BlockSpec((1, *last.shape[1:]), per_head),
-            pl.BlockSpec((1, 3 * head_dim, hidden), per_head),
-            pl.BlockSpec((1, head_dim, hidden), per_head),
+            pl.BlockSpec((step, *early.shape[1:]), lambda n: (n, 0, 0, 0)),
+            pl.BlockSpec((step, *last.shape[1:]), per_head),
+            pl.BlockSpec((step, 3 * head_dim, hidden), per_head),
+            pl.BlockSpec((step, head_dim, hidden), per_head),
             pl.BlockSpec((tokens, hidden), whole),
             pl.BlockSpec((tokens, hidden), whole),
             pl.BlockSpec((1, hidden), whole),
@@ -575,15 +618,47 @@
         out_specs=(
             pl.BlockSpec((tokens, hidden), whole),
             pl.BlockSpec((tokens, hidden), whole),
-            pl.BlockSpec((1, 1, 3 * head_dim), per_head),
-            pl.BlockSpec((8, hidden), whole),
+            pl.BlockSpec((heads, 8, LANES), lambda n: (0, 0, 0)),
         ),
-        scratch_shapes=[pltpu.VMEM((tokens, hidden), jnp.float32)] * 2,
+        scratch_shapes=[pltpu.VMEM((tokens, hidden), jnp.float32)] * 2 + [pltpu.VMEM((8, hidden), jnp.float32)],
         compiler_params=pltpu.CompilerParams(vmem_limit_bytes=VMEM_LIMIT),
         cost_estimate=pl.CostEstimate(
             flops=2 * tokens * hidden * 4 * heads * head_dim, bytes_accessed=8 * hidden * heads * head_dim, transcendentals=0),
         name="token_side",
     )(early, last, wq, wo, x, dy, gain, bout)
+
+
+def sums_kernel(size, tiles_ref, all_ref, come, total, own_sem, send_a, recv_a, send_b, recv_b):
+    me = lax.axis_index("sp")
+    greet_all(me, size)
+    own = pltpu.make_async_copy(tiles_ref.at[me], come.at[me], own_sem)
+    own.start()
+    spread_out = Direct(me, size, lambda j: tiles_ref.at[j], lambda j: come.at[j], send_a, recv_a)
+    spread_out.start()
+    own.wait()
+    spread_out.wait_recv()
+    total[...] = jnp.sum(come[...], axis=0)
+    all_ref[me] = total[...]
+    collect = Direct(me, size, lambda j: total, lambda j: all_ref.at[j], send_b, recv_b)
+    collect.start()
+    spread_out.wait_send()
+    collect.wait_recv()
+    collect.wait_send()
+
+
+def sum_tiles(tiles, size, collective_id):
+    sem = pltpu.SemaphoreType.DMA
+    return pl.pallas_call(
+        functools.partial(sums_kernel, size),
+        out_shape=jax.ShapeDtypeStruct(tiles.shape, tiles.dtype),
+        in_specs=[pl.BlockSpec(memory_space=pl.ANY)],
+        out_specs=pl.BlockSpec(memory_space=pltpu.VMEM),
+        scratch_shapes=[pltpu.VMEM(tiles.shape, tiles.dtype), pltpu.VMEM(tiles.shape[1:], tiles.dtype),
+                        sem, sem((size,)), sem((size,)), sem((size,)), sem((size,))],
+        compiler_params=pltpu.CompilerParams(collective_id=collective_id, has_side_effects=True),
+        cost_estimate=pl.CostEstimate(flops=10_000_000_000, bytes_accessed=2 * 4 * tiles.size, transcendentals=0),
+        name="sum_tiles",
+    )(tiles)
 
 
 def settle_kernel(block, depth, ahead, first, src_ref, *refs):
@@ -650,34 +725,30 @@
         batch, tok, hidden = x_blk.shape
         heads, head_dim = w_qkv.shape[1], w_qkv.shape[3]
         tokens = batch * tok
-        rank = lax.axis_index("sp")
         wq = jnp.transpose(w_qkv, (1, 2, 3, 0)).reshape(heads, 3 * head_dim, hidden)
         wo = w_out.reshape(heads, head_dim, hidden)
-        dy_flat = dy_blk.reshape(tokens, hidden)
+        row = lambda a: a.reshape(1, hidden)
 
         def gather(a):
-            return lax.all_gather(a, "sp", axis=0, tiled=True)
-
-        x_norm = norm_forward(x_blk, ln_gain, ln_bias)
-        own = jnp.stack([dy_blk, x_norm], axis=0).reshape(2, batch, COLOURS, tok // COLOURS, hidden).transpose(1, 2, 0, 3, 4)
-        meta = jnp.pad(jnp.concatenate([pos_blk, keep_blk], axis=0), ((0, 8 - 2 * batch), (0, LANES - tok)))
-        bias = lax.dynamic_slice_in_dim(b_qkv, rank, 1, 0).reshape(1, 3 * head_dim)
-        slope = jnp.exp2(-8.0 * (rank + 1).astype(jnp.float32) / heads).reshape(1)
-        _, parts, early, grad_head, grad_tail, grad_out = block_call(own, wq, bias, wo, meta, slope, size, 256, 0)
-
-        rows, split = 3 * head_dim, 3 * head_dim - TAIL_ROWS
-        grad_wq = settle(gather(grad_head).reshape(heads, split, hidden), 0, rows, split // 2)
-        grad_wq = settle(gather(grad_tail).reshape(heads, TAIL_ROWS, hidden), split, rows, TAIL_ROWS, grad_wq)
+            return lax.all_gather(a, "sp", axis=0, tiled=True).reshape(heads, a.shape[0], hidden)
+
+        _, parts, early, grad_a, grad_b, grad_c, grad_out = block_call(
+            x_blk, dy_blk, row(ln_gain), row(ln_bias), pos_blk, keep_blk, wq, jnp.transpose(b_qkv, (1, 0, 2)), wo, size, 256, 0)
+
+        rows = 3 * head_dim
+        first, second, third = split_rows(rows)
+        grad_wq = settle(gather(grad_a), 0, rows, first)
+        grad_wq = settle(gather(grad_b), first, rows, second // 2, grad_wq)
+        grad_wq = settle(gather(grad_c), first + second, rows, third, grad_wq)
         out_all, last = spread(grad_out, parts, size, 1)
         grad_wo = settle(out_all, 0, head_dim, head_dim)
 
-        y, grad_x, bq_part, sums = token_side(
-            early, last, wq, wo, x_blk.reshape(tokens, hidden), dy_flat, ln_gain.reshape(1, hidden), b_out.reshape(1, hidden), head_dim)
-        bq, gain, bias_sum, bo = lax.psum((bq_part.reshape(-1), sums[0], sums[1], sums[2]), "sp")
+        y, grad_x, tiles = token_side(
+            early, last, wq, wo, x_blk.reshape(tokens, hidden), dy_blk.reshape(tokens, hidden), row(ln_gain), row(b_out), head_dim)
+        totals = sum_tiles(tiles, size, 2)[:, :, :head_dim]
         grad_wq = jnp.transpose(grad_wq.reshape(heads, 3, head_dim, hidden), (3, 0, 1, 2))
-        return (y.reshape(x_blk.shape), grad_x.reshape(x_blk.shape), grad_wq, bq.reshape(heads, 3, head_dim),
-                grad_wo.reshape(heads * head_dim, hidden),
-                bo, gain, bias_sum)
+        return (y.reshape(x_blk.shape), grad_x.reshape(x_blk.shape), grad_wq, totals[:, 3:6],
+                grad_wo.reshape(heads * head_dim, hidden), totals[:, 2].reshape(-1), totals[:, 0].reshape(-1), totals[:, 1].reshape(-1))
 
     act_spec = P("dp", "sp", None)
     tok_spec = P("dp", "sp")

time: 578 us -> 598 us (1.035)
  waiting for transfers between devices: 5.02 us -> 74.6 us
  blocking collectives: 47.2 us -> 0 us
    all_gather x2 -> x3, waiting for transfers between devices: 4.23 us -> 73.1 us  [gather(): lax.all_gather(a, 'sp', axis=0, tiled=True)]
    psum x1 -> x0, blocking collectives: 47.2 us -> none  [block_fn(): lax.psum((bq_part.reshape(-1), sums[0], sums[1], sums[2]), 'sp')]
    pallas_call x1, Pallas kernels: 48.8 us -> 31.9 us  [token_side(): pl.pallas_call(functools.partial(token_kernel, head_dim, 16), grid=(heads...]
    pallas_call x0 -> x1, Pallas kernels: none -> 15.6 us  [sum_tiles(): pl.pallas_call(functools.partial(sums_kernel, size), out_shape=jax.ShapeD...]
    pallas_call x3 -> x4, Pallas kernels: 70.1 us -> 74.5 us  [settle(): pl.pallas_call(functools.partial(settle_kernel, block, depth, ahead, firs...]
  transfers between devices with their start and end apart: 2 -> 3, of which waited for: 1 -> 2; matrix products, arithmetic and copies ran while one was open for 1% -> 1% of each run, Pallas kernels for 45% -> 45%
where the time goes in v5:
time: 598 us; the launch traced here: 597 us
  Pallas kernels  501 us (84%)
  waiting for transfers between devices  74.6 us (12%)
  between operations  13.9 us (2%)
  local copies, waits for them, and re-layouts  8 us (1%)
    pallas_call x1, Pallas kernels, block_call(): pl.pallas_call(functools.partial(block_kernel, size, (batch, tok, head_di...  224 us
    pallas_call x1, Pallas kernels, spread(): pl.pallas_call(functools.partial(spread_kernel, size), out_shape=(jax.Sha...  154 us
    pallas_call x4, Pallas kernels, settle(): pl.pallas_call(functools.partial(settle_kernel, block, depth, ahead, firs...  74.5 us
    all_gather x3, waiting for transfers between devices, gather(): lax.all_gather(a, 'sp', axis=0, tiled=True)  73.1 us
    pallas_call x1, Pallas kernels, token_side(): pl.pallas_call(functools.partial(token_kernel, head_dim, 16), grid=(heads...  31.9 us
    pallas_call x1, Pallas kernels, sum_tiles(): pl.pallas_call(functools.partial(sums_kernel, size), out_shape=jax.ShapeD...  15.6 us
  transfers between devices with their start and end apart: 3, of which 2 were waited for; matrix products, arithmetic and copies ran while one was open for 1% of the time, Pallas kernels for 45%

profile of v5, /device:TPU:97, one launch (start us, length us, event | category | flops | bytes accessed | tf_op | source)
XLA Modules:
  0.0 597.4 jit_solution(16155589454211477802)
XLA Ops:
  7.2 0.1 all-gather.8.cloned.1.call-start
  7.2 1.3 reshape.67.gain_ref
  8.6 1.3 reshape.68.shift_ref
  9.9 224.4 %block.1 = (bf16[3,32,4,2,16,2560]{5,4,3,2,1,0:T(8,128)(2,1)}, bf16[3,32,32,640]{3,2,1,0:T(8,128)(2,1)}, bf16[32,2,32,640]{3,2,1,0:T(8,128)(2,1)}, f32[72,2560]{...) custom-call(bf16[3,4,16,2560]{3,2,1,0:T(8,128)(2,1)} %bitcast.26, ...), custom_call_target="tpu_custom_call" | custom-call | flops 119460012032 | bytes 60000000 | tf_op jit(solution)/shard_map/block/pallas_call | solution.py:398
  234.3 0.1 all-gather.6.cloned.1.call-start
  234.4 0.7 all-gather.6.cloned.1.call-update
  235.1 0.1 all-gather.4.cloned.1.call-start
  235.2 0.7 all-gather.4.cloned.1.call-update
  236.0 154.3 %spread.1 = (f32[32,80,2560]{2,1,0:T(8,128)}, bf16[32,32,640]{2,1,0:T(8,128)(2,1)}) custom-call(f32[80,2560]{1,0:T(8,128)} %get-tuple-element.20.own_ref, bf16[3,32,32,640]{3,2,1,0:T(8,128)(2,1)} %get-tuple-element.21.parts_ref), custom_call_target="tpu_custom_call" | custom-call | flops 99999997952 | bytes 52428800 | tf_op jit(solution)/shard_map/spread/pallas_call | solution.py:517
  390.3 0.6 reshape.73.bout_ref
  390.9 31.9 %token_side.1 = (bf16[192,2560]{1,0:T(8,128)(2,1)}, bf16[192,2560]{1,0:T(8,128)(2,1)}, f32[32,8,128]{2,1,0:T(8,128)}) custom-call(bf16[32,2,32,640]{3,2,1,0:T(8,128)(2,1)} %get-tuple-element.19.early_ref, bf16[32,32,640]{2,1,0:T(8,128)(2,1)} %get-tuple-element.22.last_ref, bf16[32,240,2560]{2,1,0:T(8,128)(2,1)} %bitcast.20, bf16[32,80,2560]{2,1,0:T(8,128)(2,1)} %bitcast.24, ...), custom_call_target="tpu_custom_call" | custom-call | flops 10066329600 | bytes 52428800 | tf_op jit(solution)/shard_map/token_side/pallas_call | solution.py:600
  422.8 15.6 %sum_tiles.1 = f32[32,8,128]{2,1,0:T(8,128)} custom-call(f32[32,8,128]{2,1,0:T(8,128)} %get-tuple-element.28.tiles_ref), custom_call_target="tpu_custom_call" | custom-call | flops 10000000000 | bytes 262144 | tf_op jit(solution)/shard_map/sum_tiles/pallas_call | solution.py:651
  438.4 0.9 slice.17
  439.3 1.2 slice_reduce_fusion
  440.5 0.7 reshape_squeeze.10
  441.2 0.7 reshape_squeeze.11
  441.9 0.7 reshape_squeeze.9
  442.5 0.6 copy.20
  443.2 17.9 %settle.7 = f32[32,80,2560]{2,1,0:T(8,128)} custom-call(f32[32,80,2560]{2,1,0:T(8,128)} %get-tuple-element.29.src_ref), custom_call_target="tpu_custom_call" | custom-call | flops 10000000000 | bytes 52428800 | tf_op jit(solution)/shard_map/settle/pallas_call | solution.py:708
  461.0 16.3 %settle.4.refs_0_ = f32[32,240,2560]{2,1,0:T(8,128)} custom-call(f32[32,72,2560]{2,1,0:T(8,128)} %bitcast.22), custom_call_target="tpu_custom_call" | custom-call | flops 10000000000 | bytes 47185920 | tf_op jit(solution)/shard_map/settle/pallas_call | solution.py:708
  477.4 67.3 %all-gather.6.cloned.1.call-done = f32[5120,2560]{1,0:T(8,128)} async-done(((f32[160,2560]{1,0:T(8,128)}), f32[5120,2560]{1,0:T(8,128)}) %all-gather.6.cloned.1.call-update) | async-done | bytes 52428816 | tf_op jit(solution)/shard_map/all_gather | solution.py:733
  544.7 34.3 %settle.5.refs_0_ = f32[32,240,2560]{2,1,0:T(8,128)} custom-call(f32[32,160,2560]{2,1,0:T(8,128)} %bitcast.18, f32[32,240,2560]{2,1,0:T(8,128)} %settle.4.refs_0_), custom_call_target="tpu_custom_call", output_to_operand_aliasing={{}: (1, {})} | custom-call | flops 10000000000 | bytes 104857600 | tf_op jit(solution)/shard_map/settle/pallas_call | solution.py:708
  579.0 5.8 all-gather.4.cloned.1.call-done
  584.8 6.0 %settle.6 = f32[32,240,2560]{2,1,0:T(8,128)} custom-call(f32[32,8,2560]{2,1,0:T(8,128)} %bitcast.25, f32[32,240,2560]{2,1,0:T(8,128)} %settle.5.refs_0_), custom_call_target="tpu_custom_call", output_to_operand_aliasing={{}: (1, {})} | custom-call | flops 10000000000 | bytes 5242880 | tf_op jit(solution)/shard_map/settle/pallas_call | solution.py:708
  (4 shorter events, 0.1 us)
Async XLA Ops:
  7.2 453.9 %all-gather.8.cloned.1.call-start = ((), (), s32[]{:S(2)}) async-start(), calls=%async_computation.2 | async-start | bytes 24330240 | tf_op jit(solution)/shard_map/all_gather | solution.py:733
  234.3 310.4 %all-gather.6.cloned.1.call-start = ((), (), s32[]{:S(2)}) async-start(), calls=%async_computation.1 | async-start | bytes 54067200 | tf_op jit(solution)/shard_map/all_gather | solution.py:733
  235.1 349.6 %all-gather.4.cloned.1.call-start = ((), (), s32[]{:S(2)}) async-start(), calls=%async_computation | async-start | bytes 2703360 | tf_op jit(solution)/shard_map/all_gather | solution.py:733
  235.9 154.3 %copy-start = (f32[2560]{0:T(1024)S(1)}, f32[2560]{0:T(1024)}, u32[]{:S(2)}) copy-start(f32[2560]{0:T(1024)} %param.18) | copy-start | bytes 30724
Sparse Core Ops, SparseCore 0:
  234.5 150.8 all-gather.7
  387.5 157.1 all-gather.5
  546.8 37.9 all-gather.3

commit v6 on v5

--- a/solution.py
+++ b/solution.py
@@ -32,33 +32,30 @@
 
 
 class Direct:
-    def __init__(self, me, size, src, dst, send_sems, recv_sems):
-        self.me, self.size, self.src, self.dst, self.send_sems, self.recv_sems = me, size, src, dst, send_sems, recv_sems
-
-    def copy(self, d, peer, slot):
-        return pltpu.make_async_remote_copy(
-            src_ref=self.src(peer), dst_ref=self.dst(slot), send_sem=self.send_sems.at[d], recv_sem=self.recv_sems.at[d],
-            device_id={"sp": peer}, device_id_type=MESH)
-
-    def loop(self, step):
+    def __init__(self, me, size, src, dst, whole, send_sem, recv_sem):
+        self.me, self.size, self.src, self.dst, self.whole, self.send_sem, self.recv_sem = me, size, src, dst, whole, send_sem, recv_sem
+
+    def start(self):
         def body(d, carry):
-            step(d)
+            peer = lax.rem(self.me + d, self.size)
+            pltpu.make_async_remote_copy(
+                src_ref=self.src(peer), dst_ref=self.dst(self.me), send_sem=self.send_sem, recv_sem=self.recv_sem,
+                device_id={"sp": peer}, device_id_type=MESH).start()
             return carry
 
         lax.fori_loop(1, self.size, body, 0)
 
-    def start(self):
-        self.loop(lambda d: self.copy(d, lax.rem(self.me + d, self.size), self.me).start())
+    def total(self):
+        ref = self.whole.at[pl.ds(0, self.size - 1)]
+        return pltpu.make_async_remote_copy(
+            src_ref=ref, dst_ref=ref, send_sem=self.send_sem, recv_sem=self.recv_sem,
+            device_id={"sp": self.me}, device_id_type=MESH)
 
     def wait_recv(self):
-        def one(d):
-            peer = lax.rem(self.me + self.size - d, self.size)
-            self.copy(d, peer, peer).wait_recv()
-
-        self.loop(one)
+        self.total().wait_recv()
 
     def wait_send(self):
-        self.loop(lambda d: self.copy(d, lax.rem(self.me + d, self.size), self.me).wait_send())
+        self.total().wait_send()
 
 
 FIRST_OF = (2, 3, 0, 1)
@@ -123,21 +120,21 @@
         dst = gat_ref.at[b, block, colour]
         return pltpu.make_async_remote_copy(
             src_ref=stage.at[b, colour] if is_own(place) else dst, dst_ref=dst,
-            send_sem=ici_send.at[b, link, place], recv_sem=ici_recv.at[b, link, place],
+            send_sem=ici_send.at[link], recv_sem=ici_recv.at[link, place],
             device_id={"sp": torus.neighbour(link)}, device_id_type=MESH)
 
     def arrival(b, link, place):
         block, colour = torus.chunk(link, place, 1)
         ref = gat_ref.at[b, block, colour]
         return pltpu.make_async_remote_copy(
-            src_ref=ref, dst_ref=ref, send_sem=ici_send.at[b, link, place], recv_sem=ici_recv.at[b, link, place],
+            src_ref=ref, dst_ref=ref, send_sem=ici_send.at[link], recv_sem=ici_recv.at[link, place],
             device_id={"sp": me}, device_id_type=MESH)
 
     def share(b, link, place, shift):
         block, colour = torus.chunk(link, place, 1)
         ref = gat_ref.at[b, block + shift, colour]
         return pltpu.make_async_remote_copy(
-            src_ref=ref, dst_ref=ref, send_sem=d2d_send.at[b, link, place], recv_sem=d2d_recv.at[b, link, place],
+            src_ref=ref, dst_ref=ref, send_sem=d2d_send.at[link], recv_sem=d2d_recv.at[link, place],
             device_id={"sp": sibling}, device_id_type=MESH)
 
     def share_own(b, block):
@@ -154,11 +151,9 @@
     load_wo = pltpu.make_async_copy(wo_ref.at[me], wobuf, load_sems.at[3])
     for load in (load_x, load_dy, load_wq, load_wo):
         load.start()
-    meta = Direct(me, size, lambda j: metatile, lambda j: metabuf.at[j], meta_send, meta_recv)
-    early = batch - 1
-    trades = [Direct(me, size, lambda j, b=b: parts_ref.at[b, j], lambda j, b=b: partstok_ref.at[j, b], part_send.at[b], part_recv.at[b])
-              for b in range(early)]
-    own_parts = [pltpu.make_async_copy(parts_ref.at[b, me], partstok_ref.at[me, b], load_sems.at[4 + b]) for b in range(early)]
+    meta = Direct(me, size, lambda j: metatile, lambda j: metabuf.at[j], metabuf, meta_send, meta_recv)
+    trade = Direct(me, size, lambda j: parts_ref.at[0, j], lambda j: partstok_ref.at[j], partstok_ref, part_send, part_recv)
+    own_parts = pltpu.make_async_copy(parts_ref.at[0, me], partstok_ref.at[me], load_sems.at[4])
 
     def prepare():
         metatile[...] = jnp.zeros_like(metatile)
@@ -167,15 +162,16 @@
         metabuf[me] = metatile[...]
         load_x.wait()
 
-        def normalise(n, carry):
-            b, c = n // COLOURS, lax.rem(n, COLOURS)
-            x = xin[b, c].astype(jnp.float32)
+        gain, shift = gain_ref[...].reshape(1, 1, hidden), shift_ref[...].reshape(1, 1, hidden)
+
+        def normalise(b, carry):
+            x = xin[b].astype(jnp.float32)
             centered = x - jnp.mean(x, axis=-1, keepdims=True)
             inv_std = lax.rsqrt(jnp.mean(centered * centered, axis=-1, keepdims=True) + NORM_EPS)
-            stage[b, c, 1] = (centered * inv_std * gain_ref[...] + shift_ref[...]).astype(jnp.bfloat16)
+            stage[b, :, 1] = (centered * inv_std * gain + shift).astype(jnp.bfloat16)
             return carry
 
-        lax.fori_loop(0, batch * COLOURS, normalise, 0)
+        lax.fori_loop(0, batch, normalise, 0)
         load_dy.wait()
 
     greet_all(me, size, prepare)
@@ -327,9 +323,6 @@
             def _():
                 for link in range(4):
                     share(b_shared, link, shared, flip).wait_recv()
-                for link in range(4):
-                    share(b_shared, link, shared, 0).wait_send()
-                    send(b_shared, link, shared).wait_send()
 
             if place == 1:
                 @pl.when(i == 0)
@@ -357,9 +350,8 @@
             if place == READY:
                 @pl.when(i == batch)
                 def _():
-                    for b in range(early):
-                        own_parts[b].start()
-                        trades[b].start()
+                    own_parts.start()
+                    trade.start()
 
             for later in (0, 1):
                 if (later, place) in tasks:
@@ -370,15 +362,21 @@
         return carry
 
     lax.fori_loop(0, batch + 2, turn, 0)
-    for b in range(early):
-        own_parts[b].wait()
-        trades[b].wait_recv()
-        trades[b].wait_send()
+    own_parts.wait()
+    trade.wait_recv()
+    trade.wait_send()
+    sent = gat_ref.at[:, pl.ds(0, places), 0]
+    for link in range(4):
+        for sem in (ici_send, d2d_send):
+            pltpu.make_async_remote_copy(
+                src_ref=sent, dst_ref=sent, send_sem=sem.at[link], recv_sem=ici_recv.at[link, 0],
+                device_id={"sp": sibling}, device_id_type=MESH).wait_send()
 
 
 def split_rows(rows):
-    first = 8 * (rows * 3 // 80)
-    return first, rows - first - 8, 8
+    own = 8 * (rows // 60)
+    first = 16 * (rows // 24)
+    return first, rows - first - own, own
 
 
 def block_call(x, dy, gain, shift, pos, keep, wq, bias, wo, size, q_block, collective_id):
@@ -400,7 +398,7 @@
         out_shape=(
             jax.ShapeDtypeStruct((batch, size, COLOURS, 2, rows, hidden), bf16),
             jax.ShapeDtypeStruct((batch, size, tok // 2, 8 * head_dim), bf16),
-            jax.ShapeDtypeStruct((size, batch - 1, tok // 2, 8 * head_dim), bf16),
+            jax.ShapeDtypeStruct((size, tok // 2, 8 * head_dim), bf16),
             *(jax.ShapeDtypeStruct((n, hidden), f32) for n in split_rows(3 * head_dim)),
             jax.ShapeDtypeStruct((head_dim, hidden), f32),
         ),
@@ -423,9 +421,8 @@
             pltpu.VMEM((seq_len, pad_dim), bf16),
             pltpu.VMEM((seq_len, 3 * head_dim), bf16),
             pltpu.VMEM((size, tok // 2, 8 * head_dim), bf16),
-            sem((4 + batch,)), sem((batch,)), sem((side, side)), sem,
-            sem((batch, 4, places)), sem((batch, 4, places)), sem((batch, 4, places)), sem((batch, 4, places)),
-            sem((batch,)), sem((batch,)), sem((size,)), sem((size,)), sem((batch - 1, size)), sem((batch - 1, size)),
+            sem((5,)), sem((batch,)), sem((side, side)), sem,
+            sem((4,)), sem((4, places)), sem((4,)), sem((4, places)), sem((batch,)), sem((batch,)), sem, sem, sem, sem,
         ],
         compiler_params=pltpu.CompilerParams(collective_id=collective_id, has_side_effects=True, vmem_limit_bytes=VMEM_LIMIT),
         cost_estimate=pl.CostEstimate(flops=flops, bytes_accessed=60_000_000, transcendentals=batch * seq_len * seq_len // 2),
@@ -433,11 +430,10 @@
     )(x.reshape(cut), dy.reshape(cut), gain, shift, pos, keep, wq, bias, wo)
 
 
-def spread_kernel(size, own_ref, parts_ref, gat_ref, last_ref, stage, load_sem, keep_sem, part_sem,
+def spread_kernel(size, begin, own_ref, parts_ref, after_ref, gat_ref, late_ref, stage, load_sem, keep_sem, own_part_sems,
                   ici_send, ici_recv, d2d_send, d2d_recv, own_send, own_recv, part_send, part_recv):
     torus = Torus(size)
     me, sibling = torus.me, torus.sibling
-    b = parts_ref.shape[0] - 1
     part = own_ref.shape[1] // COLOURS
 
     def view(block, colour):
@@ -448,20 +444,20 @@
         dst = view(block, colour)
         return pltpu.make_async_remote_copy(
             src_ref=stage.at[:, pl.ds(colour * part, part)] if is_own(place) else dst, dst_ref=dst,
-            send_sem=ici_send.at[link, place], recv_sem=ici_recv.at[link, place],
+            send_sem=ici_send.at[link], recv_sem=ici_recv.at[link, place],
             device_id={"sp": torus.neighbour(link)}, device_id_type=MESH)
 
     def arrival(link, place):
         ref = view(*torus.chunk(link, place, 1))
         return pltpu.make_async_remote_copy(
-            src_ref=ref, dst_ref=ref, send_sem=ici_send.at[link, place], recv_sem=ici_recv.at[link, place],
+            src_ref=ref, dst_ref=ref, send_sem=ici_send.at[link], recv_sem=ici_recv.at[link, place],
             device_id={"sp": me}, device_id_type=MESH)
 
     def share(link, place, shift):
         block, colour = torus.chunk(link, place, 1)
         ref = view(block + shift, colour)
         return pltpu.make_async_remote_copy(
-            src_ref=ref, dst_ref=ref, send_sem=d2d_send.at[link, place], recv_sem=d2d_recv.at[link, place],
+            src_ref=ref, dst_ref=ref, send_sem=d2d_send.at[link], recv_sem=d2d_recv.at[link, place],
             device_id={"sp": sibling}, device_id_type=MESH)
 
     def share_own(block):
@@ -472,8 +468,12 @@
     load = pltpu.make_async_copy(own_ref, stage, load_sem)
     load.start()
     keep = pltpu.make_async_copy(stage, gat_ref.at[me], keep_sem)
-    trade = Direct(me, size, lambda j: parts_ref.at[b, j], lambda j: last_ref.at[j], part_send, part_recv)
-    own_part = pltpu.make_async_copy(parts_ref.at[b, me], last_ref.at[me], part_sem)
+    trades, own_parts = [], []
+    for n in range(parts_ref.shape[0] - begin):
+        b = begin + n
+        trades.append(Direct(me, size, lambda j, b=b: parts_ref.at[b, j], lambda j, n=n: late_ref.at[n, j], late_ref.at[n],
+                             part_send.at[n], part_recv.at[n]))
+        own_parts.append(pltpu.make_async_copy(parts_ref.at[b, me], late_ref.at[n, me], own_part_sems.at[n]))
     greet_all(me, size)
     load.wait()
 
@@ -494,42 +494,49 @@
             if shared is not None:
                 share(link, shared, torus.flip).wait_recv()
         if g == 1:
-            trade.start()
-            own_part.start()
+            for copy in trades + own_parts:
+                copy.start()
             share_own(me).start()
             keep.start()
     share_own(sibling).wait_recv()
-    own_part.wait()
     keep.wait()
-    trade.wait_recv()
-    trade.wait_send()
+    for copy in own_parts:
+        copy.wait()
+    for trade in trades:
+        trade.wait_recv()
+        trade.wait_send()
     share_own(me).wait_send()
-    for place in range(PLACES):
-        for link in range(4):
-            send(link, place).wait_send()
-            share(link, place, 0).wait_send()
-
-
-def spread(block, parts, size, collective_id):
+    sent = gat_ref.at[pl.ds(0, PLACES), :, pl.ds(0, part)]
+    for link in range(4):
+        for sem in (ici_send, d2d_send):
+            pltpu.make_async_remote_copy(
+                src_ref=sent, dst_ref=sent, send_sem=sem.at[link], recv_sem=ici_recv.at[link, 0],
+                device_id={"sp": sibling}, device_id_type=MESH).wait_send()
+
+
+def spread(block, parts, begin, after, size, collective_id):
     rows, cols = block.shape
+    late = parts.shape[0] - begin
     anywhere = pl.BlockSpec(memory_space=pl.ANY)
     sem = pltpu.SemaphoreType.DMA
+    late_shape = (late, *parts.shape[1:]) if late else (8, LANES)
     return pl.pallas_call(
-        functools.partial(spread_kernel, size),
-        out_shape=(jax.ShapeDtypeStruct((size, rows, cols), block.dtype), jax.ShapeDtypeStruct(parts.shape[1:], parts.dtype)),
-        in_specs=[anywhere, anywhere],
+        functools.partial(spread_kernel, size, begin),
+        out_shape=(jax.ShapeDtypeStruct((size, rows, cols), block.dtype), jax.ShapeDtypeStruct(late_shape, parts.dtype)),
+        in_specs=[anywhere, anywhere, anywhere],
         out_specs=(anywhere, anywhere),
         scratch_shapes=[
-            pltpu.VMEM((rows, cols), block.dtype), sem, sem, sem,
-            sem((4, PLACES)), sem((4, PLACES)), sem((4, PLACES)), sem((4, PLACES)), sem, sem, sem((size,)), sem((size,)),
+            pltpu.VMEM((rows, cols), block.dtype), sem, sem, sem((max(late, 1),)),
+            sem((4,)), sem((4, PLACES)), sem((4,)), sem((4, PLACES)), sem, sem, sem((max(late, 1),)), sem((max(late, 1),)),
         ],
         compiler_params=pltpu.CompilerParams(collective_id=collective_id, has_side_effects=True),
-        cost_estimate=pl.CostEstimate(flops=100_000_000_000, bytes_accessed=8 * size * rows * cols, transcendentals=0),
+        cost_estimate=pl.CostEstimate(
+            flops=100_000_000_000 if late else 30_000_000_000, bytes_accessed=8 * size * rows * cols, transcendentals=0),
         name="spread",
-    )(block, parts)
-
-
-def token_kernel(head_dim, chunk, early_ref, last_ref, wq_ref, wo_ref, x_ref, dy_ref, gain_ref, bout_ref,
+    )(block, parts, after)
+
+
+def token_kernel(head_dim, chunk, early_ref, late_ref, wq_ref, wo_ref, x_ref, dy_ref, gain_ref, bout_ref,
                  y_ref, gx_ref, tiles_ref, dn_acc, y_acc, sums):
     n = pl.program_id(0)
     step = wq_ref.shape[0]
@@ -541,8 +548,7 @@
     dn_term = y_term = 0.0
     for h in range(step):
         parts = []
-        for b in range(early_ref.shape[1] + 1):
-            pair = early_ref[h, b] if b < early_ref.shape[1] else last_ref[h]
+        for pair in [early_ref[h]] + [late_ref[b, h] for b in range(late_ref.shape[0])]:
             parts += [pair[:, :4 * head_dim], pair[:, 4 * head_dim:]]
         parts = jnp.concatenate(parts, axis=0)
         dqkv = parts[:, :3 * head_dim]
@@ -591,7 +597,7 @@
             tiles_ref[j, 0:3, 0:head_dim] = sums[0:3, j * head_dim:(j + 1) * head_dim]
 
 
-def token_side(early, last, wq, wo, x, dy, gain, bout, head_dim):
+def token_side(early, late, wq, wo, x, dy, gain, bout, head_dim):
     heads = early.shape[0]
     tokens, hidden = x.shape
     step = 4
@@ -606,8 +612,8 @@
             jax.ShapeDtypeStruct((heads, 8, LANES), jnp.float32),
         ),
         in_specs=[
-            pl.BlockSpec((step, *early.shape[1:]), lambda n: (n, 0, 0, 0)),
-            pl.BlockSpec((step, *last.shape[1:]), per_head),
+            pl.BlockSpec((step, *early.shape[1:]), per_head),
+            pl.BlockSpec((late.shape[0], step, *late.shape[2:]), lambda n: (0, n, 0, 0)),
             pl.BlockSpec((step, 3 * head_dim, hidden), per_head),
             pl.BlockSpec((step, head_dim, hidden), per_head),
             pl.BlockSpec((tokens, hidden), whole),
@@ -625,7 +631,7 @@
         cost_estimate=pl.CostEstimate(
             flops=2 * tokens * hidden * 4 * heads * head_dim, bytes_accessed=8 * hidden * heads * head_dim, transcendentals=0),
         name="token_side",
-    )(early, last, wq, wo, x, dy, gain, bout)
+    )(early, late, wq, wo, x, dy, gain, bout)
 
 
 def sums_kernel(size, tiles_ref, all_ref, come, total, own_sem, send_a, recv_a, send_b, recv_b):
@@ -633,15 +639,15 @@
     greet_all(me, size)
     own = pltpu.make_async_copy(tiles_ref.at[me], come.at[me], own_sem)
     own.start()
-    spread_out = Direct(me, size, lambda j: tiles_ref.at[j], lambda j: come.at[j], send_a, recv_a)
-    spread_out.start()
+    deal = Direct(me, size, lambda j: tiles_ref.at[j], lambda j: come.at[j], come, send_a, recv_a)
+    deal.start()
     own.wait()
-    spread_out.wait_recv()
+    deal.wait_recv()
     total[...] = jnp.sum(come[...], axis=0)
     all_ref[me] = total[...]
-    collect = Direct(me, size, lambda j: total, lambda j: all_ref.at[j], send_b, recv_b)
+    collect = Direct(me, size, lambda j: total, lambda j: all_ref.at[j], all_ref, send_b, recv_b)
     collect.start()
-    spread_out.wait_send()
+    deal.wait_send()
     collect.wait_recv()
     collect.wait_send()
 
@@ -654,7 +660,7 @@
         in_specs=[pl.BlockSpec(memory_space=pl.ANY)],
         out_specs=pl.BlockSpec(memory_space=pltpu.VMEM),
         scratch_shapes=[pltpu.VMEM(tiles.shape, tiles.dtype), pltpu.VMEM(tiles.shape[1:], tiles.dtype),
-                        sem, sem((size,)), sem((size,)), sem((size,)), sem((size,))],
+                        sem, sem, sem, sem, sem],
         compiler_params=pltpu.CompilerParams(collective_id=collective_id, has_side_effects=True),
         cost_estimate=pl.CostEstimate(flops=10_000_000_000, bytes_accessed=2 * 4 * tiles.size, transcendentals=0),
         name="sum_tiles",
@@ -700,7 +706,7 @@
     lax.fori_loop(max(0, count - depth), count, drain, 0)
 
 
-def settle(x, first, total, block, into=None):
+def settle(x, first, total, block, into=None, after=()):
     depth, ahead = 12, 6
     count, _, cols = x.shape
     sem = pltpu.SemaphoreType.DMA((depth,))
@@ -708,14 +714,14 @@
     return pl.pallas_call(
         functools.partial(settle_kernel, block, depth, ahead, first),
         out_shape=jax.ShapeDtypeStruct((count, total, cols), x.dtype),
-        in_specs=[pl.BlockSpec(memory_space=pl.ANY)] * (1 + len(old)),
+        in_specs=[pl.BlockSpec(memory_space=pl.ANY)] * (1 + len(old) + len(after)),
         out_specs=pl.BlockSpec(memory_space=pl.ANY),
         scratch_shapes=[pltpu.VMEM((depth, block, cols), x.dtype), sem, sem],
         input_output_aliases={1: 0} if old else {},
         compiler_params=pltpu.CompilerParams(vmem_limit_bytes=VMEM_LIMIT),
         cost_estimate=pl.CostEstimate(flops=10_000_000_000, bytes_accessed=8 * x.size, transcendentals=0),
         name="settle",
-    )(x, *old)
+    )(x, *old, *after)
 
 
 def solution(mesh):
@@ -733,19 +739,21 @@
             return lax.all_gather(a, "sp", axis=0, tiled=True).reshape(heads, a.shape[0], hidden)
 
         _, parts, early, grad_a, grad_b, grad_c, grad_out = block_call(
-            x_blk, dy_blk, row(ln_gain), row(ln_bias), pos_blk, keep_blk, wq, jnp.transpose(b_qkv, (1, 0, 2)), wo, size, 256, 0)
+            x_blk, dy_blk, ln_gain, ln_bias, pos_blk, keep_blk, wq, jnp.transpose(b_qkv, (1, 0, 2)), wo, size, 256, 0)
+
+        all_out, late = spread(grad_out, parts, 1, grad_a, size, 1)
+        y, grad_x, tiles = token_side(
+            early, late, wq, wo, x_blk.reshape(tokens, hidden), dy_blk.reshape(tokens, hidden), row(ln_gain), row(b_out), head_dim)
+        totals = sum_tiles(tiles, size, 2)
+        grad_wo = settle(all_out, 0, head_dim, head_dim, after=(totals,))
 
         rows = 3 * head_dim
-        first, second, third = split_rows(rows)
-        grad_wq = settle(gather(grad_a), 0, rows, first)
-        grad_wq = settle(gather(grad_b), first, rows, second // 2, grad_wq)
-        grad_wq = settle(gather(grad_c), first + second, rows, third, grad_wq)
-        out_all, last = spread(grad_out, parts, size, 1)
-        grad_wo = settle(out_all, 0, head_dim, head_dim)
-
-        y, grad_x, tiles = token_side(
-            early, last, wq, wo, x_blk.reshape(tokens, hidden), dy_blk.reshape(tokens, hidden), row(ln_gain), row(b_out), head_dim)
-        totals = sum_tiles(tiles, size, 2)[:, :, :head_dim]
+        first, second, own = split_rows(rows)
+        all_c, _ = spread(grad_c, parts, batch, grad_wo, size, 3)
+        grad_wq = settle(gather(grad_a), 0, rows, first // 2, after=(all_c,))
+        grad_wq = settle(all_c, first + second, rows, own, grad_wq)
+        grad_wq = settle(gather(grad_b), first, rows, second, grad_wq)
+        totals = totals[:, :, :head_dim]
         grad_wq = jnp.transpose(grad_wq.reshape(heads, 3, head_dim, hidden), (3, 0, 1, 2))
         return (y.reshape(x_blk.shape), grad_x.reshape(x_blk.shape), grad_wq, totals[:, 3:6],
                 grad_wo.reshape(heads * head_dim, hidden), totals[:, 2].reshape(-1), totals[:, 0].reshape(-1), totals[:, 1].reshape(-1))

time: 598 us -> 565 us (0.945)
  waiting for transfers between devices: 74.6 us -> 0.83 us
  Pallas kernels: 501 us -> 543 us
    all_gather x3 -> x2, waiting for transfers between devices: 73.1 us -> 0.04 us  [gather(): lax.all_gather(a, 'sp', axis=0, tiled=True)]
    pallas_call x1 -> x2, Pallas kernels: 154 us -> 216 us  [spread(): pl.pallas_call(functools.partial(spread_kernel, size, begin), out_shape=(...]
    pallas_call x1, Pallas kernels: 224 us -> 206 us  [block_call(): pl.pallas_call(functools.partial(block_kernel, size, (batch, tok, head_di...]
  transfers between devices with their start and end apart: 3 -> 2, of which waited for: 2 -> 0; matrix products, arithmetic and copies ran while one was open for 1% -> 1% of each run, Pallas kernels for 45% -> 58%
where the time goes in v6:
time: 565 us; the launch traced here: 564 us
  Pallas kernels  543 us (96%)
  between operations  14.2 us (3%)
  local copies, waits for them, and re-layouts  6.01 us (1%)
    pallas_call x2, Pallas kernels, spread(): pl.pallas_call(functools.partial(spread_kernel, size, begin), out_shape=(...  216 us
    pallas_call x1, Pallas kernels, block_call(): pl.pallas_call(functools.partial(block_kernel, size, (batch, tok, head_di...  206 us
    pallas_call x4, Pallas kernels, settle(): pl.pallas_call(functools.partial(settle_kernel, block, depth, ahead, firs...  71.8 us
    pallas_call x1, Pallas kernels, token_side(): pl.pallas_call(functools.partial(token_kernel, head_dim, 16), grid=(heads...  31.9 us
    pallas_call x1, Pallas kernels, sum_tiles(): pl.pallas_call(functools.partial(sums_kernel, size), out_shape=jax.ShapeD...  17.2 us
  transfers between devices with their start and end apart: 2, of which 0 were waited for; matrix products, arithmetic and copies ran while one was open for 1% of the time, Pallas kernels for 58%

profile of v6, /device:TPU:97, one launch (start us, length us, event | category | flops | bytes accessed | tf_op | source)
XLA Modules:
  0.0 564.4 jit_solution(1524286459373095117)
XLA Ops:
  7.2 0.1 all-gather.5.cloned.1.call-start
  7.3 0.0 copy-start
  7.3 205.9 %block.1 = (bf16[3,32,4,2,16,2560]{5,4,3,2,1,0:T(8,128)(2,1)}, bf16[3,32,32,640]{3,2,1,0:T(8,128)(2,1)}, bf16[32,32,640]{2,1,0:T(8,128)(2,1)}, f32[160,2560]{1,0...) custom-call(bf16[3,4,16,2560]{3,2,1,0:T(8,128)(2,1)} %bitcast.24, ...), custom_call_target="tpu_custom_call" | custom-call | flops 119460012032 | bytes 60000000 | tf_op jit(solution)/shard_map/block/pallas_call | solution.py:396
  213.2 0.1 all-gather.5.cloned.1.call-update
  213.2 0.1 all-gather.3.cloned.1.call-start
  213.3 0.7 all-gather.3.cloned.1.call-update
  214.0 0.6 reshape.64.gain_ref
  214.7 0.6 reshape.65.bout_ref
  215.3 163.2 %spread.2 = (f32[32,80,2560]{2,1,0:T(8,128)}, bf16[2,32,32,640]{3,2,1,0:T(8,128)(2,1)}) custom-call(f32[80,2560]{1,0:T(8,128)} %get-tuple-element.21.own_ref, bf16[3,32,32,640]{3,2,1,0:T(8,128)(2,1)} %get-tuple-element.22.parts_ref, f32[160,2560]{1,0:T(8,128)} %get-tuple-element.23.after_ref), custom_call_target="tpu_custom_call" | custom-call | flops 99999997952 | bytes 52428800 | tf_op jit(solution)/shard_map/spread/pallas_call | solution.py:523
  378.5 31.9 %token_side.1 = (bf16[192,2560]{1,0:T(8,128)(2,1)}, bf16[192,2560]{1,0:T(8,128)(2,1)}, f32[32,8,128]{2,1,0:T(8,128)}) custom-call(bf16[32,32,640]{2,1,0:T(8,128)(2,1)} %get-tuple-element.20.early_ref, bf16[2,32,32,640]{3,2,1,0:T(8,128)(2,1)} %get-tuple-element.24.late_ref, bf16[32,240,2560]{2,1,0:T(8,128)(2,1)} %bitcast.19, bf16[32,80,2560]{2,1,0:T(8,128)(2,1)} %bitcast.23, ...), custom_call_target="tpu_custom_call" | custom-call | flops 10066329600 | bytes 52428800 | tf_op jit(solution)/shard_map/token_side/pallas_call | solution.py:606
  410.4 17.2 %sum_tiles.1.refs_0_ = f32[32,8,128]{2,1,0:T(8,128)} custom-call(f32[32,8,128]{2,1,0:T(8,128)} %get-tuple-element.30.tiles_ref), custom_call_target="tpu_custom_call" | custom-call | flops 10000000000 | bytes 262144 | tf_op jit(solution)/shard_map/sum_tiles/pallas_call | solution.py:657
  427.6 0.9 slice.17
  428.5 1.2 slice_reduce_fusion
  429.8 0.7 reshape_squeeze.10
  430.5 0.7 reshape_squeeze.11
  431.1 0.7 reshape_squeeze.9
  431.8 0.6 copy.20
  432.4 17.9 %settle.4.after_ref = f32[32,80,2560]{2,1,0:T(8,128)} custom-call(f32[32,80,2560]{2,1,0:T(8,128)} %get-tuple-element.29.src_ref, f32[32,8,128]{2,1,0:T(8,128)} %sum_tiles.1.refs_0_), custom_call_target="tpu_custom_call" | custom-call | flops 10000000000 | bytes 52428800 | tf_op jit(solution)/shard_map/settle/pallas_call | solution.py:714
  450.3 53.2 %spread.3 = (f32[32,32,2560]{2,1,0:T(8,128)}, bf16[8,128]{1,0:T(8,128)(2,1)}) custom-call(f32[32,2560]{1,0:T(8,128)} %get-tuple-element.28.own_ref, bf16[3,32,32,640]{3,2,1,0:T(8,128)(2,1)} %get-tuple-element.22.parts_ref, f32[32,80,2560]{2,1,0:T(8,128)} %settle.4.after_ref), custom_call_target="tpu_custom_call" | custom-call | flops 30000001024 | bytes 20971520 | tf_op jit(solution)/shard_map/spread/pallas_call | solution.py:523
  503.5 0.0 all-gather.5.cloned.1.call-done
  503.5 34.4 %settle.5.refs_0_ = f32[32,240,2560]{2,1,0:T(8,128)} custom-call(f32[32,160,2560]{2,1,0:T(8,128)} %bitcast.17, f32[32,32,2560]{2,1,0:T(8,128)} %get-tuple-element.31.refs_0_.src_ref), custom_call_target="tpu_custom_call" | custom-call | flops 10000000000 | bytes 104857600 | tf_op jit(solution)/shard_map/settle/pallas_call | solution.py:714
  538.0 8.5 %settle.6.refs_0_ = f32[32,240,2560]{2,1,0:T(8,128)} custom-call(f32[32,32,2560]{2,1,0:T(8,128)} %get-tuple-element.31.refs_0_.src_ref, f32[32,240,2560]{2,1,0:T(8,128)} %settle.5.refs_0_), custom_call_target="tpu_custom_call", output_to_operand_aliasing={{}: (1, {})} | custom-call | flops 10000000000 | bytes 20971520 | tf_op jit(solution)/shard_map/settle/pallas_call | solution.py:714
  546.4 0.0 all-gather.3.cloned.1.call-done
  546.4 11.1 %settle.7 = f32[32,240,2560]{2,1,0:T(8,128)} custom-call(f32[32,48,2560]{2,1,0:T(8,128)} %bitcast.21, f32[32,240,2560]{2,1,0:T(8,128)} %settle.6.refs_0_), custom_call_target="tpu_custom_call", output_to_operand_aliasing={{}: (1, {})} | custom-call | flops 10000000000 | bytes 31457280 | tf_op jit(solution)/shard_map/settle/pallas_call | solution.py:714
  (3 shorter events, 0.0 us)
Async XLA Ops:
  7.2 496.3 %all-gather.5.cloned.1.call-start = ((), (), s32[]{:S(2)}) async-start(), calls=%async_computation.1 | async-start | bytes 54067200 | tf_op jit(solution)/shard_map/all_gather | solution.py:739
  7.3 206.8 %copy-start = (f32[2560]{0:T(1024)S(1)}, f32[2560]{0:T(1024)}, u32[]{:S(2)}) copy-start(f32[2560]{0:T(1024)} %gain_ref.1) | copy-start | bytes 30724
  7.3 207.4 %copy-start.1 = (f32[2560]{0:T(1024)S(1)}, f32[2560]{0:T(1024)}, u32[]{:S(2)}) copy-start(f32[2560]{0:T(1024)} %param.18) | copy-start | bytes 30724
  213.2 333.2 %all-gather.3.cloned.1.call-start = ((), (), s32[]{:S(2)}) async-start(), calls=%async_computation | async-start | bytes 16220160 | tf_op jit(solution)/shard_map/all_gather | solution.py:739
Sparse Core Ops, SparseCore 0:
  213.3 239.5 all-gather.4
  455.0 71.8 all-gather.2

commit v7 on v6

--- a/solution.py
+++ b/solution.py
@@ -11,6 +11,7 @@
 NORM_EPS = 1e-5
 MASK_FILL = -1e30
 LANES = 128
+LOG2E = 1.4426950408889634
 MESH = pl.DeviceIdType.MESH
 VMEM_LIMIT = 61 * 1024 * 1024
 
@@ -102,7 +103,7 @@
 
 
 def block_kernel(size, dims, x_ref, dy_ref, gain_ref, shift_ref, pos_ref, keep_ref, wq_ref, bias_ref, wo_ref,
-                 gat_ref, parts_ref, partstok_ref, gwa_ref, gwb_ref, gwc_ref, gwo_ref,
+                 gat_ref, parts_ref, partstok_ref, gwa_ref, gwb_ref, gwc_ref, gwd_ref, gwo_ref,
                  xin, stage, wbuf, wobuf, metatile, metabuf, rowbuf, sbuf, qkvb, dob, dk_acc, dv_acc, dq_all, o_all, d_all, pbuf,
                  load_sems, own_sems, piece_sems, parts_sem, ici_send, ici_recv, d2d_send, d2d_recv, own_send, own_recv,
                  meta_send, meta_recv, part_send, part_recv):
@@ -229,12 +230,13 @@
         do = dob[mine, :]
         pos = rowbuf[pl.ds(b, 1), :span]
         keep = rowbuf[pl.ds(b + batch, 1), :span]
-        bias = jnp.where(keep > 0, -slope * (pos[:, span - 1:] - pos).astype(jnp.float32), MASK_FILL)
-        scores = dot(q, k, 1, 1) * scale + bias
-        row_id = lax.broadcasted_iota(jnp.int32, (q_block, span), 0) + i * q_block
-        col_id = lax.broadcasted_iota(jnp.int32, (q_block, span), 1)
-        scores = jnp.where(col_id <= row_id, scores, MASK_FILL)
-        expo = jnp.exp(scores - jnp.max(scores, axis=-1, keepdims=True))
+        bias = jnp.where(keep > 0, (-slope * LOG2E) * (pos[:, span - 1:] - pos).astype(jnp.float32), MASK_FILL)
+        scores = dot(q, k, 1, 1) * (scale * LOG2E) + bias
+        row_id = lax.broadcasted_iota(jnp.int32, (q_block, q_block), 0)
+        col_id = lax.broadcasted_iota(jnp.int32, (q_block, q_block), 1)
+        corner = jnp.where(col_id <= row_id, scores[:, span - q_block:], MASK_FILL)
+        scores = jnp.concatenate([scores[:, :span - q_block], corner], axis=1) if i else corner
+        expo = jnp.exp2(scores - jnp.max(scores, axis=-1, keepdims=True))
         prob = expo * (1.0 / jnp.sum(expo, axis=-1, keepdims=True))
         prob_lo = prob.astype(jnp.bfloat16)
         o = dot(prob_lo, v, 1, 0).astype(jnp.bfloat16)
@@ -256,7 +258,7 @@
         pbuf[...] = jnp.concatenate([whole[:, :tok // 2], whole[:, tok // 2:]], axis=2)
         store_parts(b).start()
 
-    width = min(512, hidden)
+    width = min(1280, hidden)
 
     def gradient(p):
         d = jnp.concatenate([d_all[rows_at(p, e), :] for e in range(side)], axis=0)
@@ -266,7 +268,7 @@
             at = pl.ds(pl.multiple_of(n * width, width), width)
             term = dot(d, rows_of(p, 1, at), 0, 0)
             row = 0
-            for ref in (gwa_ref, gwb_ref, gwc_ref):
+            for ref in (gwa_ref, gwb_ref, gwc_ref, gwd_ref):
                 ref[:, at] += term[row:row + ref.shape[0]]
                 row += ref.shape[0]
             gwo_ref[:, at] += dot(o, rows_of(p, 0, at), 0, 0)
@@ -289,7 +291,7 @@
     for i in range(count):
         tasks.setdefault((0, READY + spot[i]), []).append(lambda b, i=i: attend(b, i))
 
-    for ref in (gwa_ref, gwb_ref, gwc_ref, gwo_ref):
+    for ref in (gwa_ref, gwb_ref, gwc_ref, gwd_ref, gwo_ref):
         ref[...] = jnp.zeros_like(ref)
 
     def phase_of(i, place):
@@ -374,9 +376,9 @@
 
 
 def split_rows(rows):
-    own = 8 * (rows // 60)
-    first = 16 * (rows // 24)
-    return first, rows - first - own, own
+    own, third = 8 * (rows // 34), 8 * max(1, rows // 80)
+    first = (rows - own - third) // 2
+    return first, first, third, own
 
 
 def block_call(x, dy, gain, shift, pos, keep, wq, bias, wo, size, q_block, collective_id):
@@ -403,7 +405,7 @@
             jax.ShapeDtypeStruct((head_dim, hidden), f32),
         ),
         in_specs=[anywhere, anywhere, vmem, vmem, vmem, vmem, anywhere, vmem, anywhere],
-        out_specs=(anywhere, anywhere, anywhere, vmem, vmem, vmem, vmem),
+        out_specs=(anywhere, anywhere, anywhere, vmem, vmem, vmem, vmem, vmem),
         scratch_shapes=[
             pltpu.VMEM(cut, bf16),
             pltpu.VMEM((batch, COLOURS, 2, rows, hidden), bf16),
@@ -430,149 +432,184 @@
     )(x.reshape(cut), dy.reshape(cut), gain, shift, pos, keep, wq, bias, wo)
 
 
-def spread_kernel(size, begin, own_ref, parts_ref, after_ref, gat_ref, late_ref, stage, load_sem, keep_sem, own_part_sems,
-                  ici_send, ici_recv, d2d_send, d2d_recv, own_send, own_recv, part_send, part_recv):
-    torus = Torus(size)
-    me, sibling = torus.me, torus.sibling
-    part = own_ref.shape[1] // COLOURS
-
-    def view(block, colour):
-        return gat_ref.at[block, :, pl.ds(colour * part, part)]
-
-    def send(link, place):
-        block, colour = torus.chunk(link, place, 0)
-        dst = view(block, colour)
+class Spread:
+    def __init__(self, size, own_ref, gat_ref, stage, sems):
+        self.torus, self.size, self.gat_ref, self.stage = Torus(size), size, gat_ref, stage
+        self.load_sem, self.keep_sem, self.ici_send, self.ici_recv, self.d2d_send, self.d2d_recv, self.own_send, self.own_recv = sems
+        self.part = stage.shape[1] // COLOURS
+        self.load = pltpu.make_async_copy(own_ref, stage, self.load_sem)
+        self.keep = pltpu.make_async_copy(stage, gat_ref.at[self.torus.me], self.keep_sem)
+
+    def columns(self, colour):
+        return pl.ds(colour * self.part, self.part)
+
+    def view(self, block, colour):
+        return self.gat_ref.at[block, :, self.columns(colour)]
+
+    def remote(self, src, dst, send_sem, recv_sem, device):
         return pltpu.make_async_remote_copy(
-            src_ref=stage.at[:, pl.ds(colour * part, part)] if is_own(place) else dst, dst_ref=dst,
-            send_sem=ici_send.at[link], recv_sem=ici_recv.at[link, place],
-            device_id={"sp": torus.neighbour(link)}, device_id_type=MESH)
-
-    def arrival(link, place):
-        ref = view(*torus.chunk(link, place, 1))
-        return pltpu.make_async_remote_copy(
-            src_ref=ref, dst_ref=ref, send_sem=ici_send.at[link], recv_sem=ici_recv.at[link, place],
-            device_id={"sp": me}, device_id_type=MESH)
-
-    def share(link, place, shift):
-        block, colour = torus.chunk(link, place, 1)
-        ref = view(block + shift, colour)
-        return pltpu.make_async_remote_copy(
-            src_ref=ref, dst_ref=ref, send_sem=d2d_send.at[link], recv_sem=d2d_recv.at[link, place],
-            device_id={"sp": sibling}, device_id_type=MESH)
-
-    def share_own(block):
-        return pltpu.make_async_remote_copy(
-            src_ref=stage, dst_ref=gat_ref.at[block], send_sem=own_send, recv_sem=own_recv,
-            device_id={"sp": sibling}, device_id_type=MESH)
-
-    load = pltpu.make_async_copy(own_ref, stage, load_sem)
-    load.start()
-    keep = pltpu.make_async_copy(stage, gat_ref.at[me], keep_sem)
+            src_ref=src, dst_ref=dst, send_sem=send_sem, recv_sem=recv_sem, device_id={"sp": device}, device_id_type=MESH)
+
+    def send(self, link, place):
+        block, colour = self.torus.chunk(link, place, 0)
+        dst = self.view(block, colour)
+        src = self.stage.at[:, self.columns(colour)] if is_own(place) else dst
+        return self.remote(src, dst, self.ici_send.at[link], self.ici_recv.at[link, place], self.torus.neighbour(link))
+
+    def arrival(self, link, place):
+        ref = self.view(*self.torus.chunk(link, place, 1))
+        return self.remote(ref, ref, self.ici_send.at[link], self.ici_recv.at[link, place], self.torus.me)
+
+    def share(self, link, place, shift):
+        block, colour = self.torus.chunk(link, place, 1)
+        ref = self.view(block + shift, colour)
+        return self.remote(ref, ref, self.d2d_send.at[link], self.d2d_recv.at[link, place], self.torus.sibling)
+
+    def share_own(self, block):
+        return self.remote(self.stage, self.gat_ref.at[block], self.own_send, self.own_recv, self.torus.sibling)
+
+    STEPS = PLACES + LATE + LAG + 2
+
+    def step(self, g):
+        def place_of(g):
+            place = g % PLACES
+            return place if g >= 0 and g // PLACES == (1 if place == LATE else 0) else None
+
+        came, now, shared = place_of(g - LAG), place_of(g), place_of(g - LAG - 1)
+        for link in range(4):
+            if came is not None:
+                self.arrival(link, came).wait_recv()
+                self.share(link, came, 0).start()
+        for link in range(4):
+            if now is not None:
+                self.send(link, now).start()
+        for link in range(4):
+            if shared is not None:
+                self.share(link, shared, self.torus.flip).wait_recv()
+        if g == 1:
+            self.share_own(self.torus.me).start()
+            self.keep.start()
+
+    def close(self):
+        self.share_own(self.torus.sibling).wait_recv()
+        self.keep.wait()
+        self.share_own(self.torus.me).wait_send()
+        sent = self.gat_ref.at[pl.ds(0, PLACES), :, pl.ds(0, self.part)]
+        for link in range(4):
+            for sem in (self.ici_send, self.d2d_send):
+                self.remote(sent, sent, sem.at[link], self.ici_recv.at[link, 0], self.torus.sibling).wait_send()
+
+    @staticmethod
+    def scratch(rows, cols, dtype):
+        sem = pltpu.SemaphoreType.DMA
+        return [pltpu.VMEM((rows, cols), dtype), sem, sem, sem((4,)), sem((4, PLACES)), sem((4,)), sem((4, PLACES)), sem, sem]
+
+
+def spread_kernel(size, own_ref, after_ref, gat_ref, stage, *sems):
+    spread = Spread(size, own_ref, gat_ref, stage, sems)
+    spread.load.start()
+    greet_all(spread.torus.me, size)
+    spread.load.wait()
+    for g in range(Spread.STEPS):
+        spread.step(g)
+    spread.close()
+
+
+def spread_rows(block, after, size, collective_id):
+    rows, cols = block.shape
+    anywhere = pl.BlockSpec(memory_space=pl.ANY)
+    return pl.pallas_call(
+        functools.partial(spread_kernel, size),
+        out_shape=jax.ShapeDtypeStruct((size, rows, cols), block.dtype),
+        in_specs=[anywhere, anywhere],
+        out_specs=anywhere,
+        scratch_shapes=Spread.scratch(rows, cols, block.dtype),
+        compiler_params=pltpu.CompilerParams(collective_id=collective_id, has_side_effects=True),
+        cost_estimate=pl.CostEstimate(flops=50_000_000_000, bytes_accessed=8 * size * rows * cols, transcendentals=0),
+        name="spread",
+    )(block, after)
+
+
+TOKEN_AT = 8
+TOKEN_STEPS = 8
+
+
+def token_kernel(size, head_dim, chunk, own_ref, parts_ref, early_ref, wq_ref, wo_ref, x_ref, dy_ref, gain_ref, bout_ref,
+                 gat_ref, late_ref, y_ref, gx_ref, totals_ref,
+                 stage, load_sem, keep_sem, ici_send, ici_recv, d2d_send, d2d_recv, own_send, own_recv,
+                 wqbuf, wobuf, pbuf, dn_acc, y_acc, sums, tiles, come, total,
+                 part_send, part_recv, own_part_sems, wq_sems, wo_sems, p_sems, deal_send, deal_recv, collect_send, collect_recv):
+    spread = Spread(size, own_ref, gat_ref, stage,
+                    (load_sem, keep_sem, ici_send, ici_recv, d2d_send, d2d_recv, own_send, own_recv))
+    me = spread.torus.me
+    late = late_ref.shape[0]
+    heads, hidden = wq_ref.shape[0], wq_ref.shape[2]
+    per = heads // TOKEN_STEPS
     trades, own_parts = [], []
-    for n in range(parts_ref.shape[0] - begin):
-        b = begin + n
+    for n in range(late):
+        b = parts_ref.shape[0] - late + n
         trades.append(Direct(me, size, lambda j, b=b: parts_ref.at[b, j], lambda j, n=n: late_ref.at[n, j], late_ref.at[n],
                              part_send.at[n], part_recv.at[n]))
         own_parts.append(pltpu.make_async_copy(parts_ref.at[b, me], late_ref.at[n, me], own_part_sems.at[n]))
-    greet_all(me, size)
-    load.wait()
-
-    def place_of(g):
-        place = g % PLACES
-        return place if g >= 0 and g // PLACES == (1 if place == LATE else 0) else None
-
-    for g in range(PLACES + LATE + LAG + 2):
-        came, now, shared = place_of(g - LAG), place_of(g), place_of(g - LAG - 1)
-        for link in range(4):
-            if came is not None:
-                arrival(link, came).wait_recv()
-                share(link, came, 0).start()
-        for link in range(4):
-            if now is not None:
-                send(link, now).start()
-        for link in range(4):
-            if shared is not None:
-                share(link, shared, torus.flip).wait_recv()
-        if g == 1:
-            for copy in trades + own_parts:
+    deal = Direct(me, size, lambda j: tiles.at[j], lambda j: come.at[j], come, deal_send, deal_recv)
+    collect = Direct(me, size, lambda j: total, lambda j: totals_ref.at[j], totals_ref, collect_send, collect_recv)
+
+    def weights(m):
+        at, slot = pl.ds(m * per, per), m % 2
+        return (pltpu.make_async_copy(wq_ref.at[at], wqbuf.at[slot], wq_sems.at[slot]),
+                pltpu.make_async_copy(wo_ref.at[at], wobuf.at[slot], wo_sems.at[slot]))
+
+    def rows(m):
+        at, slot = pl.ds(m * per, per), m % 2
+        return [pltpu.make_async_copy(early_ref.at[at], pbuf.at[slot, 0], p_sems.at[slot, 0])] + [
+            pltpu.make_async_copy(late_ref.at[n, at], pbuf.at[slot, 1 + n], p_sems.at[slot, 1 + n]) for n in range(late)]
+
+    spread.load.start()
+    for copy in weights(0):
+        copy.start()
+    dn_acc[...] = jnp.zeros_like(dn_acc)
+    y_acc[...] = jnp.zeros_like(y_acc)
+    sums[...] = jnp.zeros_like(sums)
+    tiles[...] = jnp.zeros_like(tiles)
+    width = hidden // 4
+
+    def heads_step(m):
+        slot = m % 2
+        for copy in (*weights(m), *rows(m)):
+            copy.wait()
+        if m + 1 < TOKEN_STEPS:
+            for copy in (*weights(m + 1), *rows(m + 1)):
                 copy.start()
-            share_own(me).start()
-            keep.start()
-    share_own(sibling).wait_recv()
-    keep.wait()
-    for copy in own_parts:
-        copy.wait()
-    for trade in trades:
-        trade.wait_recv()
-        trade.wait_send()
-    share_own(me).wait_send()
-    sent = gat_ref.at[pl.ds(0, PLACES), :, pl.ds(0, part)]
-    for link in range(4):
-        for sem in (ici_send, d2d_send):
-            pltpu.make_async_remote_copy(
-                src_ref=sent, dst_ref=sent, send_sem=sem.at[link], recv_sem=ici_recv.at[link, 0],
-                device_id={"sp": sibling}, device_id_type=MESH).wait_send()
-
-
-def spread(block, parts, begin, after, size, collective_id):
-    rows, cols = block.shape
-    late = parts.shape[0] - begin
-    anywhere = pl.BlockSpec(memory_space=pl.ANY)
-    sem = pltpu.SemaphoreType.DMA
-    late_shape = (late, *parts.shape[1:]) if late else (8, LANES)
-    return pl.pallas_call(
-        functools.partial(spread_kernel, size, begin),
-        out_shape=(jax.ShapeDtypeStruct((size, rows, cols), block.dtype), jax.ShapeDtypeStruct(late_shape, parts.dtype)),
-        in_specs=[anywhere, anywhere, anywhere],
-        out_specs=(anywhere, anywhere),
-        scratch_shapes=[
-            pltpu.VMEM((rows, cols), block.dtype), sem, sem, sem((max(late, 1),)),
-            sem((4,)), sem((4, PLACES)), sem((4,)), sem((4, PLACES)), sem, sem, sem((max(late, 1),)), sem((max(late, 1),)),
-        ],
-        compiler_params=pltpu.CompilerParams(collective_id=collective_id, has_side_effects=True),
-        cost_estimate=pl.CostEstimate(
-            flops=100_000_000_000 if late else 30_000_000_000, bytes_accessed=8 * size * rows * cols, transcendentals=0),
-        name="spread",
-    )(block, parts, after)
-
-
-def token_kernel(head_dim, chunk, early_ref, late_ref, wq_ref, wo_ref, x_ref, dy_ref, gain_ref, bout_ref,
-                 y_ref, gx_ref, tiles_ref, dn_acc, y_acc, sums):
-    n = pl.program_id(0)
-    step = wq_ref.shape[0]
-
-    @pl.when(n == 0)
-    def _():
-        tiles_ref[...] = jnp.zeros_like(tiles_ref)
-
-    dn_term = y_term = 0.0
-    for h in range(step):
-        parts = []
-        for pair in [early_ref[h]] + [late_ref[b, h] for b in range(late_ref.shape[0])]:
-            parts += [pair[:, :4 * head_dim], pair[:, 4 * head_dim:]]
-        parts = jnp.concatenate(parts, axis=0)
-        dqkv = parts[:, :3 * head_dim]
-        total = jnp.sum(dqkv.astype(jnp.float32), axis=0, keepdims=True)
-        for c in range(3):
-            tiles_ref[n * step + h, 3 + c:4 + c, 0:head_dim] = total[:, c * head_dim:(c + 1) * head_dim]
-        dn_term += dot(dqkv, wq_ref[h], 1, 0)
-        y_term += dot(parts[:, 3 * head_dim:], wo_ref[h], 1, 0)
-
-    @pl.when(n == 0)
-    def _():
-        dn_acc[...] = dn_term
-        y_acc[...] = y_term
-
-    @pl.when(n > 0)
-    def _():
-        dn_acc[...] += dn_term
-        y_acc[...] += y_term
-
-    @pl.when(n == pl.num_programs(0) - 1)
-    def _():
-        sums[...] = jnp.zeros_like(sums)
-        gain = gain_ref[...]
-        bout = bout_ref[...]
+
+        def pair(i, carry):
+            ds, os = [], []
+            for h in range(2):
+                parts = []
+                for n in range(1 + late):
+                    both = pbuf[slot, n, i * 2 + h]
+                    parts += [both[:, :4 * head_dim], both[:, 4 * head_dim:]]
+                parts = jnp.concatenate(parts, axis=0)
+                ds.append(parts[:, :3 * head_dim])
+                os.append(parts[:, 3 * head_dim:])
+                added = jnp.sum(ds[h].astype(jnp.float32), axis=0, keepdims=True)
+                for c in range(3):
+                    tiles[m * per + i * 2 + h, 3 + c:4 + c, 0:head_dim] = added[:, c * head_dim:(c + 1) * head_dim]
+
+            def columns(n, carry):
+                at = pl.ds(pl.multiple_of(n * width, width), width)
+                dn_acc[:, at] += dot(ds[0], wqbuf[slot, i * 2, :, at], 1, 0) + dot(ds[1], wqbuf[slot, i * 2 + 1, :, at], 1, 0)
+                y_acc[:, at] += dot(os[0], wobuf[slot, i * 2, :, at], 1, 0) + dot(os[1], wobuf[slot, i * 2 + 1, :, at], 1, 0)
+                return carry
+
+            lax.fori_loop(0, 4, columns, 0)
+            return carry
+
+        lax.fori_loop(0, per // 2, pair, 0)
+
+    def norm_step(half):
+        gain = gain_ref[...].reshape(1, hidden)
+        bout = bout_ref[...].reshape(1, hidden)
+        count = x_ref.shape[0] // chunk
 
         def body(c, carry):
             at = pl.ds(pl.multiple_of(c * chunk, chunk), chunk)
@@ -592,79 +629,95 @@
             sums[2:3, :] += jnp.sum(dy, axis=0, keepdims=True)
             return carry
 
-        lax.fori_loop(0, x_ref.shape[0] // chunk, body, 0)
-        for j in range(tiles_ref.shape[0]):
-            tiles_ref[j, 0:3, 0:head_dim] = sums[0:3, j * head_dim:(j + 1) * head_dim]
-
-
-def token_side(early, late, wq, wo, x, dy, gain, bout, head_dim):
-    heads = early.shape[0]
-    tokens, hidden = x.shape
-    step = 4
-    whole = lambda n: (0, 0)
-    per_head = lambda n: (n, 0, 0)
-    return pl.pallas_call(
-        functools.partial(token_kernel, head_dim, 16),
-        grid=(heads // step,),
-        out_shape=(
-            jax.ShapeDtypeStruct((tokens, hidden), jnp.bfloat16),
-            jax.ShapeDtypeStruct((tokens, hidden), jnp.bfloat16),
-            jax.ShapeDtypeStruct((heads, 8, LANES), jnp.float32),
-        ),
-        in_specs=[
-            pl.BlockSpec((step, *early.shape[1:]), per_head),
-            pl.BlockSpec((late.shape[0], step, *late.shape[2:]), lambda n: (0, n, 0, 0)),
-            pl.BlockSpec((step, 3 * head_dim, hidden), per_head),
-            pl.BlockSpec((step, head_dim, hidden), per_head),
-            pl.BlockSpec((tokens, hidden), whole),
-            pl.BlockSpec((tokens, hidden), whole),
-            pl.BlockSpec((1, hidden), whole),
-            pl.BlockSpec((1, hidden), whole),
-        ],
-        out_specs=(
-            pl.BlockSpec((tokens, hidden), whole),
-            pl.BlockSpec((tokens, hidden), whole),
-            pl.BlockSpec((heads, 8, LANES), lambda n: (0, 0, 0)),
-        ),
-        scratch_shapes=[pltpu.VMEM((tokens, hidden), jnp.float32)] * 2 + [pltpu.VMEM((8, hidden), jnp.float32)],
-        compiler_params=pltpu.CompilerParams(vmem_limit_bytes=VMEM_LIMIT),
-        cost_estimate=pl.CostEstimate(
-            flops=2 * tokens * hidden * 4 * heads * head_dim, bytes_accessed=8 * hidden * heads * head_dim, transcendentals=0),
-        name="token_side",
-    )(early, late, wq, wo, x, dy, gain, bout)
-
-
-def sums_kernel(size, tiles_ref, all_ref, come, total, own_sem, send_a, recv_a, send_b, recv_b):
-    me = lax.axis_index("sp")
+        lax.fori_loop(half * count // 2, (half + 1) * count // 2, body, 0)
+
     greet_all(me, size)
-    own = pltpu.make_async_copy(tiles_ref.at[me], come.at[me], own_sem)
-    own.start()
-    deal = Direct(me, size, lambda j: tiles_ref.at[j], lambda j: come.at[j], come, send_a, recv_a)
-    deal.start()
-    own.wait()
-    deal.wait_recv()
-    total[...] = jnp.sum(come[...], axis=0)
-    all_ref[me] = total[...]
-    collect = Direct(me, size, lambda j: total, lambda j: all_ref.at[j], all_ref, send_b, recv_b)
-    collect.start()
+    spread.load.wait()
+    for g in range(Spread.STEPS):
+        spread.step(g)
+        m = g - TOKEN_AT
+        if g == 1:
+            for copy in trades + own_parts:
+                copy.start()
+        if m == 0:
+            for copy in own_parts:
+                copy.wait()
+            for trade in trades:
+                trade.wait_recv()
+            for copy in rows(0):
+                copy.start()
+        if 0 <= m < TOKEN_STEPS:
+            heads_step(m)
+        elif m in (TOKEN_STEPS, TOKEN_STEPS + 1):
+            norm_step(m - TOKEN_STEPS)
+        elif m == TOKEN_STEPS + 2:
+            for j in range(size):
+                tiles[j, 0:3, 0:head_dim] = sums[0:3, j * head_dim:(j + 1) * head_dim]
+            come[me] = tiles[me]
+        elif m == TOKEN_STEPS + 3:
+            deal.start()
+        elif m == TOKEN_STEPS + 5:
+            deal.wait_recv()
+            total[...] = jnp.sum(come[...], axis=0)
+            totals_ref[me] = total[...]
+            collect.start()
+    spread.close()
+    for trade in trades:
+        trade.wait_send()
     deal.wait_send()
     collect.wait_recv()
     collect.wait_send()
 
 
-def sum_tiles(tiles, size, collective_id):
+def token_side(block, parts, early, wq, wo, x, dy, gain, bout, size, collective_id):
+    rows, cols = block.shape
+    late = parts.shape[0] - 1
+    heads, head_dim, hidden = wo.shape
+    tokens = x.shape[0]
+    per = heads // TOKEN_STEPS
+    anywhere = pl.BlockSpec(memory_space=pl.ANY)
+    vmem = pl.BlockSpec(memory_space=pltpu.VMEM)
     sem = pltpu.SemaphoreType.DMA
+    bf16, f32 = jnp.bfloat16, jnp.float32
     return pl.pallas_call(
-        functools.partial(sums_kernel, size),
-        out_shape=jax.ShapeDtypeStruct(tiles.shape, tiles.dtype),
-        in_specs=[pl.BlockSpec(memory_space=pl.ANY)],
-        out_specs=pl.BlockSpec(memory_space=pltpu.VMEM),
-        scratch_shapes=[pltpu.VMEM(tiles.shape, tiles.dtype), pltpu.VMEM(tiles.shape[1:], tiles.dtype),
-                        sem, sem, sem, sem, sem],
-        compiler_params=pltpu.CompilerParams(collective_id=collective_id, has_side_effects=True),
-        cost_estimate=pl.CostEstimate(flops=10_000_000_000, bytes_accessed=2 * 4 * tiles.size, transcendentals=0),
-        name="sum_tiles",
-    )(tiles)
+        functools.partial(token_kernel, size, head_dim, 16),
+        out_shape=(
+            jax.ShapeDtypeStruct((size, rows, cols), block.dtype),
+            jax.ShapeDtypeStruct((late, *parts.shape[1:]), parts.dtype),
+            jax.ShapeDtypeStruct((tokens, hidden), bf16),
+            jax.ShapeDtypeStruct((tokens, hidden), bf16),
+            jax.ShapeDtypeStruct((size, 8, LANES), f32),
+        ),
+        in_specs=[anywhere] * 5 + [vmem] * 4,
+        out_specs=(anywhere, anywhere, vmem, vmem, vmem),
+        scratch_shapes=Spread.scratch(rows, cols, block.dtype) + [
+            pltpu.VMEM((2, per, 3 * head_dim, hidden), bf16),
+            pltpu.VMEM((2, per, head_dim, hidden), bf16),
+            pltpu.VMEM((2, 1 + late, per, *parts.shape[2:]), bf16),
+            pltpu.VMEM((tokens, hidden), f32),
+            pltpu.VMEM((tokens, hidden), f32),
+            pltpu.VMEM((8, hidden), f32),
+            pltpu.VMEM((size, 8, LANES), f32),
+            pltpu.VMEM((size, 8, LANES), f32),
+            pltpu.VMEM((8, LANES), f32),
+            sem((late,)), sem((late,)), sem((late,)), sem((2,)), sem((2,)), sem((2, 1 + late)), sem, sem, sem, sem,
+        ],
+        compiler_params=pltpu.CompilerParams(collective_id=collective_id, has_side_effects=True, vmem_limit_bytes=VMEM_LIMIT),
+        cost_estimate=pl.CostEstimate(flops=120_000_000_000, bytes_accessed=8 * size * rows * cols, transcendentals=0),
+        name="token_side",
+    )(block, parts, early, wq, wo, x, dy, gain, bout)
+
+
+def hand_kernel(y_ref, gx_ref, y_out, gx_out):
+    y_out[...] = y_ref[...]
+    gx_out[...] = gx_ref[...]
+
+
+def hand_over(y, gx):
+    spec = pl.BlockSpec((y.shape[0] // 4, y.shape[1]), lambda i: (i, 0))
+    return pl.pallas_call(
+        hand_kernel, grid=(4,), out_shape=(jax.ShapeDtypeStruct(y.shape, y.dtype),) * 2, in_specs=[spec] * 2, out_specs=(spec,) * 2,
+        cost_estimate=pl.CostEstimate(flops=1_000_000_000, bytes_accessed=8 * y.size, transcendentals=0), name="hand_over")(y, gx)
 
 
 def settle_kernel(block, depth, ahead, first, src_ref, *refs):
@@ -733,26 +786,25 @@
         tokens = batch * tok
         wq = jnp.transpose(w_qkv, (1, 2, 3, 0)).reshape(heads, 3 * head_dim, hidden)
         wo = w_out.reshape(heads, head_dim, hidden)
-        row = lambda a: a.reshape(1, hidden)
 
         def gather(a):
             return lax.all_gather(a, "sp", axis=0, tiled=True).reshape(heads, a.shape[0], hidden)
 
-        _, parts, early, grad_a, grad_b, grad_c, grad_out = block_call(
+        _, parts, early, grad_a, grad_b, grad_c, grad_d, grad_out = block_call(
             x_blk, dy_blk, ln_gain, ln_bias, pos_blk, keep_blk, wq, jnp.transpose(b_qkv, (1, 0, 2)), wo, size, 256, 0)
 
-        all_out, late = spread(grad_out, parts, 1, grad_a, size, 1)
-        y, grad_x, tiles = token_side(
-            early, late, wq, wo, x_blk.reshape(tokens, hidden), dy_blk.reshape(tokens, hidden), row(ln_gain), row(b_out), head_dim)
-        totals = sum_tiles(tiles, size, 2)
-        grad_wo = settle(all_out, 0, head_dim, head_dim, after=(totals,))
+        all_out, _, y, grad_x, totals = token_side(
+            grad_out, parts, early, wq, wo, x_blk.reshape(tokens, hidden), dy_blk.reshape(tokens, hidden), ln_gain, b_out, size, 1)
+        y, grad_x = hand_over(y, grad_x)
+        grad_wo = settle(all_out, 0, head_dim, head_dim, after=(y,))
 
         rows = 3 * head_dim
-        first, second, own = split_rows(rows)
-        all_c, _ = spread(grad_c, parts, batch, grad_wo, size, 3)
-        grad_wq = settle(gather(grad_a), 0, rows, first // 2, after=(all_c,))
-        grad_wq = settle(all_c, first + second, rows, own, grad_wq)
-        grad_wq = settle(gather(grad_b), first, rows, second, grad_wq)
+        first, second, third, own = split_rows(rows)
+        grad_wq = settle(gather(grad_a), 0, rows, first, after=(grad_wo,))
+        all_d = spread_rows(grad_d, grad_wq, size, 2)
+        grad_wq = settle(gather(grad_b), first, rows, second, grad_wq, after=(all_d,))
+        grad_wq = settle(all_d, first + second + third, rows, own, grad_wq)
+        grad_wq = settle(gather(grad_c), first + second, rows, third, grad_wq)
         totals = totals[:, :, :head_dim]
         grad_wq = jnp.transpose(grad_wq.reshape(heads, 3, head_dim, hidden), (3, 0, 1, 2))
         return (y.reshape(x_blk.shape), grad_x.reshape(x_blk.shape), grad_wq, totals[:, 3:6],

time: 565 us -> 573 us (1.014)
  Pallas kernels: 543 us -> 552 us
    pallas_call x4 -> x3, Pallas kernels: 266 us -> 274 us  [the longest x1 182 us: token_side(): pl.pallas_call(functools.partial(token_kernel, size, head_dim, 16), out_s...]
    pallas_call x4 -> x5, Pallas kernels: 71.8 us -> 74.1 us  [settle(): pl.pallas_call(functools.partial(settle_kernel, block, depth, ahead, firs...]
  transfers between devices with their start and end apart: 2 -> 3, of which waited for: 0 -> 0; matrix products, arithmetic and copies ran while one was open for 1% -> 1% of each run, Pallas kernels for 58% -> 60%
where the time goes in v7:
time: 573 us; the launch traced here: 572 us
  Pallas kernels  552 us (96%)
  between operations  13.9 us (2%)
    pallas_call x1, Pallas kernels, block_call(): pl.pallas_call(functools.partial(block_kernel, size, (batch, tok, head_di...  204 us
    pallas_call x1, Pallas kernels, token_side(): pl.pallas_call(functools.partial(token_kernel, size, head_dim, 16), out_s...  182 us
    pallas_call x1, Pallas kernels, spread_rows(): pl.pallas_call(functools.partial(spread_kernel, size), out_shape=jax.Shap...  87.9 us
    pallas_call x5, Pallas kernels, settle(): pl.pallas_call(functools.partial(settle_kernel, block, depth, ahead, firs...  74.1 us
  transfers between devices with their start and end apart: 3, of which 0 were waited for; matrix products, arithmetic and copies ran while one was open for 1% of the time, Pallas kernels for 60%

profile of v7, /device:TPU:97, one launch (start us, length us, event | category | flops | bytes accessed | tf_op | source)
XLA Modules:
  0.0 572.3 jit_solution(12943138084106719544)
XLA Ops:
  7.2 0.1 all-gather.6.cloned.1.call-start
  7.2 204.0 %block.1 = (bf16[3,32,4,2,16,2560]{5,4,3,2,1,0:T(8,128)(2,1)}, bf16[3,32,32,640]{3,2,1,0:T(8,128)(2,1)}, bf16[32,32,640]{2,1,0:T(8,128)(2,1)}, f32[80,2560]{1,0:...) custom-call(bf16[3,4,16,2560]{3,2,1,0:T(8,128)(2,1)} %bitcast.27, ...), custom_call_target="tpu_custom_call" | custom-call | flops 119460012032 | bytes 60000000 | tf_op jit(solution)/shard_map/block/pallas_call | solution.py:398
  211.3 0.1 all-gather.6.cloned.1.call-update
  211.3 0.1 all-gather.8.cloned.1.call-start
  211.4 0.7 all-gather.8.cloned.1.call-update
  212.2 0.1 all-gather.4.cloned.1.call-start
  212.2 0.7 all-gather.4.cloned.1.call-update
  212.9 182.0 %token_side.1 = (f32[32,80,2560]{2,1,0:T(8,128)}, bf16[2,32,32,640]{3,2,1,0:T(8,128)(2,1)}, bf16[192,2560]{1,0:T(8,128)(2,1)}, bf16[192,2560]{1,0:T(8,128)(2,1)}, f32[32,8,128]{2,1,0:T(8,128)}) custom-call(f32[80,2560]{1,0:T(8,128)} %get-tuple-element.21.own_ref, bf16[3,32,32,640]{3,2,1,0:T(8,128)(2,1)} %get-tuple-element.22.parts_ref, ...), custom_call_target="tpu_custom_call" | custom-call | flops 120000004096 | bytes 52428800 | tf_op jit(solution)/shard_map/token_side/pallas_call | solution.py:682
  395.0 0.9 slice.17
  395.9 1.2 slice_reduce_fusion
  397.1 0.7 reshape_squeeze.10
  397.8 0.7 reshape_squeeze.11
  398.5 0.7 reshape_squeeze.9
  399.1 0.6 copy.21
  399.8 3.8 hand_over.1
  403.5 17.9 %settle.5.refs_0_ = f32[32,80,2560]{2,1,0:T(8,128)} custom-call(f32[32,80,2560]{2,1,0:T(8,128)} %get-tuple-element.31.src_ref, bf16[192,2560]{1,0:T(8,128)(2,1)} %get-tuple-element.26.refs_0_), custom_call_target="tpu_custom_call" | custom-call | flops 10000000000 | bytes 52428800 | tf_op jit(solution)/shard_map/settle/pallas_call | solution.py:767
  421.4 0.0 all-gather.6.cloned.1.call-done
  421.4 17.9 %settle.6.after_ref.refs_0_ = f32[32,240,2560]{2,1,0:T(8,128)} custom-call(f32[32,80,2560]{2,1,0:T(8,128)} %bitcast.20, f32[32,80,2560]{2,1,0:T(8,128)} %settle.5.refs_0_), custom_call_target="tpu_custom_call" | custom-call | flops 10000000000 | bytes 52428800 | tf_op jit(solution)/shard_map/settle/pallas_call | solution.py:767
  439.4 87.9 %spread.1.refs_1_.src_ref = f32[32,56,2560]{2,1,0:T(8,128)} custom-call(f32[56,2560]{1,0:T(8,128)} %get-tuple-element.29.own_ref, f32[32,240,2560]{2,1,0:T(8,128)} %settle.6.after_ref.refs_0_), custom_call_target="tpu_custom_call" | custom-call | flops 49999998976 | bytes 36700160 | tf_op jit(solution)/shard_map/spread/pallas_call | solution.py:521
  527.3 0.0 all-gather.8.cloned.1.call-done
  527.3 17.9 %settle.7.refs_0_ = f32[32,240,2560]{2,1,0:T(8,128)} custom-call(f32[32,80,2560]{2,1,0:T(8,128)} %bitcast.19, f32[32,240,2560]{2,1,0:T(8,128)} %settle.6.after_ref.refs_0_, f32[32,56,2560]{2,1,0:T(8,128)} %spread.1.refs_1_.src_ref), custom_call_target="tpu_custom_call", output_to_operand_aliasing={{}: (1, {})} | custom-call | flops 10000000000 | bytes 52428800 | tf_op jit(solution)/shard_map/settle/pallas_call | solution.py:767
  545.2 13.2 %settle.8.refs_0_ = f32[32,240,2560]{2,1,0:T(8,128)} custom-call(f32[32,56,2560]{2,1,0:T(8,128)} %spread.1.refs_1_.src_ref, f32[32,240,2560]{2,1,0:T(8,128)} %settle.7.refs_0_), custom_call_target="tpu_custom_call", output_to_operand_aliasing={{}: (1, {})} | custom-call | flops 10000000000 | bytes 36700160 | tf_op jit(solution)/shard_map/settle/pallas_call | solution.py:767
  558.5 0.0 all-gather.4.cloned.1.call-done
  558.5 7.2 %settle.9 = f32[32,240,2560]{2,1,0:T(8,128)} custom-call(f32[32,24,2560]{2,1,0:T(8,128)} %bitcast.21, f32[32,240,2560]{2,1,0:T(8,128)} %settle.8.refs_0_), custom_call_target="tpu_custom_call", output_to_operand_aliasing={{}: (1, {})} | custom-call | flops 10000000000 | bytes 15728640 | tf_op jit(solution)/shard_map/settle/pallas_call | solution.py:767
Async XLA Ops:
  7.2 414.3 %all-gather.6.cloned.1.call-start = ((), (), s32[]{:S(2)}) async-start(), calls=%async_computation.1 | async-start | bytes 27033600 | tf_op jit(solution)/shard_map/all_gather | solution.py:791
  211.3 316.0 %all-gather.8.cloned.1.call-start = ((), (), s32[]{:S(2)}) async-start(), calls=%async_computation.2 | async-start | bytes 27033600 | tf_op jit(solution)/shard_map/all_gather | solution.py:791
  212.2 346.3 %all-gather.4.cloned.1.call-start = ((), (), s32[]{:S(2)}) async-start(), calls=%async_computation | async-start | bytes 8110080 | tf_op jit(solution)/shard_map/all_gather | solution.py:791
Sparse Core Ops, SparseCore 0:
  211.5 172.4 all-gather.5
  386.0 119.2 all-gather.7
  507.3 49.0 all-gather.3

commit v8 on v7

--- a/solution.py
+++ b/solution.py
@@ -103,7 +103,7 @@
 
 
 def block_kernel(size, dims, x_ref, dy_ref, gain_ref, shift_ref, pos_ref, keep_ref, wq_ref, bias_ref, wo_ref,
-                 gat_ref, parts_ref, partstok_ref, gwa_ref, gwb_ref, gwc_ref, gwd_ref, gwo_ref,
+                 gat_ref, parts_ref, partstok_ref, gwa_ref, gwb_ref, gwo_ref,
                  xin, stage, wbuf, wobuf, metatile, metabuf, rowbuf, sbuf, qkvb, dob, dk_acc, dv_acc, dq_all, o_all, d_all, pbuf,
                  load_sems, own_sems, piece_sems, parts_sem, ici_send, ici_recv, d2d_send, d2d_recv, own_send, own_recv,
                  meta_send, meta_recv, part_send, part_recv):
@@ -267,11 +267,11 @@
         def columns(n, carry):
             at = pl.ds(pl.multiple_of(n * width, width), width)
             term = dot(d, rows_of(p, 1, at), 0, 0)
-            row = 0
-            for ref in (gwa_ref, gwb_ref, gwc_ref, gwd_ref):
-                ref[:, at] += term[row:row + ref.shape[0]]
-                row += ref.shape[0]
-            gwo_ref[:, at] += dot(o, rows_of(p, 0, at), 0, 0)
+            row = gwa_ref.shape[0]
+            gwa_ref[:, at] += term[:row]
+            gwb_ref[:, at] += term[row:row + gwb_ref.shape[0]]
+            gwo_ref[:head_dim, at] += dot(o, rows_of(p, 0, at), 0, 0)
+            gwo_ref[head_dim:, at] += term[row + gwb_ref.shape[0]:]
             return carry
 
         lax.fori_loop(0, hidden // width, columns, 0)
@@ -291,7 +291,7 @@
     for i in range(count):
         tasks.setdefault((0, READY + spot[i]), []).append(lambda b, i=i: attend(b, i))
 
-    for ref in (gwa_ref, gwb_ref, gwc_ref, gwd_ref, gwo_ref):
+    for ref in (gwa_ref, gwb_ref, gwo_ref):
         ref[...] = jnp.zeros_like(ref)
 
     def phase_of(i, place):
@@ -376,9 +376,8 @@
 
 
 def split_rows(rows):
-    own, third = 8 * (rows // 34), 8 * max(1, rows // 80)
-    first = (rows - own - third) // 2
-    return first, first, third, own
+    first, own = 8 * (rows * 13 // 240), 8 * (rows // 80 or 1)
+    return first, rows - first - own, own
 
 
 def block_call(x, dy, gain, shift, pos, keep, wq, bias, wo, size, q_block, collective_id):
@@ -395,17 +394,17 @@
     bf16, f32 = jnp.bfloat16, jnp.float32
     flops = batch * (6 * seq_len * seq_len * 256 + 4 * seq_len * 4 * head_dim * hidden) + 80_000_000_000
     cut = (batch, COLOURS, rows, hidden)
+    first, second, own = split_rows(3 * head_dim)
     return pl.pallas_call(
         functools.partial(block_kernel, size, (batch, tok, head_dim, pad_dim, hidden, min(q_block, seq_len))),
         out_shape=(
             jax.ShapeDtypeStruct((batch, size, COLOURS, 2, rows, hidden), bf16),
             jax.ShapeDtypeStruct((batch, size, tok // 2, 8 * head_dim), bf16),
             jax.ShapeDtypeStruct((size, tok // 2, 8 * head_dim), bf16),
-            *(jax.ShapeDtypeStruct((n, hidden), f32) for n in split_rows(3 * head_dim)),
-            jax.ShapeDtypeStruct((head_dim, hidden), f32),
+            *(jax.ShapeDtypeStruct((n, hidden), f32) for n in (first, second, head_dim + own)),
         ),
         in_specs=[anywhere, anywhere, vmem, vmem, vmem, vmem, anywhere, vmem, anywhere],
-        out_specs=(anywhere, anywhere, anywhere, vmem, vmem, vmem, vmem, vmem),
+        out_specs=(anywhere, anywhere, anywhere, vmem, vmem, vmem),
         scratch_shapes=[
             pltpu.VMEM(cut, bf16),
             pltpu.VMEM((batch, COLOURS, 2, rows, hidden), bf16),
@@ -503,31 +502,6 @@
     def scratch(rows, cols, dtype):
         sem = pltpu.SemaphoreType.DMA
         return [pltpu.VMEM((rows, cols), dtype), sem, sem, sem((4,)), sem((4, PLACES)), sem((4,)), sem((4, PLACES)), sem, sem]
-
-
-def spread_kernel(size, own_ref, after_ref, gat_ref, stage, *sems):
-    spread = Spread(size, own_ref, gat_ref, stage, sems)
-    spread.load.start()
-    greet_all(spread.torus.me, size)
-    spread.load.wait()
-    for g in range(Spread.STEPS):
-        spread.step(g)
-    spread.close()
-
-
-def spread_rows(block, after, size, collective_id):
-    rows, cols = block.shape
-    anywhere = pl.BlockSpec(memory_space=pl.ANY)
-    return pl.pallas_call(
-        functools.partial(spread_kernel, size),
-        out_shape=jax.ShapeDtypeStruct((size, rows, cols), block.dtype),
-        in_specs=[anywhere, anywhere],
-        out_specs=anywhere,
-        scratch_shapes=Spread.scratch(rows, cols, block.dtype),
-        compiler_params=pltpu.CompilerParams(collective_id=collective_id, has_side_effects=True),
-        cost_estimate=pl.CostEstimate(flops=50_000_000_000, bytes_accessed=8 * size * rows * cols, transcendentals=0),
-        name="spread",
-    )(block, after)
 
 
 TOKEN_AT = 8
@@ -720,16 +694,15 @@
         cost_estimate=pl.CostEstimate(flops=1_000_000_000, bytes_accessed=8 * y.size, transcendentals=0), name="hand_over")(y, gx)
 
 
-def settle_kernel(block, depth, ahead, first, src_ref, *refs):
+def settle_kernel(block, depth, ahead, per, origin, first, src_ref, *refs):
     dst_ref, buf, read_sems, write_sems = refs[-4:]
-    per = src_ref.shape[1] // block
     count = src_ref.shape[0] * per
 
     def slab(ref, i, start):
         return ref.at[i // per, pl.ds(pl.multiple_of(start + lax.rem(i, per) * block, 8), block)]
 
     def read(i):
-        return pltpu.make_async_copy(slab(src_ref, i, 0), buf.at[lax.rem(i, depth)], read_sems.at[lax.rem(i, depth)])
+        return pltpu.make_async_copy(slab(src_ref, i, origin), buf.at[lax.rem(i, depth)], read_sems.at[lax.rem(i, depth)])
 
     def write(i):
         return pltpu.make_async_copy(buf.at[lax.rem(i, depth)], slab(dst_ref, i, first), write_sems.at[lax.rem(i, depth)])
@@ -759,13 +732,14 @@
     lax.fori_loop(max(0, count - depth), count, drain, 0)
 
 
-def settle(x, first, total, block, into=None, after=()):
+def settle(x, origin, rows, first, total, pieces=1, into=None, after=()):
+    block = rows // pieces
     depth, ahead = 12, 6
     count, _, cols = x.shape
     sem = pltpu.SemaphoreType.DMA((depth,))
     old = [] if into is None else [into]
     return pl.pallas_call(
-        functools.partial(settle_kernel, block, depth, ahead, first),
+        functools.partial(settle_kernel, block, depth, ahead, pieces, origin, first),
         out_shape=jax.ShapeDtypeStruct((count, total, cols), x.dtype),
         in_specs=[pl.BlockSpec(memory_space=pl.ANY)] * (1 + len(old) + len(after)),
         out_specs=pl.BlockSpec(memory_space=pl.ANY),
@@ -790,21 +764,19 @@
         def gather(a):
             return lax.all_gather(a, "sp", axis=0, tiled=True).reshape(heads, a.shape[0], hidden)
 
-        _, parts, early, grad_a, grad_b, grad_c, grad_d, grad_out = block_call(
+        _, parts, early, grad_a, grad_b, grad_out = block_call(
             x_blk, dy_blk, ln_gain, ln_bias, pos_blk, keep_blk, wq, jnp.transpose(b_qkv, (1, 0, 2)), wo, size, 256, 0)
 
         all_out, _, y, grad_x, totals = token_side(
             grad_out, parts, early, wq, wo, x_blk.reshape(tokens, hidden), dy_blk.reshape(tokens, hidden), ln_gain, b_out, size, 1)
         y, grad_x = hand_over(y, grad_x)
-        grad_wo = settle(all_out, 0, head_dim, head_dim, after=(y,))
+        grad_wo = settle(all_out, 0, head_dim, 0, head_dim, after=(y,))
 
         rows = 3 * head_dim
-        first, second, third, own = split_rows(rows)
-        grad_wq = settle(gather(grad_a), 0, rows, first, after=(grad_wo,))
-        all_d = spread_rows(grad_d, grad_wq, size, 2)
-        grad_wq = settle(gather(grad_b), first, rows, second, grad_wq, after=(all_d,))
-        grad_wq = settle(all_d, first + second + third, rows, own, grad_wq)
-        grad_wq = settle(gather(grad_c), first + second, rows, third, grad_wq)
+        first, second, own = split_rows(rows)
+        grad_wq = settle(all_out, head_dim, own, first + second, rows, after=(grad_wo,))
+        grad_wq = settle(gather(grad_a), 0, first, 0, rows, into=grad_wq)
+        grad_wq = settle(gather(grad_b), 0, second, first, rows, into=grad_wq)
         totals = totals[:, :, :head_dim]
         grad_wq = jnp.transpose(grad_wq.reshape(heads, 3, head_dim, hidden), (3, 0, 1, 2))
         return (y.reshape(x_blk.shape), grad_x.reshape(x_blk.shape), grad_wq, totals[:, 3:6],

time: 573 us -> 575 us (level)
  waiting for transfers between devices: 1.57 us -> 55.7 us
  Pallas kernels: 552 us -> 500 us
    pallas_call x6 -> x4, Pallas kernels: 162 us -> 72.7 us  [settle(): pl.pallas_call(functools.partial(settle_kernel, block, depth, ahead, piec...]
    all_gather x3 -> x2, waiting for transfers between devices: 0.06 us -> 54.9 us  [gather(): lax.all_gather(a, 'sp', axis=0, tiled=True)]
    pallas_call x1, Pallas kernels: 182 us -> 219 us  [token_side(): pl.pallas_call(functools.partial(token_kernel, size, head_dim, 16), out_s...]
  transfers between devices with their start and end apart: 3 -> 2, of which waited for: 0 -> 1; matrix products, arithmetic and copies ran while one was open for 1% -> 1% of each run, Pallas kernels for 60% -> 47%
where the time goes in v8:
time: 575 us; the launch traced here: 574 us
  Pallas kernels  500 us (87%)
  waiting for transfers between devices  55.7 us (10%)
  between operations  14.2 us (2%)
    pallas_call x1, Pallas kernels, token_side(): pl.pallas_call(functools.partial(token_kernel, size, head_dim, 16), out_s...  219 us
    pallas_call x1, Pallas kernels, block_call(): pl.pallas_call(functools.partial(block_kernel, size, (batch, tok, head_di...  204 us
    pallas_call x4, Pallas kernels, settle(): pl.pallas_call(functools.partial(settle_kernel, block, depth, ahead, piec...  72.7 us
    all_gather x2, waiting for transfers between devices, gather(): lax.all_gather(a, 'sp', axis=0, tiled=True)  54.9 us
  transfers between devices with their start and end apart: 2, of which 1 were waited for; matrix products, arithmetic and copies ran while one was open for 1% of the time, Pallas kernels for 47%

profile of v8, /device:TPU:97, one launch (start us, length us, event | category | flops | bytes accessed | tf_op | source)
XLA Modules:
  0.0 574.4 jit_solution(10786147139902555229)
XLA Ops:
  7.2 0.1 all-gather.5.cloned.1.call-start
  7.2 203.9 %block.1 = (bf16[3,32,4,2,16,2560]{5,4,3,2,1,0:T(8,128)(2,1)}, bf16[3,32,32,640]{3,2,1,0:T(8,128)(2,1)}, bf16[32,32,640]{2,1,0:T(8,128)(2,1)}, f32[104,2560]{1,0...) custom-call(bf16[3,4,16,2560]{3,2,1,0:T(8,128)(2,1)} %bitcast.25, bf16[3,4,16,2560]{3,2,1,0:T(8,128)(2,1)} %bitcast.27, ...), custom_call_target="tpu_custom_call" | custom-call | flops 119460012032 | bytes 60000000 | tf_op jit(solution)/shard_map/block/pallas_call | solution.py:398
  211.2 0.1 all-gather.5.cloned.1.call-update
  211.3 0.1 all-gather.3.cloned.1.call-start
  211.3 0.7 all-gather.3.cloned.1.call-update
  212.1 219.2 %token_side.1 = (f32[32,104,2560]{2,1,0:T(8,128)}, bf16[2,32,32,640]{3,2,1,0:T(8,128)(2,1)}, bf16[192,2560]{1,0:T(8,128)(2,1)}, bf16[192,2560]{1,0:T(8,128)(2,1)}, f32[32,8,128]{2,1,0:T(8,128)}) custom-call(f32[104,2560]{1,0:T(8,128)} %get-tuple-element.19.own_ref, bf16[3,32,32,640]{3,2,1,0:T(8,128)(2,1)} %get-tuple-element.20.parts_ref, ...), custom_call_target="tpu_custom_call" | custom-call | flops 120000004096 | bytes 68157440 | tf_op jit(solution)/shard_map/token_side/pallas_call | solution.py:656
  431.3 0.9 slice.17
  432.2 1.2 slice_reduce_fusion
  433.4 0.7 reshape_squeeze.10
  434.1 0.7 reshape_squeeze.11
  434.7 0.7 reshape_squeeze.9
  435.4 0.6 copy.20
  436.0 3.8 hand_over.1
  439.8 17.9 %settle.4.refs_0_ = f32[32,80,2560]{2,1,0:T(8,128)} custom-call(f32[32,104,2560]{2,1,0:T(8,128)} %get-tuple-element.28.src_ref, bf16[192,2560]{1,0:T(8,128)(2,1)} %get-tuple-element.24.refs_0_), custom_call_target="tpu_custom_call" | custom-call | flops 10000000000 | bytes 68157440 | tf_op jit(solution)/shard_map/settle/pallas_call | solution.py:741
  457.7 7.2 %settle.5.refs_0_ = f32[32,240,2560]{2,1,0:T(8,128)} custom-call(f32[32,104,2560]{2,1,0:T(8,128)} %get-tuple-element.28.src_ref, f32[32,80,2560]{2,1,0:T(8,128)} %settle.4.refs_0_), custom_call_target="tpu_custom_call" | custom-call | flops 10000000000 | bytes 68157440 | tf_op jit(solution)/shard_map/settle/pallas_call | solution.py:741
  464.9 0.0 all-gather.5.cloned.1.call-done
  464.9 22.8 %settle.6.refs_0_ = f32[32,240,2560]{2,1,0:T(8,128)} custom-call(f32[32,104,2560]{2,1,0:T(8,128)} %bitcast.19, f32[32,240,2560]{2,1,0:T(8,128)} %settle.5.refs_0_), custom_call_target="tpu_custom_call", output_to_operand_aliasing={{}: (1, {})} | custom-call | flops 10000000000 | bytes 68157440 | tf_op jit(solution)/shard_map/settle/pallas_call | solution.py:741
  487.8 54.9 %all-gather.3.cloned.1.call-done = f32[3584,2560]{1,0:T(8,128)} async-done(((f32[112,2560]{1,0:T(8,128)}), f32[3584,2560]{1,0:T(8,128)}) %all-gather.3.cloned.1.call-update) | async-done | bytes 36700176 | tf_op jit(solution)/shard_map/all_gather | solution.py:765
  542.7 24.9 %settle.7 = f32[32,240,2560]{2,1,0:T(8,128)} custom-call(f32[32,112,2560]{2,1,0:T(8,128)} %bitcast.18, f32[32,240,2560]{2,1,0:T(8,128)} %settle.6.refs_0_), custom_call_target="tpu_custom_call", output_to_operand_aliasing={{}: (1, {})} | custom-call | flops 10000000000 | bytes 73400320 | tf_op jit(solution)/shard_map/settle/pallas_call | solution.py:741
Async XLA Ops:
  7.2 457.8 %all-gather.5.cloned.1.call-start = ((), (), s32[]{:S(2)}) async-start(), calls=%async_computation.1 | async-start | bytes 35143680 | tf_op jit(solution)/shard_map/all_gather | solution.py:765
  211.3 331.4 %all-gather.3.cloned.1.call-start = ((), (), s32[]{:S(2)}) async-start(), calls=%async_computation | async-start | bytes 37847040 | tf_op jit(solution)/shard_map/all_gather | solution.py:765
Sparse Core Ops, SparseCore 0:
  211.4 212.7 all-gather.4
  426.3 116.3 all-gather.2

commit v9 on v7

--- a/solution.py
+++ b/solution.py
@@ -66,6 +66,7 @@
 LAG = 3
 COLOURS = 4
 READY = 6
+EARLY = 2
 STEP_OF = ((1, 0), (-1, 0), (0, 1), (0, -1))
 PLACES = len(CYCLE)
 
@@ -103,7 +104,7 @@
 
 
 def block_kernel(size, dims, x_ref, dy_ref, gain_ref, shift_ref, pos_ref, keep_ref, wq_ref, bias_ref, wo_ref,
-                 gat_ref, parts_ref, partstok_ref, gwa_ref, gwb_ref, gwc_ref, gwd_ref, gwo_ref,
+                 gat_ref, parts_ref, partstok_ref, gwa_ref, gwb_ref, gwc_ref, gwo_ref,
                  xin, stage, wbuf, wobuf, metatile, metabuf, rowbuf, sbuf, qkvb, dob, dk_acc, dv_acc, dq_all, o_all, d_all, pbuf,
                  load_sems, own_sems, piece_sems, parts_sem, ici_send, ici_recv, d2d_send, d2d_recv, own_send, own_recv,
                  meta_send, meta_recv, part_send, part_recv):
@@ -153,8 +154,10 @@
     for load in (load_x, load_dy, load_wq, load_wo):
         load.start()
     meta = Direct(me, size, lambda j: metatile, lambda j: metabuf.at[j], metabuf, meta_send, meta_recv)
-    trade = Direct(me, size, lambda j: parts_ref.at[0, j], lambda j: partstok_ref.at[j], partstok_ref, part_send, part_recv)
-    own_parts = pltpu.make_async_copy(parts_ref.at[0, me], partstok_ref.at[me], load_sems.at[4])
+    early = partstok_ref.shape[0]
+    trades = [Direct(me, size, lambda j, b=b: parts_ref.at[b, j], lambda j, b=b: partstok_ref.at[b, j], partstok_ref.at[b],
+                     part_send.at[b], part_recv.at[b]) for b in range(early)]
+    own_parts = [pltpu.make_async_copy(parts_ref.at[b, me], partstok_ref.at[b, me], load_sems.at[4 + b]) for b in range(early)]
 
     def prepare():
         metatile[...] = jnp.zeros_like(metatile)
@@ -268,10 +271,11 @@
             at = pl.ds(pl.multiple_of(n * width, width), width)
             term = dot(d, rows_of(p, 1, at), 0, 0)
             row = 0
-            for ref in (gwa_ref, gwb_ref, gwc_ref, gwd_ref):
+            for ref in (gwa_ref, gwb_ref, gwc_ref):
                 ref[:, at] += term[row:row + ref.shape[0]]
                 row += ref.shape[0]
-            gwo_ref[:, at] += dot(o, rows_of(p, 0, at), 0, 0)
+            gwo_ref[:head_dim, at] += dot(o, rows_of(p, 0, at), 0, 0)
+            gwo_ref[head_dim:, at] += term[row:]
             return carry
 
         lax.fori_loop(0, hidden // width, columns, 0)
@@ -291,7 +295,7 @@
     for i in range(count):
         tasks.setdefault((0, READY + spot[i]), []).append(lambda b, i=i: attend(b, i))
 
-    for ref in (gwa_ref, gwb_ref, gwc_ref, gwd_ref, gwo_ref):
+    for ref in (gwa_ref, gwb_ref, gwc_ref, gwo_ref):
         ref[...] = jnp.zeros_like(ref)
 
     def phase_of(i, place):
@@ -352,8 +356,8 @@
             if place == READY:
                 @pl.when(i == batch)
                 def _():
-                    own_parts.start()
-                    trade.start()
+                    for copy in own_parts + trades:
+                        copy.start()
 
             for later in (0, 1):
                 if (later, place) in tasks:
@@ -364,9 +368,11 @@
         return carry
 
     lax.fori_loop(0, batch + 2, turn, 0)
-    own_parts.wait()
-    trade.wait_recv()
-    trade.wait_send()
+    for copy in own_parts:
+        copy.wait()
+    for trade in trades:
+        trade.wait_recv()
+        trade.wait_send()
     sent = gat_ref.at[:, pl.ds(0, places), 0]
     for link in range(4):
         for sem in (ici_send, d2d_send):
@@ -376,9 +382,8 @@
 
 
 def split_rows(rows):
-    own, third = 8 * (rows // 34), 8 * max(1, rows // 80)
-    first = (rows - own - third) // 2
-    return first, first, third, own
+    first, short, own = 8 * (rows * 16 // 240), 8 * (rows // 80 or 1), 8 * (rows // 60 or 1)
+    return first, rows - first - short - own, short, own
 
 
 def block_call(x, dy, gain, shift, pos, keep, wq, bias, wo, size, q_block, collective_id):
@@ -395,17 +400,17 @@
     bf16, f32 = jnp.bfloat16, jnp.float32
     flops = batch * (6 * seq_len * seq_len * 256 + 4 * seq_len * 4 * head_dim * hidden) + 80_000_000_000
     cut = (batch, COLOURS, rows, hidden)
+    first, second, short, own = split_rows(3 * head_dim)
     return pl.pallas_call(
         functools.partial(block_kernel, size, (batch, tok, head_dim, pad_dim, hidden, min(q_block, seq_len))),
         out_shape=(
             jax.ShapeDtypeStruct((batch, size, COLOURS, 2, rows, hidden), bf16),
             jax.ShapeDtypeStruct((batch, size, tok // 2, 8 * head_dim), bf16),
-            jax.ShapeDtypeStruct((size, tok // 2, 8 * head_dim), bf16),
-            *(jax.ShapeDtypeStruct((n, hidden), f32) for n in split_rows(3 * head_dim)),
-            jax.ShapeDtypeStruct((head_dim, hidden), f32),
+            jax.ShapeDtypeStruct((EARLY, size, tok // 2, 8 * head_dim), bf16),
+            *(jax.ShapeDtypeStruct((n, hidden), f32) for n in (first, second, short, head_dim + own)),
         ),
         in_specs=[anywhere, anywhere, vmem, vmem, vmem, vmem, anywhere, vmem, anywhere],
-        out_specs=(anywhere, anywhere, anywhere, vmem, vmem, vmem, vmem, vmem),
+        out_specs=(anywhere, anywhere, anywhere, vmem, vmem, vmem, vmem),
         scratch_shapes=[
             pltpu.VMEM(cut, bf16),
             pltpu.VMEM((batch, COLOURS, 2, rows, hidden), bf16),
@@ -423,8 +428,8 @@
             pltpu.VMEM((seq_len, pad_dim), bf16),
             pltpu.VMEM((seq_len, 3 * head_dim), bf16),
             pltpu.VMEM((size, tok // 2, 8 * head_dim), bf16),
-            sem((5,)), sem((batch,)), sem((side, side)), sem,
-            sem((4,)), sem((4, places)), sem((4,)), sem((4, places)), sem((batch,)), sem((batch,)), sem, sem, sem, sem,
+            sem((4 + EARLY,)), sem((batch,)), sem((side, side)), sem,
+            sem((4,)), sem((4, places)), sem((4,)), sem((4, places)), sem((batch,)), sem((batch,)), sem, sem, sem((EARLY,)), sem((EARLY,)),
         ],
         compiler_params=pltpu.CompilerParams(collective_id=collective_id, has_side_effects=True, vmem_limit_bytes=VMEM_LIMIT),
         cost_estimate=pl.CostEstimate(flops=flops, bytes_accessed=60_000_000, transcendentals=batch * seq_len * seq_len // 2),
@@ -542,7 +547,7 @@
     spread = Spread(size, own_ref, gat_ref, stage,
                     (load_sem, keep_sem, ici_send, ici_recv, d2d_send, d2d_recv, own_send, own_recv))
     me = spread.torus.me
-    late = late_ref.shape[0]
+    early, late = early_ref.shape[0], late_ref.shape[0]
     heads, hidden = wq_ref.shape[0], wq_ref.shape[2]
     per = heads // TOKEN_STEPS
     trades, own_parts = [], []
@@ -561,8 +566,8 @@
 
     def rows(m):
         at, slot = pl.ds(m * per, per), m % 2
-        return [pltpu.make_async_copy(early_ref.at[at], pbuf.at[slot, 0], p_sems.at[slot, 0])] + [
-            pltpu.make_async_copy(late_ref.at[n, at], pbuf.at[slot, 1 + n], p_sems.at[slot, 1 + n]) for n in range(late)]
+        sources = [early_ref.at[n, at] for n in range(early)] + [late_ref.at[n, at] for n in range(late)]
+        return [pltpu.make_async_copy(src, pbuf.at[slot, n], p_sems.at[slot, n]) for n, src in enumerate(sources)]
 
     spread.load.start()
     for copy in weights(0):
@@ -585,7 +590,7 @@
             ds, os = [], []
             for h in range(2):
                 parts = []
-                for n in range(1 + late):
+                for n in range(early + late):
                     both = pbuf[slot, n, i * 2 + h]
                     parts += [both[:, :4 * head_dim], both[:, 4 * head_dim:]]
                 parts = jnp.concatenate(parts, axis=0)
@@ -671,7 +676,7 @@
 
 def token_side(block, parts, early, wq, wo, x, dy, gain, bout, size, collective_id):
     rows, cols = block.shape
-    late = parts.shape[0] - 1
+    late = parts.shape[0] - early.shape[0]
     heads, head_dim, hidden = wo.shape
     tokens = x.shape[0]
     per = heads // TOKEN_STEPS
@@ -693,14 +698,14 @@
         scratch_shapes=Spread.scratch(rows, cols, block.dtype) + [
             pltpu.VMEM((2, per, 3 * head_dim, hidden), bf16),
             pltpu.VMEM((2, per, head_dim, hidden), bf16),
-            pltpu.VMEM((2, 1 + late, per, *parts.shape[2:]), bf16),
+            pltpu.VMEM((2, parts.shape[0], per, *parts.shape[2:]), bf16),
             pltpu.VMEM((tokens, hidden), f32),
             pltpu.VMEM((tokens, hidden), f32),
             pltpu.VMEM((8, hidden), f32),
             pltpu.VMEM((size, 8, LANES), f32),
             pltpu.VMEM((size, 8, LANES), f32),
             pltpu.VMEM((8, LANES), f32),
-            sem((late,)), sem((late,)), sem((late,)), sem((2,)), sem((2,)), sem((2, 1 + late)), sem, sem, sem, sem,
+            sem((late,)), sem((late,)), sem((late,)), sem((2,)), sem((2,)), sem((2, parts.shape[0])), sem, sem, sem, sem,
         ],
         compiler_params=pltpu.CompilerParams(collective_id=collective_id, has_side_effects=True, vmem_limit_bytes=VMEM_LIMIT),
         cost_estimate=pl.CostEstimate(flops=120_000_000_000, bytes_accessed=8 * size * rows * cols, transcendentals=0),
@@ -720,16 +725,15 @@
         cost_estimate=pl.CostEstimate(flops=1_000_000_000, bytes_accessed=8 * y.size, transcendentals=0), name="hand_over")(y, gx)
 
 
-def settle_kernel(block, depth, ahead, first, src_ref, *refs):
+def settle_kernel(block, depth, ahead, per, origin, first, src_ref, *refs):
     dst_ref, buf, read_sems, write_sems = refs[-4:]
-    per = src_ref.shape[1] // block
     count = src_ref.shape[0] * per
 
     def slab(ref, i, start):
         return ref.at[i // per, pl.ds(pl.multiple_of(start + lax.rem(i, per) * block, 8), block)]
 
     def read(i):
-        return pltpu.make_async_copy(slab(src_ref, i, 0), buf.at[lax.rem(i, depth)], read_sems.at[lax.rem(i, depth)])
+        return pltpu.make_async_copy(slab(src_ref, i, origin), buf.at[lax.rem(i, depth)], read_sems.at[lax.rem(i, depth)])
 
     def write(i):
         return pltpu.make_async_copy(buf.at[lax.rem(i, depth)], slab(dst_ref, i, first), write_sems.at[lax.rem(i, depth)])
@@ -759,13 +763,14 @@
     lax.fori_loop(max(0, count - depth), count, drain, 0)
 
 
-def settle(x, first, total, block, into=None, after=()):
+def settle(x, origin, rows, first, total, pieces=1, into=None, after=()):
+    block = rows // pieces
     depth, ahead = 12, 6
     count, _, cols = x.shape
     sem = pltpu.SemaphoreType.DMA((depth,))
     old = [] if into is None else [into]
     return pl.pallas_call(
-        functools.partial(settle_kernel, block, depth, ahead, first),
+        functools.partial(settle_kernel, block, depth, ahead, pieces, origin, first),
         out_shape=jax.ShapeDtypeStruct((count, total, cols), x.dtype),
         in_specs=[pl.BlockSpec(memory_space=pl.ANY)] * (1 + len(old) + len(after)),
         out_specs=pl.BlockSpec(memory_space=pl.ANY),
@@ -790,21 +795,22 @@
         def gather(a):
             return lax.all_gather(a, "sp", axis=0, tiled=True).reshape(heads, a.shape[0], hidden)
 
-        _, parts, early, grad_a, grad_b, grad_c, grad_d, grad_out = block_call(
+        _, parts, early, grad_a, grad_b, grad_c, grad_out = block_call(
             x_blk, dy_blk, ln_gain, ln_bias, pos_blk, keep_blk, wq, jnp.transpose(b_qkv, (1, 0, 2)), wo, size, 256, 0)
 
         all_out, _, y, grad_x, totals = token_side(
             grad_out, parts, early, wq, wo, x_blk.reshape(tokens, hidden), dy_blk.reshape(tokens, hidden), ln_gain, b_out, size, 1)
         y, grad_x = hand_over(y, grad_x)
-        grad_wo = settle(all_out, 0, head_dim, head_dim, after=(y,))
+        grad_wo = settle(all_out, 0, head_dim, 0, head_dim, after=(y,))
 
         rows = 3 * head_dim
-        first, second, third, own = split_rows(rows)
-        grad_wq = settle(gather(grad_a), 0, rows, first, after=(grad_wo,))
-        all_d = spread_rows(grad_d, grad_wq, size, 2)
-        grad_wq = settle(gather(grad_b), first, rows, second, grad_wq, after=(all_d,))
-        grad_wq = settle(all_d, first + second + third, rows, own, grad_wq)
-        grad_wq = settle(gather(grad_c), first + second, rows, third, grad_wq)
+        first, second, short, own = split_rows(rows)
+        grad_wq = settle(all_out, head_dim, own, first + second + short, rows, after=(grad_wo,))
+        all_a = gather(grad_a)
+        all_c = spread_rows(grad_c, all_a, size, 2)
+        grad_wq = settle(all_a, 0, first, 0, rows, into=grad_wq, after=(all_c,))
+        grad_wq = settle(all_c, 0, short, first + second, rows, into=grad_wq)
+        grad_wq = settle(gather(grad_b), 0, second, first, rows, into=grad_wq)
         totals = totals[:, :, :head_dim]
         grad_wq = jnp.transpose(grad_wq.reshape(heads, 3, head_dim, hidden), (3, 0, 1, 2))
         return (y.reshape(x_blk.shape), grad_x.reshape(x_blk.shape), grad_wq, totals[:, 3:6],

time: 573 us -> 578 us (level)
  Pallas kernels: 552 us -> 558 us
    pallas_call x1, Pallas kernels: 87.9 us -> 50.1 us  [spread_rows(): pl.pallas_call(functools.partial(spread_kernel, size), out_shape=jax.Shap...]
    pallas_call x1, Pallas kernels: 182 us -> 212 us  [token_side(): pl.pallas_call(functools.partial(token_kernel, size, head_dim, 16), out_s...]
    pallas_call x1, Pallas kernels: 204 us -> 217 us  [block_call(): pl.pallas_call(functools.partial(block_kernel, size, (batch, tok, head_di...]
  transfers between devices with their start and end apart: 3 -> 2, of which waited for: 0 -> 0; matrix products, arithmetic and copies ran while one was open for 1% -> 1% of each run, Pallas kernels for 60% -> 57%
where the time goes in v9:
time: 578 us
  Pallas kernels  558 us (97%)
  between operations  14.2 us (2%)
    pallas_call x1, Pallas kernels, block_call(): pl.pallas_call(functools.partial(block_kernel, size, (batch, tok, head_di...  217 us
    pallas_call x1, Pallas kernels, token_side(): pl.pallas_call(functools.partial(token_kernel, size, head_dim, 16), out_s...  212 us
    pallas_call x5, Pallas kernels, settle(): pl.pallas_call(functools.partial(settle_kernel, block, depth, ahead, piec...  74.7 us
    pallas_call x1, Pallas kernels, spread_rows(): pl.pallas_call(functools.partial(spread_kernel, size), out_shape=jax.Shap...  50.1 us
  transfers between devices with their start and end apart: 2, of which 0 were waited for; matrix products, arithmetic and copies ran while one was open for 1% of the time, Pallas kernels for 57%

profile of v9, /device:TPU:97, one launch (start us, length us, event | category | flops | bytes accessed | tf_op | source)
XLA Modules:
  0.0 577.6 jit_solution(3470619406564708605)
XLA Ops:
  7.2 0.1 all-gather.5.cloned.1.call-start
  7.2 216.8 %block.1 = (bf16[3,32,4,2,16,2560]{5,4,3,2,1,0:T(8,128)(2,1)}, bf16[3,32,32,640]{3,2,1,0:T(8,128)(2,1)}, bf16[2,32,32,640]{3,2,1,0:T(8,128)(2,1)}, f32[128,2560]...) custom-call(bf16[3,4,16,2560]{3,2,1,0:T(8,128)(2,1)} %bitcast.26, ...), custom_call_target="tpu_custom_call" | custom-call | flops 119460012032 | bytes 60000000 | tf_op jit(solution)/shard_map/block/pallas_call | solution.py:404
  224.0 0.1 all-gather.5.cloned.1.call-update
  224.1 0.1 all-gather.3.cloned.1.call-start
  224.1 0.7 all-gather.3.cloned.1.call-update
  224.9 212.4 %token_side.1 = (f32[32,112,2560]{2,1,0:T(8,128)}, bf16[1,32,32,640]{3,2,1,0:T(8,128)(2,1)}, bf16[192,2560]{1,0:T(8,128)(2,1)}, bf16[192,2560]{1,0:T(8,128)(2,1)}, f32[32,8,128]{2,1,0:T(8,128)}) custom-call(f32[112,2560]{1,0:T(8,128)} %get-tuple-element.20.own_ref, bf16[3,32,32,640]{3,2,1,0:T(8,128)(2,1)} %get-tuple-element.21.parts_ref, ...), custom_call_target="tpu_custom_call" | custom-call | flops 120000004096 | bytes 73400320 | tf_op jit(solution)/shard_map/token_side/pallas_call | solution.py:687
  437.3 0.9 slice.17
  438.2 1.2 slice_reduce_fusion
  439.4 0.7 reshape_squeeze.10
  440.1 0.7 reshape_squeeze.11
  440.8 0.7 reshape_squeeze.9
  441.4 0.6 copy.21
  442.1 3.8 hand_over.1
  445.9 17.9 %settle.5.refs_0_ = f32[32,80,2560]{2,1,0:T(8,128)} custom-call(f32[32,112,2560]{2,1,0:T(8,128)} %get-tuple-element.30.src_ref, bf16[192,2560]{1,0:T(8,128)(2,1)} %get-tuple-element.25.refs_0_), custom_call_target="tpu_custom_call" | custom-call | flops 10000000000 | bytes 73400320 | tf_op jit(solution)/shard_map/settle/pallas_call | solution.py:772
  463.7 8.5 %settle.6.refs_0_ = f32[32,240,2560]{2,1,0:T(8,128)} custom-call(f32[32,112,2560]{2,1,0:T(8,128)} %get-tuple-element.30.src_ref, f32[32,80,2560]{2,1,0:T(8,128)} %settle.5.refs_0_), custom_call_target="tpu_custom_call" | custom-call | flops 10000000000 | bytes 73400320 | tf_op jit(solution)/shard_map/settle/pallas_call | solution.py:772
  472.2 0.0 all-gather.5.cloned.1.call-done
  472.2 50.1 %spread.1.refs_1_.src_ref = f32[32,24,2560]{2,1,0:T(8,128)} custom-call(f32[24,2560]{1,0:T(8,128)} %get-tuple-element.28.own_ref, f32[32,128,2560]{2,1,0:T(8,128)} %bitcast.18), custom_call_target="tpu_custom_call" | custom-call | flops 49999998976 | bytes 15728640 | tf_op jit(solution)/shard_map/spread/pallas_call | solution.py:526
  522.3 27.9 %settle.7.refs_0_ = f32[32,240,2560]{2,1,0:T(8,128)} custom-call(f32[32,128,2560]{2,1,0:T(8,128)} %bitcast.19, f32[32,240,2560]{2,1,0:T(8,128)} %settle.6.refs_0_, f32[32,24,2560]{2,1,0:T(8,128)} %spread.1.refs_1_.src_ref), custom_call_target="tpu_custom_call", output_to_operand_aliasing={{}: (1, {})} | custom-call | flops 10000000000 | bytes 83886080 | tf_op jit(solution)/shard_map/settle/pallas_call | solution.py:772
  550.2 7.2 %settle.8.refs_0_ = f32[32,240,2560]{2,1,0:T(8,128)} custom-call(f32[32,24,2560]{2,1,0:T(8,128)} %spread.1.refs_1_.src_ref, f32[32,240,2560]{2,1,0:T(8,128)} %settle.7.refs_0_), custom_call_target="tpu_custom_call", output_to_operand_aliasing={{}: (1, {})} | custom-call | flops 10000000000 | bytes 15728640 | tf_op jit(solution)/shard_map/settle/pallas_call | solution.py:772
  557.5 0.0 all-gather.3.cloned.1.call-done
  557.5 13.3 %settle.9 = f32[32,240,2560]{2,1,0:T(8,128)} custom-call(f32[32,56,2560]{2,1,0:T(8,128)} %bitcast.20, f32[32,240,2560]{2,1,0:T(8,128)} %settle.8.refs_0_), custom_call_target="tpu_custom_call", output_to_operand_aliasing={{}: (1, {})} | custom-call | flops 10000000000 | bytes 36700160 | tf_op jit(solution)/shard_map/settle/pallas_call | solution.py:772
Async XLA Ops:
  7.2 465.0 %all-gather.5.cloned.1.call-start = ((), (), s32[]{:S(2)}) async-start(), calls=%async_computation.1 | async-start | bytes 43253760 | tf_op jit(solution)/shard_map/all_gather | solution.py:796
  224.1 333.4 %all-gather.3.cloned.1.call-start = ((), (), s32[]{:S(2)}) async-start(), calls=%async_computation | async-start | bytes 18923520 | tf_op jit(solution)/shard_map/all_gather | solution.py:796
Sparse Core Ops, SparseCore 0:
  224.2 226.6 all-gather.4
  453.0 85.8 all-gather.2

commit v10 on v9

--- a/solution.py
+++ b/solution.py
@@ -66,7 +66,7 @@
 LAG = 3
 COLOURS = 4
 READY = 6
-EARLY = 2
+EARLY = 1
 STEP_OF = ((1, 0), (-1, 0), (0, 1), (0, -1))
 PLACES = len(CYCLE)
 
@@ -274,8 +274,7 @@
             for ref in (gwa_ref, gwb_ref, gwc_ref):
                 ref[:, at] += term[row:row + ref.shape[0]]
                 row += ref.shape[0]
-            gwo_ref[:head_dim, at] += dot(o, rows_of(p, 0, at), 0, 0)
-            gwo_ref[head_dim:, at] += term[row:]
+            gwo_ref[:, at] += dot(o, rows_of(p, 0, at), 0, 0)
             return carry
 
         lax.fori_loop(0, hidden // width, columns, 0)
@@ -382,8 +381,8 @@
 
 
 def split_rows(rows):
-    first, short, own = 8 * (rows * 16 // 240), 8 * (rows // 80 or 1), 8 * (rows // 60 or 1)
-    return first, rows - first - short - own, short, own
+    first, short = 8 * (rows * 20 // 240), 8 * (rows // 60 or 1)
+    return first, rows - first - short, short
 
 
 def block_call(x, dy, gain, shift, pos, keep, wq, bias, wo, size, q_block, collective_id):
@@ -400,14 +399,14 @@
     bf16, f32 = jnp.bfloat16, jnp.float32
     flops = batch * (6 * seq_len * seq_len * 256 + 4 * seq_len * 4 * head_dim * hidden) + 80_000_000_000
     cut = (batch, COLOURS, rows, hidden)
-    first, second, short, own = split_rows(3 * head_dim)
+    first, second, short = split_rows(3 * head_dim)
     return pl.pallas_call(
         functools.partial(block_kernel, size, (batch, tok, head_dim, pad_dim, hidden, min(q_block, seq_len))),
         out_shape=(
             jax.ShapeDtypeStruct((batch, size, COLOURS, 2, rows, hidden), bf16),
             jax.ShapeDtypeStruct((batch, size, tok // 2, 8 * head_dim), bf16),
             jax.ShapeDtypeStruct((EARLY, size, tok // 2, 8 * head_dim), bf16),
-            *(jax.ShapeDtypeStruct((n, hidden), f32) for n in (first, second, short, head_dim + own)),
+            *(jax.ShapeDtypeStruct((n, hidden), f32) for n in (first, second, short, head_dim)),
         ),
         in_specs=[anywhere, anywhere, vmem, vmem, vmem, vmem, anywhere, vmem, anywhere],
         out_specs=(anywhere, anywhere, anywhere, vmem, vmem, vmem, vmem),
@@ -804,11 +803,9 @@
         grad_wo = settle(all_out, 0, head_dim, 0, head_dim, after=(y,))
 
         rows = 3 * head_dim
-        first, second, short, own = split_rows(rows)
-        grad_wq = settle(all_out, head_dim, own, first + second + short, rows, after=(grad_wo,))
-        all_a = gather(grad_a)
-        all_c = spread_rows(grad_c, all_a, size, 2)
-        grad_wq = settle(all_a, 0, first, 0, rows, into=grad_wq, after=(all_c,))
+        first, second, short = split_rows(rows)
+        all_c = spread_rows(grad_c, grad_wo, size, 2)
+        grad_wq = settle(gather(grad_a), 0, first, 0, rows, 2, after=(all_c,))
         grad_wq = settle(all_c, 0, short, first + second, rows, into=grad_wq)
         grad_wq = settle(gather(grad_b), 0, second, first, rows, into=grad_wq)
         totals = totals[:, :, :head_dim]

time: 578 us -> 562 us (0.972)
  Pallas kernels: 558 us -> 519 us
  waiting for transfers between devices: 0.83 us -> 23.5 us
    pallas_call x1, Pallas kernels: 212 us -> 175 us  [token_side(): pl.pallas_call(functools.partial(token_kernel, size, head_dim, 16), out_s...]
    all_gather x2, waiting for transfers between devices: 0.04 us -> 22.8 us  [gather(): lax.all_gather(a, 'sp', axis=0, tiled=True)]
    pallas_call x1, Pallas kernels: 50.1 us -> 64.3 us  [spread_rows(): pl.pallas_call(functools.partial(spread_kernel, size), out_shape=jax.Shap...]
    pallas_call x1, Pallas kernels: 217 us -> 204 us  [block_call(): pl.pallas_call(functools.partial(block_kernel, size, (batch, tok, head_di...]
    pallas_call x5 -> x4, Pallas kernels: 74.7 us -> 71.6 us  [settle(): pl.pallas_call(functools.partial(settle_kernel, block, depth, ahead, piec...]
  transfers between devices with their start and end apart: 2 -> 2, of which waited for: 0 -> 2; matrix products, arithmetic and copies ran while one was open for 1% -> 1% of each run, Pallas kernels for 57% -> 54%
where the time goes in v10:
time: 562 us; the launch traced here: 561 us
  Pallas kernels  519 us (92%)
  waiting for transfers between devices  23.5 us (4%)
  between operations  14.2 us (3%)
    pallas_call x1, Pallas kernels, block_call(): pl.pallas_call(functools.partial(block_kernel, size, (batch, tok, head_di...  204 us
    pallas_call x1, Pallas kernels, token_side(): pl.pallas_call(functools.partial(token_kernel, size, head_dim, 16), out_s...  175 us
    pallas_call x4, Pallas kernels, settle(): pl.pallas_call(functools.partial(settle_kernel, block, depth, ahead, piec...  71.6 us
    pallas_call x1, Pallas kernels, spread_rows(): pl.pallas_call(functools.partial(spread_kernel, size), out_shape=jax.Shap...  64.3 us
    all_gather x2, waiting for transfers between devices, gather(): lax.all_gather(a, 'sp', axis=0, tiled=True)  22.8 us
  transfers between devices with their start and end apart: 2, of which 2 were waited for; matrix products, arithmetic and copies ran while one was open for 1% of the time, Pallas kernels for 54%

profile of v10, /device:TPU:97, one launch (start us, length us, event | category | flops | bytes accessed | tf_op | source)
XLA Modules:
  0.0 561.2 jit_solution(5112639698128678646)
XLA Ops:
  7.2 0.1 all-gather.5.cloned.1.call-start
  7.2 203.9 %block.1 = (bf16[3,32,4,2,16,2560]{5,4,3,2,1,0:T(8,128)(2,1)}, bf16[3,32,32,640]{3,2,1,0:T(8,128)(2,1)}, bf16[1,32,32,640]{3,2,1,0:T(8,128)(2,1)}, f32[160,2560]...) custom-call(bf16[3,4,16,2560]{3,2,1,0:T(8,128)(2,1)} %bitcast.25, ...), custom_call_target="tpu_custom_call" | custom-call | flops 119460012032 | bytes 60000000 | tf_op jit(solution)/shard_map/block/pallas_call | solution.py:403
  211.2 0.1 all-gather.5.cloned.1.call-update
  211.2 0.1 all-gather.3.cloned.1.call-start
  211.3 0.7 all-gather.3.cloned.1.call-update
  212.0 175.0 %token_side.1 = (f32[32,80,2560]{2,1,0:T(8,128)}, bf16[2,32,32,640]{3,2,1,0:T(8,128)(2,1)}, bf16[192,2560]{1,0:T(8,128)(2,1)}, bf16[192,2560]{1,0:T(8,128)(2,1)}, f32[32,8,128]{2,1,0:T(8,128)}) custom-call(f32[80,2560]{1,0:T(8,128)} %get-tuple-element.20.own_ref, bf16[3,32,32,640]{3,2,1,0:T(8,128)(2,1)} %get-tuple-element.21.parts_ref, ...), custom_call_target="tpu_custom_call" | custom-call | flops 120000004096 | bytes 52428800 | tf_op jit(solution)/shard_map/token_side/pallas_call | solution.py:686
  387.0 0.9 slice.17
  387.9 1.2 slice_reduce_fusion
  389.1 0.7 reshape_squeeze.10
  389.8 0.7 reshape_squeeze.11
  390.5 0.7 reshape_squeeze.9
  391.2 0.6 copy.20
  391.8 3.8 hand_over.1
  395.6 17.9 %settle.4.after_ref = f32[32,80,2560]{2,1,0:T(8,128)} custom-call(f32[32,80,2560]{2,1,0:T(8,128)} %get-tuple-element.29.src_ref, bf16[192,2560]{1,0:T(8,128)(2,1)} %get-tuple-element.25.refs_0_), custom_call_target="tpu_custom_call" | custom-call | flops 10000000000 | bytes 52428800 | tf_op jit(solution)/shard_map/settle/pallas_call | solution.py:771
  413.4 64.3 %spread.1.refs_0_.src_ref = f32[32,32,2560]{2,1,0:T(8,128)} custom-call(f32[32,2560]{1,0:T(8,128)} %get-tuple-element.28.own_ref, f32[32,80,2560]{2,1,0:T(8,128)} %settle.4.after_ref), custom_call_target="tpu_custom_call" | custom-call | flops 49999998976 | bytes 20971520 | tf_op jit(solution)/shard_map/spread/pallas_call | solution.py:525
  477.7 0.2 all-gather.5.cloned.1.call-done
  477.9 34.3 %settle.5.refs_0_ = f32[32,240,2560]{2,1,0:T(8,128)} custom-call(f32[32,160,2560]{2,1,0:T(8,128)} %bitcast.17, f32[32,32,2560]{2,1,0:T(8,128)} %spread.1.refs_0_.src_ref), custom_call_target="tpu_custom_call" | custom-call | flops 10000000000 | bytes 104857600 | tf_op jit(solution)/shard_map/settle/pallas_call | solution.py:771
  512.2 8.5 %settle.6.refs_0_ = f32[32,240,2560]{2,1,0:T(8,128)} custom-call(f32[32,32,2560]{2,1,0:T(8,128)} %spread.1.refs_0_.src_ref, f32[32,240,2560]{2,1,0:T(8,128)} %settle.5.refs_0_), custom_call_target="tpu_custom_call", output_to_operand_aliasing={{}: (1, {})} | custom-call | flops 10000000000 | bytes 20971520 | tf_op jit(solution)/shard_map/settle/pallas_call | solution.py:771
  520.6 22.6 %all-gather.3.cloned.1.call-done = f32[1536,2560]{1,0:T(8,128)} async-done(((f32[48,2560]{1,0:T(8,128)}), f32[1536,2560]{1,0:T(8,128)}) %all-gather.3.cloned.1.call-update) | async-done | bytes 15728656 | tf_op jit(solution)/shard_map/all_gather | solution.py:795
  543.2 11.1 %settle.7 = f32[32,240,2560]{2,1,0:T(8,128)} custom-call(f32[32,48,2560]{2,1,0:T(8,128)} %bitcast.19, f32[32,240,2560]{2,1,0:T(8,128)} %settle.6.refs_0_), custom_call_target="tpu_custom_call", output_to_operand_aliasing={{}: (1, {})} | custom-call | flops 10000000000 | bytes 31457280 | tf_op jit(solution)/shard_map/settle/pallas_call | solution.py:771
Async XLA Ops:
  7.2 470.7 %all-gather.5.cloned.1.call-start = ((), (), s32[]{:S(2)}) async-start(), calls=%async_computation.1 | async-start | bytes 54067200 | tf_op jit(solution)/shard_map/all_gather | solution.py:795
  211.2 332.0 %all-gather.3.cloned.1.call-start = ((), (), s32[]{:S(2)}) async-start(), calls=%async_computation | async-start | bytes 16220160 | tf_op jit(solution)/shard_map/all_gather | solution.py:795
Sparse Core Ops, SparseCore 0:
  211.3 266.5 all-gather.4
  480.0 63.2 all-gather.2

commit v11 on v10

--- a/solution.py
+++ b/solution.py
@@ -381,7 +381,7 @@
 
 
 def split_rows(rows):
-    first, short = 8 * (rows * 20 // 240), 8 * (rows // 60 or 1)
+    first, short = 8 * (rows * 17 // 240), 8 * (rows // 40)
     return first, rows - first - short, short
 
 
@@ -805,7 +805,7 @@
         rows = 3 * head_dim
         first, second, short = split_rows(rows)
         all_c = spread_rows(grad_c, grad_wo, size, 2)
-        grad_wq = settle(gather(grad_a), 0, first, 0, rows, 2, after=(all_c,))
+        grad_wq = settle(gather(grad_a), 0, first, 0, rows, after=(all_c,))
         grad_wq = settle(all_c, 0, short, first + second, rows, into=grad_wq)
         grad_wq = settle(gather(grad_b), 0, second, first, rows, into=grad_wq)
         totals = totals[:, :, :head_dim]

time: 562 us -> 544 us (0.968)
  waiting for transfers between devices: 23.5 us -> 0.83 us
    all_gather x2, waiting for transfers between devices: 22.8 us -> 0.04 us  [gather(): lax.all_gather(a, 'sp', axis=0, tiled=True)]
  transfers between devices with their start and end apart: 2 -> 2, of which waited for: 2 -> 0; matrix products, arithmetic and copies ran while one was open for 1% -> 1% of each run, Pallas kernels for 54% -> 56%
where the time goes in v11:
time: 544 us
  Pallas kernels  524 us (96%)
  between operations  14.2 us (3%)
    pallas_call x1, Pallas kernels, block_call(): pl.pallas_call(functools.partial(block_kernel, size, (batch, tok, head_di...  204 us
    pallas_call x1, Pallas kernels, token_side(): pl.pallas_call(functools.partial(token_kernel, size, head_dim, 16), out_s...  176 us
    pallas_call x4, Pallas kernels, settle(): pl.pallas_call(functools.partial(settle_kernel, block, depth, ahead, piec...  72 us
    pallas_call x1, Pallas kernels, spread_rows(): pl.pallas_call(functools.partial(spread_kernel, size), out_shape=jax.Shap...  67.6 us
  transfers between devices with their start and end apart: 2, of which 0 were waited for; matrix products, arithmetic and copies ran while one was open for 1% of the time, Pallas kernels for 56%

profile of v11, /device:TPU:97, one launch (start us, length us, event | category | flops | bytes accessed | tf_op | source)
XLA Modules:
  0.0 543.7 jit_solution(14897719992584929095)
XLA Ops:
  7.2 0.1 all-gather.5.cloned.1.call-start
  7.2 204.0 %block.1 = (bf16[3,32,4,2,16,2560]{5,4,3,2,1,0:T(8,128)(2,1)}, bf16[3,32,32,640]{3,2,1,0:T(8,128)(2,1)}, bf16[1,32,32,640]{3,2,1,0:T(8,128)(2,1)}, f32[136,2560]...) custom-call(bf16[3,4,16,2560]{3,2,1,0:T(8,128)(2,1)} %bitcast.25, ...), custom_call_target="tpu_custom_call" | custom-call | flops 119460012032 | bytes 60000000 | tf_op jit(solution)/shard_map/block/pallas_call | solution.py:403
  211.2 0.1 all-gather.5.cloned.1.call-update
  211.3 0.1 all-gather.3.cloned.1.call-start
  211.4 0.7 all-gather.3.cloned.1.call-update
  212.1 176.5 %token_side.1 = (f32[32,80,2560]{2,1,0:T(8,128)}, bf16[2,32,32,640]{3,2,1,0:T(8,128)(2,1)}, bf16[192,2560]{1,0:T(8,128)(2,1)}, bf16[192,2560]{1,0:T(8,128)(2,1)}, f32[32,8,128]{2,1,0:T(8,128)}) custom-call(f32[80,2560]{1,0:T(8,128)} %get-tuple-element.20.own_ref, bf16[3,32,32,640]{3,2,1,0:T(8,128)(2,1)} %get-tuple-element.21.parts_ref, ...), custom_call_target="tpu_custom_call" | custom-call | flops 120000004096 | bytes 52428800 | tf_op jit(solution)/shard_map/token_side/pallas_call | solution.py:686
  388.6 0.9 slice.17
  389.5 1.2 slice_reduce_fusion
  390.7 0.7 reshape_squeeze.10
  391.4 0.7 reshape_squeeze.11
  392.0 0.7 reshape_squeeze.9
  392.7 0.6 copy.20
  393.3 3.8 hand_over.1
  397.1 17.9 %settle.4.after_ref = f32[32,80,2560]{2,1,0:T(8,128)} custom-call(f32[32,80,2560]{2,1,0:T(8,128)} %get-tuple-element.29.src_ref, bf16[192,2560]{1,0:T(8,128)(2,1)} %get-tuple-element.25.refs_0_), custom_call_target="tpu_custom_call" | custom-call | flops 10000000000 | bytes 52428800 | tf_op jit(solution)/shard_map/settle/pallas_call | solution.py:771
  415.0 67.6 %spread.1.refs_0_.src_ref = f32[32,48,2560]{2,1,0:T(8,128)} custom-call(f32[48,2560]{1,0:T(8,128)} %get-tuple-element.28.own_ref, f32[32,80,2560]{2,1,0:T(8,128)} %settle.4.after_ref), custom_call_target="tpu_custom_call" | custom-call | flops 49999998976 | bytes 31457280 | tf_op jit(solution)/shard_map/spread/pallas_call | solution.py:525
  482.6 0.0 all-gather.5.cloned.1.call-done
  482.6 29.8 %settle.5.refs_0_ = f32[32,240,2560]{2,1,0:T(8,128)} custom-call(f32[32,136,2560]{2,1,0:T(8,128)} %bitcast.17, f32[32,48,2560]{2,1,0:T(8,128)} %spread.1.refs_0_.src_ref), custom_call_target="tpu_custom_call" | custom-call | flops 10000000000 | bytes 89128960 | tf_op jit(solution)/shard_map/settle/pallas_call | solution.py:771
  512.5 11.1 %settle.6.refs_0_ = f32[32,240,2560]{2,1,0:T(8,128)} custom-call(f32[32,48,2560]{2,1,0:T(8,128)} %spread.1.refs_0_.src_ref, f32[32,240,2560]{2,1,0:T(8,128)} %settle.5.refs_0_), custom_call_target="tpu_custom_call", output_to_operand_aliasing={{}: (1, {})} | custom-call | flops 10000000000 | bytes 31457280 | tf_op jit(solution)/shard_map/settle/pallas_call | solution.py:771
  523.6 0.0 all-gather.3.cloned.1.call-done
  523.6 13.2 %settle.7 = f32[32,240,2560]{2,1,0:T(8,128)} custom-call(f32[32,56,2560]{2,1,0:T(8,128)} %bitcast.19, f32[32,240,2560]{2,1,0:T(8,128)} %settle.6.refs_0_), custom_call_target="tpu_custom_call", output_to_operand_aliasing={{}: (1, {})} | custom-call | flops 10000000000 | bytes 36700160 | tf_op jit(solution)/shard_map/settle/pallas_call | solution.py:771
Async XLA Ops:
  7.2 475.4 %all-gather.5.cloned.1.call-start = ((), (), s32[]{:S(2)}) async-start(), calls=%async_computation.1 | async-start | bytes 45957120 | tf_op jit(solution)/shard_map/all_gather | solution.py:795
  211.3 312.3 %all-gather.3.cloned.1.call-start = ((), (), s32[]{:S(2)}) async-start(), calls=%async_computation | async-start | bytes 18923520 | tf_op jit(solution)/shard_map/all_gather | solution.py:795
Sparse Core Ops, SparseCore 0:
  211.4 227.6 all-gather.4
  441.2 78.1 all-gather.2

commit v12 on v11

--- a/solution.py
+++ b/solution.py
@@ -512,7 +512,11 @@
 def spread_kernel(size, own_ref, after_ref, gat_ref, stage, *sems):
     spread = Spread(size, own_ref, gat_ref, stage, sems)
     spread.load.start()
-    greet_all(spread.torus.me, size)
+    barrier = pltpu.get_barrier_semaphore()
+    friends = [spread.torus.neighbour(link) for link in range(4)] + [spread.torus.sibling]
+    for friend in friends:
+        pl.semaphore_signal(barrier, inc=1, device_id={"sp": friend}, device_id_type=MESH)
+    pl.semaphore_wait(barrier, len(friends))
     spread.load.wait()
     for g in range(Spread.STEPS):
         spread.step(g)
@@ -712,15 +716,23 @@
     )(block, parts, early, wq, wo, x, dy, gain, bout)
 
 
-def hand_kernel(y_ref, gx_ref, y_out, gx_out):
-    y_out[...] = y_ref[...]
-    gx_out[...] = gx_ref[...]
+def hand_kernel(y_ref, gx_ref, y_out, gx_out, buf, sems):
+    reads = [pltpu.make_async_copy(ref, buf.at[n], sems.at[0, n]) for n, ref in enumerate((y_ref, gx_ref))]
+    writes = [pltpu.make_async_copy(buf.at[n], ref, sems.at[1, n]) for n, ref in enumerate((y_out, gx_out))]
+    for read in reads:
+        read.start()
+    for read, write in zip(reads, writes):
+        read.wait()
+        write.start()
+    for write in writes:
+        write.wait()
 
 
 def hand_over(y, gx):
-    spec = pl.BlockSpec((y.shape[0] // 4, y.shape[1]), lambda i: (i, 0))
+    spec = pl.BlockSpec(memory_space=pl.ANY)
     return pl.pallas_call(
-        hand_kernel, grid=(4,), out_shape=(jax.ShapeDtypeStruct(y.shape, y.dtype),) * 2, in_specs=[spec] * 2, out_specs=(spec,) * 2,
+        hand_kernel, out_shape=(jax.ShapeDtypeStruct(y.shape, y.dtype),) * 2, in_specs=[spec] * 2, out_specs=(spec,) * 2,
+        scratch_shapes=[pltpu.VMEM((2, *y.shape), y.dtype), pltpu.SemaphoreType.DMA((2, 2))],
         cost_estimate=pl.CostEstimate(flops=1_000_000_000, bytes_accessed=8 * y.size, transcendentals=0), name="hand_over")(y, gx)
 
 

time: 544 us -> 545 us (level)
  no operation moved by 1% of the time
where the time goes in v12:
time: 545 us; the launch traced here: 544 us
  Pallas kernels  524 us (96%)
  between operations  14.2 us (3%)
    pallas_call x1, Pallas kernels, block_call(): pl.pallas_call(functools.partial(block_kernel, size, (batch, tok, head_di...  204 us
    pallas_call x1, Pallas kernels, token_side(): pl.pallas_call(functools.partial(token_kernel, size, head_dim, 16), out_s...  176 us
    pallas_call x4, Pallas kernels, settle(): pl.pallas_call(functools.partial(settle_kernel, block, depth, ahead, piec...  72 us
    pallas_call x1, Pallas kernels, spread_rows(): pl.pallas_call(functools.partial(spread_kernel, size), out_shape=jax.Shap...  69.4 us
  transfers between devices with their start and end apart: 2, of which 0 were waited for; matrix products, arithmetic and copies ran while one was open for 1% of the time, Pallas kernels for 56%

profile of v12, /device:TPU:97, one launch (start us, length us, event | category | flops | bytes accessed | tf_op | source)
XLA Modules:
  0.0 544.3 jit_solution(325845195297480144)
XLA Ops:
  7.2 0.1 all-gather.5.cloned.1.call-start
  7.2 204.0 %block.1 = (bf16[3,32,4,2,16,2560]{5,4,3,2,1,0:T(8,128)(2,1)}, bf16[3,32,32,640]{3,2,1,0:T(8,128)(2,1)}, bf16[1,32,32,640]{3,2,1,0:T(8,128)(2,1)}, f32[136,2560]...) custom-call(bf16[3,4,16,2560]{3,2,1,0:T(8,128)(2,1)} %bitcast.25, ...), custom_call_target="tpu_custom_call" | custom-call | flops 119460012032 | bytes 60000000 | tf_op jit(solution)/shard_map/block/pallas_call | solution.py:403
  211.2 0.1 all-gather.5.cloned.1.call-update
  211.3 0.1 all-gather.3.cloned.1.call-start
  211.4 0.7 all-gather.3.cloned.1.call-update
  212.1 176.5 %token_side.1 = (f32[32,80,2560]{2,1,0:T(8,128)}, bf16[2,32,32,640]{3,2,1,0:T(8,128)(2,1)}, bf16[192,2560]{1,0:T(8,128)(2,1)}, bf16[192,2560]{1,0:T(8,128)(2,1)}, f32[32,8,128]{2,1,0:T(8,128)}) custom-call(f32[80,2560]{1,0:T(8,128)} %get-tuple-element.20.own_ref, bf16[3,32,32,640]{3,2,1,0:T(8,128)(2,1)} %get-tuple-element.21.parts_ref, ...), custom_call_target="tpu_custom_call" | custom-call | flops 120000004096 | bytes 52428800 | tf_op jit(solution)/shard_map/token_side/pallas_call | solution.py:690
  388.6 0.9 slice.17
  389.5 1.2 slice_reduce_fusion
  390.7 0.7 reshape_squeeze.10
  391.4 0.7 reshape_squeeze.11
  392.0 0.7 reshape_squeeze.9
  392.7 0.6 copy.20
  393.3 2.5 hand_over.1
  395.9 17.9 %settle.4.after_ref = f32[32,80,2560]{2,1,0:T(8,128)} custom-call(f32[32,80,2560]{2,1,0:T(8,128)} %get-tuple-element.29.src_ref, bf16[192,2560]{1,0:T(8,128)(2,1)} %get-tuple-element.25.refs_0_), custom_call_target="tpu_custom_call" | custom-call | flops 10000000000 | bytes 52428800 | tf_op jit(solution)/shard_map/settle/pallas_call | solution.py:783
  413.8 69.4 %spread.1.refs_0_.src_ref = f32[32,48,2560]{2,1,0:T(8,128)} custom-call(f32[48,2560]{1,0:T(8,128)} %get-tuple-element.28.own_ref, f32[32,80,2560]{2,1,0:T(8,128)} %settle.4.after_ref), custom_call_target="tpu_custom_call" | custom-call | flops 49999998976 | bytes 31457280 | tf_op jit(solution)/shard_map/spread/pallas_call | solution.py:529
  483.2 0.0 all-gather.5.cloned.1.call-done
  483.2 29.8 %settle.5.refs_0_ = f32[32,240,2560]{2,1,0:T(8,128)} custom-call(f32[32,136,2560]{2,1,0:T(8,128)} %bitcast.17, f32[32,48,2560]{2,1,0:T(8,128)} %spread.1.refs_0_.src_ref), custom_call_target="tpu_custom_call" | custom-call | flops 10000000000 | bytes 89128960 | tf_op jit(solution)/shard_map/settle/pallas_call | solution.py:783
  513.1 11.1 %settle.6.refs_0_ = f32[32,240,2560]{2,1,0:T(8,128)} custom-call(f32[32,48,2560]{2,1,0:T(8,128)} %spread.1.refs_0_.src_ref, f32[32,240,2560]{2,1,0:T(8,128)} %settle.5.refs_0_), custom_call_target="tpu_custom_call", output_to_operand_aliasing={{}: (1, {})} | custom-call | flops 10000000000 | bytes 31457280 | tf_op jit(solution)/shard_map/settle/pallas_call | solution.py:783
  524.2 0.0 all-gather.3.cloned.1.call-done
  524.2 13.2 %settle.7 = f32[32,240,2560]{2,1,0:T(8,128)} custom-call(f32[32,56,2560]{2,1,0:T(8,128)} %bitcast.19, f32[32,240,2560]{2,1,0:T(8,128)} %settle.6.refs_0_), custom_call_target="tpu_custom_call", output_to_operand_aliasing={{}: (1, {})} | custom-call | flops 10000000000 | bytes 36700160 | tf_op jit(solution)/shard_map/settle/pallas_call | solution.py:783
Async XLA Ops:
  7.2 476.0 %all-gather.5.cloned.1.call-start = ((), (), s32[]{:S(2)}) async-start(), calls=%async_computation.1 | async-start | bytes 45957120 | tf_op jit(solution)/shard_map/all_gather | solution.py:807
  211.3 312.9 %all-gather.3.cloned.1.call-start = ((), (), s32[]{:S(2)}) async-start(), calls=%async_computation | async-start | bytes 18923520 | tf_op jit(solution)/shard_map/all_gather | solution.py:807
Sparse Core Ops, SparseCore 0:
  211.4 231.1 all-gather.4
  444.7 76.7 all-gather.2
